TPU v7x, 16 devices: a 4x2x1 block of a 4x4x8 slice. The times are simulated.
16 devices in a mesh: dp: 2 (over y, z), sp: 8 (over x, core).
Axes of the slice: x: 4, y: 2, z: 1, core: 2. Of those that a mesh axis runs over, the one named last changes fastest.
The devices are a block of a 4x4x8 slice.
Arguments:
- x_in: bfloat16 [16, 1024, 2048], P('dp', 'sp'), parts along dimension 0
- grad_y: bfloat16 [16, 1024, 2048], P('dp', 'sp'), parts along dimension 0
- positions: int32 [16, 1024], P('dp', 'sp'), parts along dimension 0
- g_norm: bfloat16 [2048], replicated
- w_query: bfloat16 [2048, 2048], replicated
- w_key: bfloat16 [2048, 2048], replicated
- w_value: bfloat16 [2048, 2048], replicated
- w_out: bfloat16 [2048, 2048], replicated
- g_query: bfloat16 [2048], replicated
- g_key: bfloat16 [2048], replicated
Outputs:
- output 1: bfloat16 [16, 1024, 2048], P('dp', 'sp'), parts along dimension 0
- output 2: bfloat16 [16, 1024, 2048], P('dp', 'sp'), parts along dimension 0
- output 3: float32 [4096], P(('dp', 'sp')), parts along dimension 0
- output 4: float32 [4096, 2048], P(('dp', 'sp')), parts along dimension 0
- output 5: float32 [4096, 2048], P(('dp', 'sp')), parts along dimension 0
- output 6: float32 [4096, 2048], P(('dp', 'sp')), parts along dimension 0
- output 7: float32 [4096, 2048], P(('dp', 'sp')), parts along dimension 0
- output 8: float32 [4096], P(('dp', 'sp')), parts along dimension 0
- output 9: float32 [4096], P(('dp', 'sp')), parts along dimension 0
There are 2 independent parts. A program takes and returns all parts, laid end to end along the dimension named above; an argument that names none is the same for every part.
All inputs are finite; a program needn't handle non-finite values.
Results may differ from a plain program's by a relative error of at most 0.0114602.
Values are sent between devices in bfloat16 or wider.
A program may use at most 768 MiB of HBM per device.

v0:
```python
import functools
import jax
import jax.numpy as jnp
from jax import lax
from jax.sharding import PartitionSpec as P

HEAD_DIM = 128
QUERY_BLOCK = 128
NORM_EPS = 1e-5
ROPE_BASE = 10000.0
NEG_BIG = -1e30


def rope_tables(positions):
    half_dim = HEAD_DIM // 2
    inv_freq = ROPE_BASE ** (-jnp.arange(half_dim, dtype=jnp.float32) * (2.0 / HEAD_DIM))
    angles = positions.astype(jnp.float32)[..., None] * inv_freq
    return jnp.cos(angles)[:, :, None, :], jnp.sin(angles)[:, :, None, :]


def rope_apply(values, cos_t, sin_t):
    half_dim = values.shape[-1] // 2
    first_half = values[..., :half_dim]
    second_half = values[..., half_dim:]
    return jnp.concatenate([first_half * cos_t - second_half * sin_t, second_half * cos_t + first_half * sin_t], axis=-1)


def rope_revert(grads_in, cos_t, sin_t):
    half_dim = grads_in.shape[-1] // 2
    first_half = grads_in[..., :half_dim]
    second_half = grads_in[..., half_dim:]
    return jnp.concatenate([first_half * cos_t + second_half * sin_t, second_half * cos_t - first_half * sin_t], axis=-1)


def rms_forward(values, gain_vec):
    inv_rms = lax.rsqrt(jnp.mean(values * values, axis=-1, keepdims=True) + NORM_EPS)
    normed = values * inv_rms
    return normed * gain_vec.astype(jnp.float32), normed, inv_rms


def rms_backward(d_out, normed, inv_rms, gain_vec):
    d_normed = d_out * gain_vec.astype(jnp.float32)
    d_in = inv_rms * (d_normed - normed * jnp.mean(d_normed * normed, axis=-1, keepdims=True))
    return d_in, d_out * normed


def project(values, weight):
    return jnp.einsum('bsd,de->bse', values, weight, preferred_element_type=jnp.float32)


def project_back(grads_in, weight):
    return jnp.einsum('bse,de->bsd', grads_in, weight, preferred_element_type=jnp.float32)


def weight_grad(values, grads_in):
    return jnp.einsum('bsd,bse->de', values, grads_in, preferred_element_type=jnp.float32)


def block_front(x_in, positions, g_norm, w_query, w_key, w_value, g_query, g_key):
    n_batch, seq_len, d_model = x_in.shape
    head_shape = (n_batch, seq_len, d_model // HEAD_DIM, HEAD_DIM)
    cos_t, sin_t = rope_tables(positions)
    x_f = x_in.astype(jnp.float32)
    hid_f, x_hat, x_inv = rms_forward(x_f, g_norm)
    hidden = hid_f.astype(jnp.bfloat16)
    q_nrm, q_hat, q_inv = rms_forward(project(hidden, w_query), g_query)
    k_nrm, k_hat, k_inv = rms_forward(project(hidden, w_key), g_key)
    q_rot = rope_apply(q_nrm.reshape(head_shape), cos_t, sin_t).astype(jnp.bfloat16)
    k_rot = rope_apply(k_nrm.reshape(head_shape), cos_t, sin_t).astype(jnp.bfloat16)
    v_val = project(hidden, w_value).astype(jnp.bfloat16).reshape(head_shape)
    saved_fwd = (x_f, x_hat, x_inv, hidden, q_hat, q_inv, k_hat, k_inv, cos_t, sin_t)
    return q_rot, k_rot, v_val, saved_fwd


def block_back(saved_fwd, d_q, d_k, d_v, grad_y, g_norm, w_query, w_key, w_value, g_query, g_key):
    x_f, x_hat, x_inv, hidden, q_hat, q_inv, k_hat, k_inv, cos_t, sin_t = saved_fwd
    flat_shape = hidden.shape
    dq_rot = rope_revert(d_q.astype(jnp.float32), cos_t, sin_t).reshape(flat_shape)
    dk_rot = rope_revert(d_k.astype(jnp.float32), cos_t, sin_t).reshape(flat_shape)
    dq_raw, q_terms = rms_backward(dq_rot, q_hat, q_inv, g_query)
    dk_raw, k_terms = rms_backward(dk_rot, k_hat, k_inv, g_key)
    dq_bf = dq_raw.astype(jnp.bfloat16)
    dk_bf = dk_raw.astype(jnp.bfloat16)
    dv_bf = d_v.reshape(flat_shape)
    d_hidden = project_back(dq_bf, w_query) + project_back(dk_bf, w_key) + project_back(dv_bf, w_value)
    dx_norm, n_terms = rms_backward(d_hidden, x_hat, x_inv, g_norm)
    grad_x = (grad_y.astype(jnp.float32) + dx_norm).astype(jnp.bfloat16)
    return grad_x, (dq_bf, dk_bf, dv_bf), (n_terms, q_terms, k_terms)


def attend_forward(q_all, k_all, v_all, q_offset):
    q_len = q_all.shape[1]
    key_pos = jnp.arange(k_all.shape[1])
    blk_len = min(QUERY_BLOCK, q_len)
    qk_scale = q_all.shape[-1] ** -0.5

    def block_step(blk_idx, loop_state):
        out_buf, lse_buf = loop_state
        q_start = blk_idx * blk_len
        q_blk = lax.dynamic_slice_in_dim(q_all, q_start, blk_len, axis=1)
        scores = jnp.einsum('bqhd,bkhd->bhqk', q_blk, k_all, preferred_element_type=jnp.float32) * qk_scale
        q_pos = q_offset + q_start + jnp.arange(blk_len)
        scores = jnp.where(q_pos[:, None] >= key_pos[None, :], scores, NEG_BIG)
        row_max = jnp.max(scores, axis=-1, keepdims=True)
        exp_scores = jnp.exp(scores - row_max)
        row_sum = jnp.sum(exp_scores, axis=-1, keepdims=True)
        prob_bf = (exp_scores / row_sum).astype(jnp.bfloat16)
        out_blk = jnp.einsum('bhqk,bkhd->bqhd', prob_bf, v_all, preferred_element_type=jnp.float32)
        lse_blk = (row_max + jnp.log(row_sum))[..., 0]
        out_buf = lax.dynamic_update_slice_in_dim(out_buf, out_blk.astype(jnp.bfloat16), q_start, axis=1)
        lse_buf = lax.dynamic_update_slice_in_dim(lse_buf, lse_blk, q_start, axis=2)
        return out_buf, lse_buf

    init_state = (jnp.zeros(q_all.shape, jnp.bfloat16), jnp.zeros((q_all.shape[0], q_all.shape[2], q_len), jnp.float32))
    return lax.fori_loop(0, q_len // blk_len, block_step, init_state)


def attend_backward(q_all, k_all, v_all, lse_all, dout_all, q_offset):
    q_len = q_all.shape[1]
    key_pos = jnp.arange(k_all.shape[1])
    blk_len = min(QUERY_BLOCK, q_len)
    qk_scale = q_all.shape[-1] ** -0.5

    def block_step(blk_idx, loop_state):
        dq_buf, dk_acc, dv_acc = loop_state
        q_start = blk_idx * blk_len
        q_blk = lax.dynamic_slice_in_dim(q_all, q_start, blk_len, axis=1)
        do_blk = lax.dynamic_slice_in_dim(dout_all, q_start, blk_len, axis=1)
        lse_blk = lax.dynamic_slice_in_dim(lse_all, q_start, blk_len, axis=2)
        scores = jnp.einsum('bqhd,bkhd->bhqk', q_blk, k_all, preferred_element_type=jnp.float32) * qk_scale
        q_pos = q_offset + q_start + jnp.arange(blk_len)
        scores = jnp.where(q_pos[:, None] >= key_pos[None, :], scores, NEG_BIG)
        prob_f = jnp.exp(scores - lse_blk[..., None])
        d_prob = jnp.einsum('bqhd,bkhd->bhqk', do_blk, v_all, preferred_element_type=jnp.float32)
        row_dot = jnp.sum(prob_f * d_prob, axis=-1, keepdims=True)
        ds_bf = (prob_f * (d_prob - row_dot) * qk_scale).astype(jnp.bfloat16)
        prob_bf = prob_f.astype(jnp.bfloat16)
        dv_acc = dv_acc + jnp.einsum('bhqk,bqhd->bkhd', prob_bf, do_blk, preferred_element_type=jnp.float32)
        dk_acc = dk_acc + jnp.einsum('bhqk,bqhd->bkhd', ds_bf, q_blk, preferred_element_type=jnp.float32)
        dq_blk = jnp.einsum('bhqk,bkhd->bqhd', ds_bf, k_all, preferred_element_type=jnp.float32)
        dq_buf = lax.dynamic_update_slice_in_dim(dq_buf, dq_blk.astype(jnp.bfloat16), q_start, axis=1)
        return dq_buf, dk_acc, dv_acc

    init_state = (jnp.zeros(q_all.shape, jnp.bfloat16), jnp.zeros(k_all.shape, jnp.float32), jnp.zeros(v_all.shape, jnp.float32))
    return lax.fori_loop(0, q_len // blk_len, block_step, init_state)


def solution(mesh):
    to_heads = functools.partial(lax.all_to_all, axis_name='sp', split_axis=2, concat_axis=1, tiled=True)
    to_tokens = functools.partial(lax.all_to_all, axis_name='sp', split_axis=1, concat_axis=2, tiled=True)

    def sum_rows(partial_sum):
        return lax.psum_scatter(partial_sum, 'sp', scatter_dimension=0, tiled=True)

    def device_step(x_loc, grad_y, positions, g_norm, w_query, w_key, w_value, w_out, g_query, g_key):
        n_batch, loc_len, d_model = x_loc.shape
        q_loc, k_loc, v_loc, saved_fwd = block_front(x_loc, positions, g_norm, w_query, w_key, w_value, g_query, g_key)
        q_all = to_heads(q_loc)
        k_all = to_heads(k_loc)
        v_all = to_heads(v_loc)
        out_all, lse_all = attend_forward(q_all, k_all, v_all, 0)
        attended = to_tokens(out_all).reshape(n_batch, loc_len, d_model)
        y_out = (saved_fwd[0] + project(attended, w_out)).astype(jnp.bfloat16)
        grad_w_out = weight_grad(attended, grad_y)
        d_attn = project_back(grad_y, w_out).astype(jnp.bfloat16).reshape(q_loc.shape)
        dq_all, dk_acc, dv_acc = attend_backward(q_all, k_all, v_all, lse_all, to_heads(d_attn), 0)
        d_q = to_tokens(dq_all)
        d_k = to_tokens(dk_acc.astype(jnp.bfloat16))
        d_v = to_tokens(dv_acc.astype(jnp.bfloat16))
        grad_x, proj_grads, gain_terms = block_back(saved_fwd, d_q, d_k, d_v, grad_y, g_norm, w_query, w_key, w_value, g_query, g_key)
        hidden = saved_fwd[3]
        return (y_out, grad_x, sum_rows(jnp.sum(gain_terms[0], axis=(0, 1))), sum_rows(weight_grad(hidden, proj_grads[0])), sum_rows(weight_grad(hidden, proj_grads[1])), sum_rows(weight_grad(hidden, proj_grads[2])), sum_rows(grad_w_out), sum_rows(jnp.sum(gain_terms[1], axis=(0, 1))), sum_rows(jnp.sum(gain_terms[2], axis=(0, 1))))

    seq_spec = P('dp', 'sp', None)
    mat_rep = P(None, None)
    vec_rep = P(None)
    row_spec = P(('dp', 'sp'), None)
    vec_spec = P(('dp', 'sp'))
    return jax.shard_map(device_step, mesh=mesh, in_specs=(seq_spec, seq_spec, P('dp', 'sp'), vec_rep, mat_rep, mat_rep, mat_rep, mat_rep, vec_rep, vec_rep), out_specs=(seq_spec, seq_spec, vec_spec, row_spec, row_spec, row_spec, row_spec, vec_spec, vec_spec), check_vma=False)
```

profile of v0, /device:TPU:113, one launch (start us, length us, event | category | flops | bytes accessed | tf_op | source)
XLA Modules:
  0.0 1622.8 jit_solution(1168567979770159743)
XLA Ops:
  62.5 17.0 %fusion.124 = (f32[8,128,16,64]{3,2,1,0:T(8,128)}, f32[8,128,16,64]{3,2,1,0:T(8,128)}, f32[8,128,16,64]{3,2,1,0:T(8,128)}, f32[8,128,16,64]{3,2,1,0:T(8,128)}) fusion(f32[8,128,16,128]{3,2,1,0:T(8,128)} %bitcast.169, f32[8,128,16,128]{3,2,1,0:T(8,128)S(1)} %bitcast.166), kind=kLoop, calls=%fused_computation.144 | loop fusion | bytes 33554432 | tf_op jit(solution)/shard_map/slice | solution.py:23
  81.4 31.2 %subtract_convert_fusion = (bf16[8,128,16,64]{3,1,0,2:T(8,128)(2,1)}, bf16[8,128,16,64]{3,1,0,2:T(8,128)(2,1)}, bf16[8,128,16,64]{3,1,0,2:T(8,128)(2,1)}, bf16[8,128,16,64]{3,1,0,2:T(8,128)(2,1)}) fusion(f32[8,128,16,64]{3,2,1,0:T(8,128)} %get-tuple-element.406, f32[8,128,16,64]{3,2,1,0:T(8,128)} %get-tuple-element.405, ...), kind=kLoop, calls=%fused_computation.120 | loop fusion | flops 16777216 | bytes 25690112 | tf_op jit(solution)/shard_map/convert.6
  130.8 42.6 %all-to-all-done.1 = bf16[8,128,16,128]{3,1,0,2:T(8,128)(2,1)} async-done(((bf16[8,128,16,128]{3,1,0,2:T(8,128)(2,1)}), bf16[8,128,16,128]{3,1,0,2:T(8,128)(2,1)}, u32[]{:S(2)}, u32[]{:S(2)}) %all-to-all-start.1) | async-done | bytes 4194336 | tf_op jit(solution)/shard_map/all_to_all | solution.py:159
  194.7 32.9 %all-to-all-done = bf16[8,128,16,128]{3,1,0,2:T(8,128)(2,1)} async-done(((bf16[8,128,16,128]{3,1,0,2:T(8,128)(2,1)}), bf16[8,128,16,128]{3,1,0,2:T(8,128)(2,1)}, u32[]{:S(2)}, u32[]{:S(2)}) %all-to-all-start) | async-done | bytes 4194336 | tf_op jit(solution)/shard_map/all_to_all | solution.py:158
  258.5 23.3 %all-to-all-done.2 = bf16[8,128,16,128]{3,1,0,2:T(8,128)(2,1)} async-done(((bf16[8,128,16,128]{3,1,0,2:T(8,128)(2,1)}), bf16[8,128,16,128]{3,1,0,2:T(8,128)(2,1)}, u32[]{:S(2)}, u32[]{:S(2)}) %all-to-all-start.2) | async-done | bytes 4194336 | tf_op jit(solution)/shard_map/all_to_all | solution.py:160
  296.8 88.8 %while.34 = (s32[]{:T(128)}, bf16[8,1024,2,128]{3,2,0,1:T(2,128)(2,1)}, f32[8,2,1024]{2,1,0:T(2,128)S(1)}, bf16[8,1024,2,128]{3,1,2,0:T(8,128)(2,1)}, bf16[8,102...) while((s32[]{:T(128)}, ...), condition=%wide.region_6.7_spmd.clone, body=%wide.region_3.6_spmd.clone.sunk | while | flops 1099298944 | bytes 53019840 | solution.py:115
  394.4 595.9 %while.35 = (s32[]{:T(128)}, bf16[8,1024,2,128]{3,2,0,1:T(2,128)(2,1)}, f32[8,1024,2,128]{1,3,2,0:T(8,128)}, f32[8,1024,2,128]{1,3,2,0:T(8,128)}, bf16[8,1024,2,...) while((s32[]{:T(128)}, ...), condition=%wide.region_9.10_spmd.clone, body=%wide.region_7.9_spmd.clone.sunk | while | flops 2747668480 | bytes 142787824 | solution.py:145
  407.3 25.3 %bitcast_add_fusion.4 = f32[8,1024,2,128]{1,3,2,0:T(8,128)} fusion(f32[8,1024,2,128]{1,3,2,0:T(8,128)} %get-tuple-element.563, pred[]{:T(512)S(6)} %compare.3, f32[8,2,128,1024]{3,2,1,0:T(8,128)} %fusion.174, f32[8,2,128,1024]{3,2,1,0:T(8,128)} %fusion.175, f32[8,2,128]{2,1,0:T(2,128)S(1)} %constant_dynamic-slice_fusion.2, ...), kind=kOutput, calls=%fused_computation.21.clone.1 | convolution fusion | flops 564136960 | bytes 51134468 | tf_op jit(solution)/shard_map/while/body/eval_jaxpr/bhqk,bqhd->bkhd/dot_general | solution.py:139
  432.6 22.8 %fusion.176 = bf16[8,128,2,128]{3,1,2,0:T(8,128)(2,1)S(1)} fusion(bf16[8,1024,2,128]{3,1,2,0:T(8,128)(2,1)} %get-tuple-element.579, f32[8,2,128,1024]{3,2,1,0:T(8,128)} %fusion.174, f32[8,2,128,1024]{3,2,1,0:T(8,128)} %fusion.175, f32[8,2,128]{2,1,0:T(2,128)S(1)} %constant_dynamic-slice_fusion.2, pred[128,1024]{1,0:T(8,128)(4,1)S(1)} %iota_compare_fusion.5), kind=kOutput, calls=%fused_computation.43.clone.1 | convolution fusion | flops 560204800 | bytes 21635072 | tf_op jit(solution)/shard_map/while/body/eval_jaxpr/bhqk,bkhd->bqhd/dot_general | solution.py:140
  479.4 25.5 %bitcast_add_fusion.4 = f32[8,1024,2,128]{1,3,2,0:T(8,128)} fusion(f32[8,1024,2,128]{1,3,2,0:T(8,128)} %get-tuple-element.563, pred[]{:T(512)S(6)} %compare.3, f32[8,2,128,1024]{3,2,1,0:T(8,128)} %fusion.174, f32[8,2,128,1024]{3,2,1,0:T(8,128)} %fusion.175, f32[8,2,128]{2,1,0:T(2,128)S(1)} %constant_dynamic-slice_fusion.2, ...), kind=kOutput, calls=%fused_computation.21.clone.1 | convolution fusion | flops 564136960 | bytes 51134468 | tf_op jit(solution)/shard_map/while/body/eval_jaxpr/bhqk,bqhd->bkhd/dot_general | solution.py:139
  505.0 22.8 %fusion.176 = bf16[8,128,2,128]{3,1,2,0:T(8,128)(2,1)S(1)} fusion(bf16[8,1024,2,128]{3,1,2,0:T(8,128)(2,1)} %get-tuple-element.579, f32[8,2,128,1024]{3,2,1,0:T(8,128)} %fusion.174, f32[8,2,128,1024]{3,2,1,0:T(8,128)} %fusion.175, f32[8,2,128]{2,1,0:T(2,128)S(1)} %constant_dynamic-slice_fusion.2, pred[128,1024]{1,0:T(8,128)(4,1)S(1)} %iota_compare_fusion.5), kind=kOutput, calls=%fused_computation.43.clone.1 | convolution fusion | flops 560204800 | bytes 21635072 | tf_op jit(solution)/shard_map/while/body/eval_jaxpr/bhqk,bkhd->bqhd/dot_general | solution.py:140
  554.2 25.5 %bitcast_add_fusion.4 = f32[8,1024,2,128]{1,3,2,0:T(8,128)} fusion(f32[8,1024,2,128]{1,3,2,0:T(8,128)} %get-tuple-element.563, pred[]{:T(512)S(6)} %compare.3, f32[8,2,128,1024]{3,2,1,0:T(8,128)} %fusion.174, f32[8,2,128,1024]{3,2,1,0:T(8,128)} %fusion.175, f32[8,2,128]{2,1,0:T(2,128)S(1)} %constant_dynamic-slice_fusion.2, ...), kind=kOutput, calls=%fused_computation.21.clone.1 | convolution fusion | flops 564136960 | bytes 51134468 | tf_op jit(solution)/shard_map/while/body/eval_jaxpr/bhqk,bqhd->bkhd/dot_general | solution.py:139
  579.7 22.8 %fusion.176 = bf16[8,128,2,128]{3,1,2,0:T(8,128)(2,1)S(1)} fusion(bf16[8,1024,2,128]{3,1,2,0:T(8,128)(2,1)} %get-tuple-element.579, f32[8,2,128,1024]{3,2,1,0:T(8,128)} %fusion.174, f32[8,2,128,1024]{3,2,1,0:T(8,128)} %fusion.175, f32[8,2,128]{2,1,0:T(2,128)S(1)} %constant_dynamic-slice_fusion.2, pred[128,1024]{1,0:T(8,128)(4,1)S(1)} %iota_compare_fusion.5), kind=kOutput, calls=%fused_computation.43.clone.1 | convolution fusion | flops 560204800 | bytes 21635072 | tf_op jit(solution)/shard_map/while/body/eval_jaxpr/bhqk,bkhd->bqhd/dot_general | solution.py:140
  628.9 25.6 %bitcast_add_fusion.4 = f32[8,1024,2,128]{1,3,2,0:T(8,128)} fusion(f32[8,1024,2,128]{1,3,2,0:T(8,128)} %get-tuple-element.563, pred[]{:T(512)S(6)} %compare.3, f32[8,2,128,1024]{3,2,1,0:T(8,128)} %fusion.174, f32[8,2,128,1024]{3,2,1,0:T(8,128)} %fusion.175, f32[8,2,128]{2,1,0:T(2,128)S(1)} %constant_dynamic-slice_fusion.2, ...), kind=kOutput, calls=%fused_computation.21.clone.1 | convolution fusion | flops 564136960 | bytes 51134468 | tf_op jit(solution)/shard_map/while/body/eval_jaxpr/bhqk,bqhd->bkhd/dot_general | solution.py:139
  654.5 22.8 %fusion.176 = bf16[8,128,2,128]{3,1,2,0:T(8,128)(2,1)S(1)} fusion(bf16[8,1024,2,128]{3,1,2,0:T(8,128)(2,1)} %get-tuple-element.579, f32[8,2,128,1024]{3,2,1,0:T(8,128)} %fusion.174, f32[8,2,128,1024]{3,2,1,0:T(8,128)} %fusion.175, f32[8,2,128]{2,1,0:T(2,128)S(1)} %constant_dynamic-slice_fusion.2, pred[128,1024]{1,0:T(8,128)(4,1)S(1)} %iota_compare_fusion.5), kind=kOutput, calls=%fused_computation.43.clone.1 | convolution fusion | flops 560204800 | bytes 21635072 | tf_op jit(solution)/shard_map/while/body/eval_jaxpr/bhqk,bkhd->bqhd/dot_general | solution.py:140
  703.7 25.5 %bitcast_add_fusion.4 = f32[8,1024,2,128]{1,3,2,0:T(8,128)} fusion(f32[8,1024,2,128]{1,3,2,0:T(8,128)} %get-tuple-element.563, pred[]{:T(512)S(6)} %compare.3, f32[8,2,128,1024]{3,2,1,0:T(8,128)} %fusion.174, f32[8,2,128,1024]{3,2,1,0:T(8,128)} %fusion.175, f32[8,2,128]{2,1,0:T(2,128)S(1)} %constant_dynamic-slice_fusion.2, ...), kind=kOutput, calls=%fused_computation.21.clone.1 | convolution fusion | flops 564136960 | bytes 51134468 | tf_op jit(solution)/shard_map/while/body/eval_jaxpr/bhqk,bqhd->bkhd/dot_general | solution.py:139
  729.2 22.8 %fusion.176 = bf16[8,128,2,128]{3,1,2,0:T(8,128)(2,1)S(1)} fusion(bf16[8,1024,2,128]{3,1,2,0:T(8,128)(2,1)} %get-tuple-element.579, f32[8,2,128,1024]{3,2,1,0:T(8,128)} %fusion.174, f32[8,2,128,1024]{3,2,1,0:T(8,128)} %fusion.175, f32[8,2,128]{2,1,0:T(2,128)S(1)} %constant_dynamic-slice_fusion.2, pred[128,1024]{1,0:T(8,128)(4,1)S(1)} %iota_compare_fusion.5), kind=kOutput, calls=%fused_computation.43.clone.1 | convolution fusion | flops 560204800 | bytes 21635072 | tf_op jit(solution)/shard_map/while/body/eval_jaxpr/bhqk,bkhd->bqhd/dot_general | solution.py:140
  778.5 25.6 %bitcast_add_fusion.4 = f32[8,1024,2,128]{1,3,2,0:T(8,128)} fusion(f32[8,1024,2,128]{1,3,2,0:T(8,128)} %get-tuple-element.563, pred[]{:T(512)S(6)} %compare.3, f32[8,2,128,1024]{3,2,1,0:T(8,128)} %fusion.174, f32[8,2,128,1024]{3,2,1,0:T(8,128)} %fusion.175, f32[8,2,128]{2,1,0:T(2,128)S(1)} %constant_dynamic-slice_fusion.2, ...), kind=kOutput, calls=%fused_computation.21.clone.1 | convolution fusion | flops 564136960 | bytes 51134468 | tf_op jit(solution)/shard_map/while/body/eval_jaxpr/bhqk,bqhd->bkhd/dot_general | solution.py:139
  804.1 22.8 %fusion.176 = bf16[8,128,2,128]{3,1,2,0:T(8,128)(2,1)S(1)} fusion(bf16[8,1024,2,128]{3,1,2,0:T(8,128)(2,1)} %get-tuple-element.579, f32[8,2,128,1024]{3,2,1,0:T(8,128)} %fusion.174, f32[8,2,128,1024]{3,2,1,0:T(8,128)} %fusion.175, f32[8,2,128]{2,1,0:T(2,128)S(1)} %constant_dynamic-slice_fusion.2, pred[128,1024]{1,0:T(8,128)(4,1)S(1)} %iota_compare_fusion.5), kind=kOutput, calls=%fused_computation.43.clone.1 | convolution fusion | flops 560204800 | bytes 21635072 | tf_op jit(solution)/shard_map/while/body/eval_jaxpr/bhqk,bkhd->bqhd/dot_general | solution.py:140
  853.3 25.5 %bitcast_add_fusion.4 = f32[8,1024,2,128]{1,3,2,0:T(8,128)} fusion(f32[8,1024,2,128]{1,3,2,0:T(8,128)} %get-tuple-element.563, pred[]{:T(512)S(6)} %compare.3, f32[8,2,128,1024]{3,2,1,0:T(8,128)} %fusion.174, f32[8,2,128,1024]{3,2,1,0:T(8,128)} %fusion.175, f32[8,2,128]{2,1,0:T(2,128)S(1)} %constant_dynamic-slice_fusion.2, ...), kind=kOutput, calls=%fused_computation.21.clone.1 | convolution fusion | flops 564136960 | bytes 51134468 | tf_op jit(solution)/shard_map/while/body/eval_jaxpr/bhqk,bqhd->bkhd/dot_general | solution.py:139
  878.8 22.8 %fusion.176 = bf16[8,128,2,128]{3,1,2,0:T(8,128)(2,1)S(1)} fusion(bf16[8,1024,2,128]{3,1,2,0:T(8,128)(2,1)} %get-tuple-element.579, f32[8,2,128,1024]{3,2,1,0:T(8,128)} %fusion.174, f32[8,2,128,1024]{3,2,1,0:T(8,128)} %fusion.175, f32[8,2,128]{2,1,0:T(2,128)S(1)} %constant_dynamic-slice_fusion.2, pred[128,1024]{1,0:T(8,128)(4,1)S(1)} %iota_compare_fusion.5), kind=kOutput, calls=%fused_computation.43.clone.1 | convolution fusion | flops 560204800 | bytes 21635072 | tf_op jit(solution)/shard_map/while/body/eval_jaxpr/bhqk,bkhd->bqhd/dot_general | solution.py:140
  928.0 25.6 %bitcast_add_fusion.4 = f32[8,1024,2,128]{1,3,2,0:T(8,128)} fusion(f32[8,1024,2,128]{1,3,2,0:T(8,128)} %get-tuple-element.563, pred[]{:T(512)S(6)} %compare.3, f32[8,2,128,1024]{3,2,1,0:T(8,128)} %fusion.174, f32[8,2,128,1024]{3,2,1,0:T(8,128)} %fusion.175, f32[8,2,128]{2,1,0:T(2,128)S(1)} %constant_dynamic-slice_fusion.2, ...), kind=kOutput, calls=%fused_computation.21.clone.1 | convolution fusion | flops 564136960 | bytes 51134468 | tf_op jit(solution)/shard_map/while/body/eval_jaxpr/bhqk,bqhd->bkhd/dot_general | solution.py:139
  953.6 22.8 %fusion.176 = bf16[8,128,2,128]{3,1,2,0:T(8,128)(2,1)S(1)} fusion(bf16[8,1024,2,128]{3,1,2,0:T(8,128)(2,1)} %get-tuple-element.579, f32[8,2,128,1024]{3,2,1,0:T(8,128)} %fusion.174, f32[8,2,128,1024]{3,2,1,0:T(8,128)} %fusion.175, f32[8,2,128]{2,1,0:T(2,128)S(1)} %constant_dynamic-slice_fusion.2, pred[128,1024]{1,0:T(8,128)(4,1)S(1)} %iota_compare_fusion.5), kind=kOutput, calls=%fused_computation.43.clone.1 | convolution fusion | flops 560204800 | bytes 21635072 | tf_op jit(solution)/shard_map/while/body/eval_jaxpr/bhqk,bkhd->bqhd/dot_general | solution.py:140
  1002.9 53.3 %all_to_all.120 = bf16[8,1024,2,128]{3,2,0,1:T(2,128)(2,1)} all-to-all(bf16[8,1024,2,128]{3,2,0,1:T(2,128)(2,1)} %copy.50), channel_id=1, replica_groups=mesh['dp'=2,'sp'=8] {'sp'}, dimensions={1} | all-to-all | bytes 8388608 | tf_op jit(solution)/shard_map/all_to_all | solution.py:168
  1068.4 42.0 %all-to-all-done.5 = bf16[8,1024,2,128]{3,2,0,1:T(2,128)(2,1)} async-done(((bf16[8,1024,2,128]{3,2,0,1:T(2,128)(2,1)}), bf16[8,1024,2,128]{3,2,0,1:T(2,128)(2,1)}, u32[]{:S(2)}, u32[]{:S(2)}) %all-to-all-start.5) | async-done | bytes 4194336 | tf_op jit(solution)/shard_map/all_to_all | solution.py:167
  1117.3 20.0 %multiply_add_fusion.1 = (f32[8,128,16,64]{3,1,0,2:T(8,128)S(1)}, f32[8,128,16,64]{3,1,0,2:T(8,128)}, f32[8,128,16,64]{3,1,0,2:T(8,128)}, f32[8,128,16,64]{3,1,0,2:T(8,128)}) fusion(f32[8,128,16,128]{3,1,0,2:T(8,128)} %bitcast.168, f32[8,128,64]{2,1,0:T(8,128)S(1)} %copy-done.10, f32[8,128,64]{2,1,0:T(8,128)S(1)} %copy-done.8, f32[8,128,16,128]{3,1,0,2:T(8,128)} %bitcast.167), kind=kLoop, calls=%fused_computation.118 | loop fusion | flops 12582912 | bytes 34078720 | tf_op jit(solution)/shard_map/add | solution.py:32
  1215.3 76.2 %all_to_all.121 = bf16[8,1024,2,128]{3,2,0,1:T(2,128)(2,1)S(1)} all-to-all(bf16[8,1024,2,128]{3,2,0,1:T(2,128)(2,1)} %copy.53), channel_id=1, replica_groups=mesh['dp'=2,'sp'=8] {'sp'}, dimensions={1} | all-to-all | bytes 8388608 | tf_op jit(solution)/shard_map/all_to_all | solution.py:169
  1304.5 15.5 convolution_bitcast_fusion.1
  1320.1 76.1 %all_to_all.122 = bf16[8,1024,2,128]{3,2,0,1:T(2,128)(2,1)S(1)} all-to-all(bf16[8,1024,2,128]{3,2,0,1:T(2,128)(2,1)} %get-tuple-element.305), channel_id=1, replica_groups=mesh['dp'=2,'sp'=8] {'sp'}, dimensions={1} | all-to-all | bytes 8388608 | tf_op jit(solution)/shard_map/all_to_all | solution.py:162
  1454.7 19.3 %fusion.89 = (f32[2048]{0:T(1024)S(1)}, f32[8,128]{1,0:T(8,128)S(1)}, f32[8,128,2048]{2,1,0:T(8,128)}) fusion(bf16[8,128,2048]{2,1,0:T(8,128)(2,1)} %param.14, f32[8,128]{1,0:T(8,128)S(1)} %copy-done.26, f32[2048]{0:T(1024)S(1)} %copy-done.24, f32[8,128,2048]{2,1,0:T(8,128)} %fusion.98, f32[8,128,2048]{2,1,0:T(8,128)} %fusion.102, ...), kind=kOutput, calls=%fused_computation.83 | convolution fusion | flops 8608805888 | bytes 41967616 | tf_op jit(solution)/shard_map/bse,de->bsd/dot_general | solution.py:52
  1474.0 21.9 %all-reduce.3 = (f32[2048]{0:T(1024)S(1)}, f32[2048]{0:T(1024)S(1)}, f32[2048]{0:T(1024)S(1)}) all-reduce(f32[2048]{0:T(1024)S(1)} %get-tuple-element.360, f32[2048]{0:T(1024)S(1)} %copy-done.22, f32[2048]{0:T(1024)S(1)} %get-tuple-element.356), channel_id=2, replica_groups=mesh['dp'=2,'sp'=8] {'sp'}, use_global_device_ids=true, to_apply=%region_14.15.clone | all-reduce | flops 6144 | bytes 49152
  1525.5 90.2 %reduce-scatter.11.cloned.1.call-done = f32[256,2048]{1,0:T(8,128)} async-done(((f32[2048,2048]{1,0:T(8,128)}), f32[256,2048]{1,0:T(8,128)}) %reduce-scatter.11.cloned.1.call-update) | async-done | bytes 2097168 | tf_op jit(solution)/shard_map/reduce_scatter | solution.py:153
  (281 shorter events, 658.2 us)
Async XLA Ops:
  10.3 168.6 %copy-start.25 = (f32[8,128]{1,0:T(8,128)}, f32[8,128]{1,0:T(8,128)S(1)}, u32[]{:S(2)}) copy-start(f32[8,128]{1,0:T(8,128)S(1)} %add_rsqrt_fusion.2) | copy-start | bytes 12292
  11.0 167.9 %copy-start.23 = (f32[2048]{0:T(1024)}, f32[2048]{0:T(1024)S(1)}, u32[]{:S(2)}) copy-start(f32[2048]{0:T(1024)S(1)} %convert_element_type.116) | copy-start | bytes 24580
  11.0 12.8 copy-start.27
  34.9 13.0 copy-start.28
  53.8 8.6 copy-start.29
  81.3 31.2 %copy-start.7 = (f32[8,128,64]{2,1,0:T(8,128)}, f32[8,128,64]{2,1,0:T(8,128)S(1)}, u32[]{:S(2)}) copy-start(f32[8,128,64]{2,1,0:T(8,128)S(1)} %get-tuple-element.413) | copy-start | bytes 786436
  81.4 31.2 %copy-start.9 = (f32[8,128,64]{2,1,0:T(8,128)}, f32[8,128,64]{2,1,0:T(8,128)S(1)}, u32[]{:S(2)}) copy-start(f32[8,128,64]{2,1,0:T(8,128)S(1)} %get-tuple-element.414) | copy-start | bytes 786436
  118.8 54.6 %all-to-all-start.1 = ((bf16[8,128,16,128]{3,1,0,2:T(8,128)(2,1)}), bf16[8,128,16,128]{3,1,0,2:T(8,128)(2,1)}, u32[]{:S(2)}, u32[]{:S(2)}) async-start(bf16[8,128,16,128]{3,1,0,2:T(8,128)(2,1)} %pad_maximum_fusion.1), calls=%async_computation.1 | async-start | bytes 8388608 | tf_op jit(solution)/shard_map/all_to_all | solution.py:159
  173.4 54.2 %all-to-all-start = ((bf16[8,128,16,128]{3,1,0,2:T(8,128)(2,1)}), bf16[8,128,16,128]{3,1,0,2:T(8,128)(2,1)}, u32[]{:S(2)}, u32[]{:S(2)}) async-start(bf16[8,128,16,128]{3,1,0,2:T(8,128)(2,1)} %pad_maximum_fusion), calls=%async_computation | async-start | bytes 8388608 | tf_op jit(solution)/shard_map/all_to_all | solution.py:158
  227.6 54.2 %all-to-all-start.2 = ((bf16[8,128,16,128]{3,1,0,2:T(8,128)(2,1)}), bf16[8,128,16,128]{3,1,0,2:T(8,128)(2,1)}, u32[]{:S(2)}, u32[]{:S(2)}) async-start(bf16[8,128,16,128]{3,1,0,2:T(8,128)(2,1)} %bitcast.176), calls=%async_computation.2 | async-start | bytes 8388608 | tf_op jit(solution)/shard_map/all_to_all | solution.py:160
  281.8 103.8 %all-to-all-start.4 = ((bf16[8,128,16,128]{3,1,0,2:T(8,128)(2,1)}), bf16[8,128,16,128]{3,1,0,2:T(8,128)(2,1)}, u32[]{:S(2)}, u32[]{:S(2)}) async-start(bf16[8,128,16,128]{3,1,0,2:T(8,128)(2,1)} %bitcast.175), calls=%async_computation.4 | async-start | bytes 8388608 | tf_op jit(solution)/shard_map/all_to_all | solution.py:166
  394.6 7.0 copy-start.1
  541.5 7.0 copy-start.1
  1056.2 54.3 %all-to-all-start.5 = ((bf16[8,1024,2,128]{3,2,0,1:T(2,128)(2,1)}), bf16[8,1024,2,128]{3,2,0,1:T(2,128)(2,1)}, u32[]{:S(2)}, u32[]{:S(2)}) async-start(bf16[8,1024,2,128]{3,2,0,1:T(2,128)(2,1)} %get-tuple-element.307), calls=%async_computation.5 | async-start | bytes 8388608 | tf_op jit(solution)/shard_map/all_to_all | solution.py:167
  1061.8 458.5 %reduce-scatter.5.cloned.1.call-start = ((), (), s32[]{:S(2)}) async-start(), calls=%async_computation.12 | async-start | bytes 18874368 | tf_op jit(solution)/shard_map/reduce_scatter | solution.py:153
  1068.4 48.8 %copy-start.8 = (f32[8,128,64]{2,1,0:T(8,128)S(1)}, f32[8,128,64]{2,1,0:T(8,128)}, u32[]{:S(2)}) copy-start(f32[8,128,64]{2,1,0:T(8,128)} %copy-done.7) | copy-start | bytes 786436
  1068.4 48.8 %copy-start.10 = (f32[8,128,64]{2,1,0:T(8,128)S(1)}, f32[8,128,64]{2,1,0:T(8,128)}, u32[]{:S(2)}) copy-start(f32[8,128,64]{2,1,0:T(8,128)} %copy-done.9) | copy-start | bytes 786436
  1110.4 26.8 %slice-start = ((s8[8388608]{0:T(1024)(128)(4,1)}), s8[4194304]{0:T(1024)(128)(4,1)S(1)}, s32[]{:S(2)}) async-start(s8[8388608]{0:T(1024)(128)(4,1)} %bitcast.164), calls=%async_computation.16 | async-start | bytes 8388608
  1117.2 20.0 %slice-start.1 = ((s8[8388608]{0:T(1024)(128)(4,1)}), s8[4194304]{0:T(1024)(128)(4,1)S(1)}, s32[]{:S(2)}) async-start(s8[8388608]{0:T(1024)(128)(4,1)} %bitcast.164), calls=%async_computation.17 | async-start | bytes 8388608
  1117.2 20.0 %copy-start.17 = (f32[2048]{0:T(1024)S(1)}, f32[2048]{0:T(1024)}, u32[]{:S(2)}) copy-start(f32[2048]{0:T(1024)} %copy-done.16) | copy-start | bytes 24580
  1117.2 20.0 %copy-start.21 = (f32[8,128]{1,0:T(8,128)S(1)}, f32[8,128]{1,0:T(8,128)}, u32[]{:S(2)}) copy-start(f32[8,128]{1,0:T(8,128)} %copy-done.20) | copy-start | bytes 12292
  1143.8 8.2 copy-start.4
  1143.8 8.2 copy-start.24
  1143.8 8.2 copy-start.26
  1166.8 353.4 %reduce-scatter.7.cloned.1.call-start = ((), (), s32[]{:S(2)}) async-start(), calls=%async_computation.13 | async-start | bytes 18874368 | tf_op jit(solution)/shard_map/reduce_scatter | solution.py:153
  1177.8 12.3 copy-start.5
  1202.7 322.8 %reduce-scatter.9.cloned.1.call-start = ((), (), s32[]{:S(2)}) async-start(), calls=%async_computation.14 | async-start | bytes 18874368 | tf_op jit(solution)/shard_map/reduce_scatter | solution.py:153
  1320.0 295.7 %reduce-scatter.11.cloned.1.call-start = ((), (), s32[]{:S(2)}) async-start(), calls=%async_computation.15 | async-start | bytes 18874368 | tf_op jit(solution)/shard_map/reduce_scatter | solution.py:153
  1426.4 14.8 copy-start.13
  1454.7 19.3 %copy-start.22 = (f32[2048]{0:T(1024)S(1)}, f32[2048]{0:T(1024)}, u32[]{:S(2)}) copy-start(f32[2048]{0:T(1024)} %get-tuple-element.358) | copy-start | bytes 24580
  1497.8 8.8 copy-start.6
  1497.8 9.8 copy-start.12
  (24 other events, 132.6 us)
Sparse Core Ops, SparseCore 0:
  1166.9 132.6 reduce-scatter.4
  1302.5 132.3 reduce-scatter.6
  1437.8 87.6 reduce-scatter.8
  1528.3 87.3 reduce-scatter.10
where the time goes:
time: 1630 us; the launch traced here: 1620 us
  matrix products  810 us (50%)
  waiting for transfers between devices  237 us (15%)
  blocking collectives  227 us (14%)
  local copies, waits for them, and re-layouts  160 us (10%)
  other arithmetic  143 us (9%)
  starting transfers between devices  29 us (2%)
    dot_general x8, matrix products, block_step(): jnp.einsum('bhqk,bqhd->bkhd', ds_bf, q_blk, preferred_element_type=jnp.fl...  204 us
    dot_general x8, matrix products, block_step(): jnp.einsum('bhqk,bkhd->bqhd', ds_bf, k_all, preferred_element_type=jnp.fl...  183 us
    dot_general x8, matrix products, block_step(): jnp.einsum('bhqk,bqhd->bkhd', prob_bf, do_blk, preferred_element_type=jnp...  96.5 us
    reduce_scatter x4, waiting for transfers between devices, sum_rows(): return lax.psum_scatter(partial_sum, 'sp', scatter_dimension=0, tiled=True)  95.5 us
    dot_general x16, matrix products, block_step(): jnp.einsum('bqhd,bkhd->bhqk', q_blk, k_all, preferred_element_type=jnp.fl...  89.2 us
    all_to_all x1, blocking collectives, device_step(): d_v = to_tokens(dv_acc.astype(jnp.bfloat16))  76.2 us
    all_to_all x1, blocking collectives, device_step(): attended = to_tokens(out_all).reshape(n_batch, loc_len, d_model)  76.1 us
    dot_general x4, matrix products, project_back(): jnp.einsum('bse,de->bsd', grads_in, weight, preferred_element_type=jnp.fl...  60.1 us
  transfers between devices with their start and end apart: 9, of which 6 were waited for; matrix products, arithmetic and copies ran while one was open for 20% of the time, Pallas kernels for 0%

commit v1 on v0

v1 whole, which is shorter than its diff:
```python
import functools
import math
import jax
import jax.numpy as jnp
from jax import lax
from jax.experimental import pallas as pl
from jax.experimental.pallas import tpu as pltpu
from jax.sharding import PartitionSpec as P

HEAD_DIM = 128
NORM_EPS = 1e-5
ROPE_BASE = 10000.0
NEG_BIG = -1e30
LOG2E = math.log2(math.e)
Q_BLOCK = 256


def rope_tables(positions):
    half_dim = HEAD_DIM // 2
    inv_freq = ROPE_BASE ** (-jnp.arange(half_dim, dtype=jnp.float32) * (2.0 / HEAD_DIM))
    angles = positions.astype(jnp.float32)[..., None] * inv_freq
    return jnp.cos(angles)[:, None, :], jnp.sin(angles)[:, None, :]


def rope_apply(values, cos_t, sin_t):
    half_dim = values.shape[-1] // 2
    first_half = values[..., :half_dim]
    second_half = values[..., half_dim:]
    return jnp.concatenate([first_half * cos_t - second_half * sin_t, second_half * cos_t + first_half * sin_t], axis=-1)


def rope_revert(grads_in, cos_t, sin_t):
    half_dim = grads_in.shape[-1] // 2
    first_half = grads_in[..., :half_dim]
    second_half = grads_in[..., half_dim:]
    return jnp.concatenate([first_half * cos_t + second_half * sin_t, second_half * cos_t - first_half * sin_t], axis=-1)


def rms_forward(values, gain_vec):
    inv_rms = lax.rsqrt(jnp.mean(values * values, axis=-1, keepdims=True) + NORM_EPS)
    normed = values * inv_rms
    return normed * gain_vec.astype(jnp.float32), normed, inv_rms


def rms_backward(d_out, normed, inv_rms, gain_vec):
    d_normed = d_out * gain_vec.astype(jnp.float32)
    d_in = inv_rms * (d_normed - normed * jnp.mean(d_normed * normed, axis=-1, keepdims=True))
    return d_in, d_out * normed


def dot_nn(a, b):
    return lax.dot_general(a, b, (((1,), (0,)), ((), ())), preferred_element_type=jnp.float32)


def dot_nt(a, b):
    return lax.dot_general(a, b, (((1,), (1,)), ((), ())), preferred_element_type=jnp.float32)


def dot_tn(a, b):
    return lax.dot_general(a, b, (((0,), (0,)), ((), ())), preferred_element_type=jnp.float32)


def attn_fwd_kernel(seq_len, q_ref, k_ref, v_ref, o_ref, lse_ref):
    scale2 = LOG2E * HEAD_DIM ** -0.5
    for start in range(0, seq_len, Q_BLOCK):
        stop = start + Q_BLOCK
        q_blk = q_ref[start:stop, :]
        s_diag = dot_nt(k_ref[start:stop, :], q_blk)
        key_i = lax.broadcasted_iota(jnp.int32, s_diag.shape, 0)
        qry_i = lax.broadcasted_iota(jnp.int32, s_diag.shape, 1)
        s_diag = jnp.where(key_i <= qry_i, s_diag, NEG_BIG)
        m = jnp.max(s_diag, axis=0, keepdims=True)
        if start:
            s_past = dot_nt(k_ref[0:start, :], q_blk)
            m = jnp.maximum(m, jnp.max(s_past, axis=0, keepdims=True))
        m2 = m * scale2
        p_diag = jnp.exp2(s_diag * scale2 - m2)
        l = jnp.sum(p_diag, axis=0, keepdims=True)
        acc = dot_tn(v_ref[start:stop, :], p_diag.astype(jnp.bfloat16))
        if start:
            p_past = jnp.exp2(s_past * scale2 - m2)
            l = l + jnp.sum(p_past, axis=0, keepdims=True)
            acc = acc + dot_tn(v_ref[0:start, :], p_past.astype(jnp.bfloat16))
        o_ref[start:stop, :] = (acc / l).T.astype(o_ref.dtype)
        lse_ref[0, :, start:stop] = m2 + jnp.log2(l)


def attn_bwd_kernel(seq_len, q_ref, k_ref, v_ref, do_ref, lse_ref, dq_ref, dk_ref, dv_ref, dk_acc, dv_acc):
    scale = HEAD_DIM ** -0.5
    scale2 = LOG2E * scale
    dk_acc[...] = jnp.zeros_like(dk_acc)
    dv_acc[...] = jnp.zeros_like(dv_acc)
    for start in range(0, seq_len, Q_BLOCK):
        stop = start + Q_BLOCK
        q_blk = q_ref[start:stop, :]
        do_blk = do_ref[start:stop, :]
        lse = lse_ref[0, :, start:stop]
        k_all = k_ref[0:stop, :]
        s = dot_nt(k_all, q_blk)
        p = jnp.exp2(s * scale2 - lse)
        key_i = lax.broadcasted_iota(jnp.int32, (Q_BLOCK, Q_BLOCK), 0)
        qry_i = lax.broadcasted_iota(jnp.int32, (Q_BLOCK, Q_BLOCK), 1)
        p_diag = jnp.where(key_i <= qry_i, p[start:stop, :], 0.0)
        p = jnp.concatenate([p[0:start, :], p_diag], axis=0) if start else p_diag
        dp = dot_nt(v_ref[0:stop, :], do_blk)
        delta = jnp.sum(p * dp, axis=0, keepdims=True)
        ds = (p * (dp - delta) * scale).astype(jnp.bfloat16)
        dv_acc[0:stop, :] += dot_nn(p.astype(jnp.bfloat16), do_blk)
        dk_acc[0:stop, :] += dot_nn(ds, q_blk)
        dq_ref[start:stop, :] = dot_tn(k_all, ds).T.astype(dq_ref.dtype)
    dk_ref[...] = dk_acc[...].astype(dk_ref.dtype)
    dv_ref[...] = dv_acc[...].astype(dv_ref.dtype)


def attend_forward(q, k, v):
    seq_len, d_model = q.shape
    n_heads = d_model // HEAD_DIM
    head_spec = pl.BlockSpec((seq_len, HEAD_DIM), lambda h: (0, h))
    flops = 2 * 2 * seq_len * seq_len * d_model
    return pl.pallas_call(
        functools.partial(attn_fwd_kernel, seq_len),
        grid=(n_heads,),
        out_shape=(jax.ShapeDtypeStruct(q.shape, jnp.bfloat16), jax.ShapeDtypeStruct((n_heads, 1, seq_len), jnp.float32)),
        in_specs=[head_spec] * 3,
        out_specs=(head_spec, pl.BlockSpec((1, 1, seq_len), lambda h: (h, 0, 0))),
        cost_estimate=pl.CostEstimate(flops=flops, bytes_accessed=4 * q.size * 2, transcendentals=seq_len * seq_len * n_heads),
        name="attn_fwd",
    )(q, k, v)


def attend_backward(q, k, v, d_out, lse):
    seq_len, d_model = q.shape
    n_heads = d_model // HEAD_DIM
    head_spec = pl.BlockSpec((seq_len, HEAD_DIM), lambda h: (0, h))
    flops = 5 * 2 * seq_len * seq_len * d_model
    return pl.pallas_call(
        functools.partial(attn_bwd_kernel, seq_len),
        grid=(n_heads,),
        out_shape=(jax.ShapeDtypeStruct(q.shape, jnp.bfloat16),) * 3,
        in_specs=[head_spec] * 4 + [pl.BlockSpec((1, 1, seq_len), lambda h: (h, 0, 0))],
        out_specs=(head_spec,) * 3,
        scratch_shapes=[pltpu.VMEM((seq_len, HEAD_DIM), jnp.float32)] * 2,
        cost_estimate=pl.CostEstimate(flops=flops, bytes_accessed=7 * q.size * 2, transcendentals=seq_len * seq_len * n_heads),
        name="attn_bwd",
    )(q, k, v, d_out, lse)


def solution(mesh):
    to_seqs = functools.partial(lax.all_to_all, axis_name='sp', split_axis=0, concat_axis=1, tiled=True)
    to_tokens = functools.partial(lax.all_to_all, axis_name='sp', split_axis=1, concat_axis=0, tiled=True)

    def sum_rows(partial_sum):
        return lax.psum_scatter(partial_sum, 'sp', scatter_dimension=0, tiled=True)

    def device_step(x_loc, gy_loc, pos_loc, g_norm, w_query, w_key, w_value, w_out, g_query, g_key):
        d_model = x_loc.shape[-1]
        x_seq = to_seqs(x_loc)
        pos_seq = to_seqs(pos_loc)
        gy_seq = to_seqs(gy_loc)
        n_seq, seq_len = pos_seq.shape
        rows = n_seq * seq_len
        cos_t, sin_t = rope_tables(pos_seq.reshape(rows))
        x_bf = x_seq.reshape(rows, d_model)
        gy = gy_seq.reshape(rows, d_model)
        heads = (rows, d_model // HEAD_DIM, HEAD_DIM)

        hid_f, x_hat, x_inv = rms_forward(x_bf.astype(jnp.float32), g_norm)
        hidden = hid_f.astype(jnp.bfloat16)
        q_nrm, q_hat, q_inv = rms_forward(dot_nn(hidden, w_query), g_query)
        k_nrm, k_hat, k_inv = rms_forward(dot_nn(hidden, w_key), g_key)
        q_rot = rope_apply(q_nrm.reshape(heads), cos_t, sin_t).astype(jnp.bfloat16).reshape(rows, d_model)
        k_rot = rope_apply(k_nrm.reshape(heads), cos_t, sin_t).astype(jnp.bfloat16).reshape(rows, d_model)
        v_val = dot_nn(hidden, w_value).astype(jnp.bfloat16)

        outs = [attend_forward(q_rot[i:i + seq_len], k_rot[i:i + seq_len], v_val[i:i + seq_len]) for i in range(0, rows, seq_len)]
        attended = outs[0][0] if n_seq == 1 else jnp.concatenate([o[0] for o in outs])
        grad_wo = sum_rows(dot_tn(attended, gy))
        y_seq = (x_bf.astype(jnp.float32) + dot_nn(attended, w_out)).astype(jnp.bfloat16)
        y_out = to_tokens(y_seq.reshape(n_seq, seq_len, d_model))
        d_attn = dot_nt(gy, w_out).astype(jnp.bfloat16)

        bwd = [attend_backward(q_rot[i:i + seq_len], k_rot[i:i + seq_len], v_val[i:i + seq_len], d_attn[i:i + seq_len], outs[i // seq_len][1]) for i in range(0, rows, seq_len)]
        d_q, d_k, d_v = bwd[0] if n_seq == 1 else [jnp.concatenate([b[j] for b in bwd]) for j in range(3)]

        dq_rot = rope_revert(d_q.astype(jnp.float32).reshape(heads), cos_t, sin_t).reshape(rows, d_model)
        dk_rot = rope_revert(d_k.astype(jnp.float32).reshape(heads), cos_t, sin_t).reshape(rows, d_model)
        dq_raw, q_terms = rms_backward(dq_rot, q_hat, q_inv, g_query)
        dk_raw, k_terms = rms_backward(dk_rot, k_hat, k_inv, g_key)
        dq_bf = dq_raw.astype(jnp.bfloat16)
        dk_bf = dk_raw.astype(jnp.bfloat16)
        grad_wv = sum_rows(dot_tn(hidden, d_v))
        grad_wk = sum_rows(dot_tn(hidden, dk_bf))
        grad_wq = sum_rows(dot_tn(hidden, dq_bf))
        d_hidden = dot_nt(dq_bf, w_query) + dot_nt(dk_bf, w_key) + dot_nt(d_v, w_value)
        d_hidden = d_hidden.astype(jnp.bfloat16).astype(jnp.float32)
        dx_norm, n_terms = rms_backward(d_hidden, x_hat, x_inv, g_norm)
        gx_seq = (gy.astype(jnp.float32) + dx_norm).astype(jnp.bfloat16)
        grad_x = to_tokens(gx_seq.reshape(n_seq, seq_len, d_model))
        gains = [sum_rows(jnp.sum(t, axis=0)) for t in (n_terms, q_terms, k_terms)]
        return y_out, grad_x, gains[0], grad_wq, grad_wk, grad_wv, grad_wo, gains[1], gains[2]

    seq_spec = P('dp', 'sp', None)
    mat_rep = P(None, None)
    vec_rep = P(None)
    row_spec = P(('dp', 'sp'), None)
    vec_spec = P(('dp', 'sp'))
    return jax.shard_map(device_step, mesh=mesh, in_specs=(seq_spec, seq_spec, P('dp', 'sp'), vec_rep, mat_rep, mat_rep, mat_rep, mat_rep, vec_rep, vec_rep), out_specs=(seq_spec, seq_spec, vec_spec, row_spec, row_spec, row_spec, row_spec, vec_spec, vec_spec), check_vma=False)
```

time: 1630 us -> 816 us (0.50)
  matrix products: 810 us -> 167 us
  blocking collectives: 227 us -> 95 us
  waiting for transfers between devices: 237 us -> 109 us
  Pallas kernels: 0 us -> 72.6 us
  other arithmetic: 143 us -> 189 us
  local copies, waits for them, and re-layouts: 160 us -> 142 us
    dot_general x68 -> x12, matrix products: 810 us -> 167 us  [the longest x4 60.4 us: dot_nt(): lax.dot_general(a, b, (((1,), (1,)), ((), ())), preferred_element_type=jn...]
    all_to_all x3 -> x1, blocking collectives: 206 us -> 10.6 us  [device_step(): pos_seq = to_seqs(pos_loc)]
    all_to_all x5 -> x4, waiting for transfers between devices: 141 us -> 46.7 us  [the longest x1 46.7 us: device_step(): x_seq = to_seqs(x_loc)]
    pallas_call x0 -> x2, Pallas kernels: none -> 72.6 us  [the longest x1 41.3 us: attend_backward(): pl.pallas_call(functools.partial(attn_bwd_kernel, seq_len), grid=(n_heads...]
    unnamed x3 -> x6, other arithmetic: 0.01 us -> 69.1 us
    unnamed x68 -> x67, local copies, waits for them, and re-layouts: 23.4 us -> 92.4 us
    unnamed x1, blocking collectives: 21.9 us -> 84.4 us
    reduce_scatter x4, waiting for transfers between devices: 95.5 us -> 62.2 us  [sum_rows(): return lax.psum_scatter(partial_sum, 'sp', scatter_dimension=0, tiled=True)]
  transfers between devices with their start and end apart: 9 -> 8, of which waited for: 6 -> 2; matrix products, arithmetic and copies ran while one was open for 20% -> 49% of each run, Pallas kernels for 0% -> 0%
where the time goes in v1:
time: 816 us; the launch traced here: 811 us
  other arithmetic  189 us (23%)
  matrix products  167 us (20%)
  local copies, waits for them, and re-layouts  142 us (17%)
  waiting for transfers between devices  109 us (13%)
  blocking collectives  95 us (12%)
  Pallas kernels  72.6 us (9%)
  starting transfers between devices  21.5 us (3%)
  between operations  15.1 us (2%)
    unnamed x67, local copies, waits for them, and re-layouts  92.4 us
    unnamed x1, blocking collectives  84.4 us
    unnamed x6, other arithmetic  69.1 us
    reduce_scatter x4, waiting for transfers between devices, sum_rows(): return lax.psum_scatter(partial_sum, 'sp', scatter_dimension=0, tiled=True)  62.2 us
    dot_general x4, matrix products, dot_nt(): lax.dot_general(a, b, (((1,), (1,)), ((), ())), preferred_element_type=jn...  60.4 us
    dot_general x4, matrix products, dot_tn(): lax.dot_general(a, b, (((0,), (0,)), ((), ())), preferred_element_type=jn...  54.2 us
    dot_general x4, matrix products, dot_nn(): lax.dot_general(a, b, (((1,), (0,)), ((), ())), preferred_element_type=jn...  52.1 us
    all_to_all x1, waiting for transfers between devices, device_step(): x_seq = to_seqs(x_loc)  46.7 us
  transfers between devices with their start and end apart: 8, of which 2 were waited for; matrix products, arithmetic and copies ran while one was open for 49% of the time, Pallas kernels for 0%

profile of v1, /device:TPU:113, one launch (start us, length us, event | category | flops | bytes accessed | tf_op | source)
XLA Modules:
  0.0 811.0 jit_solution(14702046625494484021)
XLA Ops:
  7.2 10.6 %all_to_all.55 = s32[8,1,128]{2,1,0:T(1,128)S(1)} all-to-all(s32[8,1,128]{2,1,0:T(1,128)} %bitcast.125), channel_id=1, replica_groups=mesh['dp'=2,'sp'=8] {'sp'}, dimensions={0} | all-to-all | bytes 8192 | tf_op jit(solution)/shard_map/all_to_all | solution.py:158
  24.9 46.7 %all-to-all-done = bf16[8,128,2048]{2,1,0:T(8,128)(2,1)} async-done(((bf16[8,128,2048]{2,1,0:T(8,128)(2,1)}), bf16[8,128,2048]{2,1,0:T(8,128)(2,1)}, u32[]{:S(2)}, u32[]{:S(2)}) %all-to-all-start) | async-done | bytes 4194336 | tf_op jit(solution)/shard_map/all_to_all | solution.py:157
  84.0 12.9 %multiply_reduce_fusion.3 = (f32[1024]{0:T(1024)S(1)}, f32[1024,2048]{1,0:T(8,128)S(1)}) fusion(bf16[1024,2048]{1,0:T(8,128)(2,1)S(1)} %fusion.11, bf16[2048,2048]{1,0:T(8,128)(2,1)} %param.14), kind=kOutput, calls=%fused_computation.43 | convolution fusion | flops 8594127872 | bytes 20975616 | tf_op jit(solution)/shard_map/dot_general | solution.py:52
  109.6 13.4 %multiply_reduce_fusion.2 = (f32[1024]{0:T(1024)S(1)}, f32[1024,2048]{1,0:T(8,128)}) fusion(bf16[1024,2048]{1,0:T(8,128)(2,1)S(1)} %fusion.11, bf16[2048,2048]{1,0:T(8,128)(2,1)} %param.15), kind=kOutput, calls=%fused_computation.39 | convolution fusion | flops 8594127872 | bytes 20975616 | tf_op jit(solution)/shard_map/dot_general | solution.py:52
  130.4 8.6 %copy.27 = f32[128,8,16,128]{3,2,1,0:T(8,128)} copy(f32[128,8,16,128]{3,1,2,0:T(8,128)} %multiply_bitcast_fusion) | data formatting | bytes 16777216
  139.0 16.7 %subtract_convert_fusion = (bf16[1024,16,64]{2,1,0:T(8,128)(2,1)S(1)}, bf16[1024,16,64]{2,1,0:T(8,128)(2,1)}, bf16[1024,16,64]{2,1,0:T(8,128)(2,1)}, bf16[1024,16,64]{2,1,0:T(8,128)(2,1)}) fusion(f32[1024,16,128]{2,1,0:T(8,128)} %bitcast.104, f32[1024,64]{1,0:T(8,128)S(1)} %get-tuple-element.41, f32[1024,64]{1,0:T(8,128)S(1)} %get-tuple-element.40, ...), kind=kLoop, calls=%fused_computation.37 | loop fusion | flops 16777216 | bytes 25690112 | tf_op jit(solution)/shard_map/convert.3
  171.7 12.6 %convolution_convert_fusion.1.v_ref = bf16[1024,2048]{1,0:T(8,128)(2,1)} fusion(bf16[1024,2048]{1,0:T(8,128)(2,1)S(1)} %copy-done.5, bf16[2048,2048]{1,0:T(8,128)(2,1)} %param.16), kind=kOutput, calls=%fused_computation.49 | convolution fusion | flops 8592031744 | bytes 16777216 | tf_op jit(solution)/shard_map/dot_general | solution.py:52
  184.3 13.9 %convolution_convert_fusion.do_ref = bf16[1024,2048]{1,0:T(8,128)(2,1)} fusion(bf16[1024,2048]{1,0:T(8,128)(2,1)} %bitcast.5, bf16[2048,2048]{1,0:T(8,128)(2,1)} %param.17), kind=kOutput, calls=%fused_computation.48 | convolution fusion | flops 8592031744 | bytes 16777216 | tf_op jit(solution)/shard_map/dot_general | solution.py:56
  198.2 31.3 %attn_fwd.1 = (bf16[1024,2048]{1,0:T(8,128)(2,1)}, f32[16,1,1024]{2,1,0:T(1,128)}) custom-call(bf16[1024,2048]{1,0:T(8,128)(2,1)} %bitcast.120, bf16[1024,2048]{1,0:T(8,128)(2,1)} %bitcast.122, bf16[1024,2048]{1,0:T(8,128)(2,1)} %convolution_convert_fusion.1.v_ref), custom_call_target="tpu_custom_call" | custom-call | flops 8589934592 | bytes 16777216 | tf_op jit(solution)/shard_map/attn_fwd/pallas_call | solution.py:120
  229.5 41.3 %attn_bwd.1 = (bf16[1024,2048]{1,0:T(8,128)(2,1)}, bf16[1024,2048]{1,0:T(8,128)(2,1)}, bf16[1024,2048]{1,0:T(8,128)(2,1)}) custom-call(bf16[1024,2048]{1,0:T(8,128)(2,1)} %bitcast.121, bf16[1024,2048]{1,0:T(8,128)(2,1)} %bitcast.123, bf16[1024,2048]{1,0:T(8,128)(2,1)} %convolution_convert_fusion.1.v_ref, bf16[1024,2048]{1,0:T(8,128)(2,1)} %convolution_convert_fusion.do_ref, ...), custom_call_target="tpu_custom_call" | custom-call | flops 21474836480 | bytes 29360128 | tf_op jit(solution)/shard_map/attn_bwd/pallas_call | solution.py:136
  285.6 27.6 %multiply_add_fusion = (f32[1024,16,64]{2,1,0:T(8,128)}, f32[1024,16,64]{2,1,0:T(8,128)}, f32[1024,16,64]{2,1,0:T(8,128)}, f32[1024,16,64]{2,1,0:T(8,128)}) fusion(f32[1024,16,128]{2,1,0:T(8,128)} %bitcast.110, f32[1024,64]{1,0:T(8,128)S(1)} %get-tuple-element.41, f32[1024,64]{1,0:T(8,128)S(1)} %get-tuple-element.40, f32[1024,16,128]{2,1,0:T(8,128)} %bitcast.109), kind=kLoop, calls=%fused_computation.31 | loop fusion | flops 12582912 | bytes 34078720 | tf_op jit(solution)/shard_map/add | solution.py:36
  313.2 11.2 %pad_maximum_fusion.1 = f32[1024,16,128]{2,1,0:T(8,128)} fusion(f32[1024,16,64]{2,1,0:T(8,128)} %get-tuple-element.29, f32[1024,16,64]{2,1,0:T(8,128)} %get-tuple-element.28), kind=kLoop, calls=%fused_computation.16 | loop fusion | flops 2097152 | bytes 16777216 | tf_op jit(solution)/shard_map/concatenate | solution.py:36
  324.4 9.8 %fusion.7 = (f32[2048]{0:T(1024)}, f32[1024]{0:T(1024)S(1)}) fusion(f32[128,8,16,128]{3,2,1,0:T(8,128)} %bitcast.105, f32[1024,2048]{1,0:T(8,128)} %get-tuple-element.43, f32[1024]{0:T(1024)S(1)} %add_rsqrt_fusion, f32[2048]{0:T(1024)S(1)} %convert_element_type.84), kind=kLoop, calls=%fused_computation.11 | loop fusion | flops 12579840 | bytes 16801792 | tf_op jit(solution)/shard_map/reduce_sum | solution.py:199
  342.1 11.7 %fusion.18 = f32[2048,2048]{1,0:T(8,128)} fusion(bf16[1024,2048]{1,0:T(8,128)(2,1)S(1)} %copy-done.6, bf16[1024,2048]{1,0:T(8,128)(2,1)S(1)} %multiply_convert_fusion), kind=kOutput, calls=%fused_computation.65 | convolution fusion | flops 8589934592 | bytes 25165824 | tf_op jit(solution)/shard_map/dot_general | solution.py:60
  354.0 11.2 %pad_maximum_fusion = f32[1024,16,128]{2,1,0:T(8,128)} fusion(f32[1024,16,64]{2,1,0:T(8,128)} %get-tuple-element.36, f32[1024,16,64]{2,1,0:T(8,128)} %get-tuple-element.37), kind=kLoop, calls=%fused_computation.15 | loop fusion | flops 2097152 | bytes 16777216 | tf_op jit(solution)/shard_map/concatenate | solution.py:36
  365.2 10.1 %fusion.8 = (f32[2048]{0:T(1024)}, f32[1024]{0:T(1024)S(1)}) fusion(f32[128,8,16,128]{3,2,1,0:T(8,128)} %bitcast.107, f32[1024,2048]{1,0:T(8,128)} %copy-done.2, f32[1024]{0:T(1024)S(1)} %copy-done.16, f32[2048]{0:T(1024)S(1)} %copy-done.12), kind=kLoop, calls=%fused_computation.14 | loop fusion | flops 12579840 | bytes 16801792 | tf_op jit(solution)/shard_map/reduce_sum | solution.py:199
  383.1 11.7 %fusion.17 = f32[2048,2048]{1,0:T(8,128)} fusion(bf16[1024,2048]{1,0:T(8,128)(2,1)S(1)} %copy-done.7, bf16[1024,2048]{1,0:T(8,128)(2,1)S(1)} %multiply_convert_fusion.1), kind=kOutput, calls=%fused_computation.64 | convolution fusion | flops 8589934592 | bytes 25165824 | tf_op jit(solution)/shard_map/dot_general | solution.py:60
  394.9 15.2 %fusion.19 = f32[2048,2048]{1,0:T(8,128)} fusion(bf16[1024,2048]{1,0:T(8,128)(2,1)} %copy-done.4, bf16[1024,2048]{1,0:T(8,128)(2,1)} %get-tuple-element.18), kind=kOutput, calls=%fused_computation.66 | convolution fusion | flops 8589934592 | bytes 25165824 | tf_op jit(solution)/shard_map/dot_general | solution.py:60
  410.2 15.6 %fusion.20 = f32[2048,2048]{1,0:T(8,128)} fusion(bf16[1024,2048]{1,0:T(8,128)(2,1)} %get-tuple-element.14, bf16[1024,2048]{1,0:T(8,128)(2,1)} %bitcast.5), kind=kOutput, calls=%fused_computation.67 | convolution fusion | flops 8589934592 | bytes 25165824 | tf_op jit(solution)/shard_map/dot_general | solution.py:60
  426.0 14.6 %fusion.16 = f32[1024,2048]{1,0:T(8,128)} fusion(bf16[1024,2048]{1,0:T(8,128)(2,1)} %copy-done.8, bf16[2048,2048]{1,0:T(8,128)(2,1)} %param.15), kind=kOutput, calls=%fused_computation.63 | convolution fusion | flops 8589934592 | bytes 20971520 | tf_op jit(solution)/shard_map/dot_general | solution.py:56
  440.6 13.2 %fusion.15 = f32[1024,2048]{1,0:T(8,128)} fusion(bf16[1024,2048]{1,0:T(8,128)(2,1)S(1)} %copy-done.10, bf16[2048,2048]{1,0:T(8,128)(2,1)} %param.14), kind=kOutput, calls=%fused_computation.62 | convolution fusion | flops 8589934592 | bytes 20971520 | tf_op jit(solution)/shard_map/dot_general | solution.py:56
  453.8 18.6 %fusion.6 = (f32[2048]{0:T(1024)S(1)}, f32[1024]{0:T(1024)S(1)}, bf16[1024,2048]{1,0:T(8,128)(2,1)}) fusion(bf16[8,128,2048]{2,1,0:T(8,128)(2,1)} %all-to-all-done, f32[1024]{0:T(1024)S(1)} %copy-done.18, f32[2048]{0:T(1024)S(1)} %copy-done.14, bf16[1024,2048]{1,0:T(8,128)(2,1)} %get-tuple-element.18, bf16[2048,2048]{1,0:T(8,128)(2,1)} %param.16, ...), kind=kOutput, calls=%fused_computation.8 | convolution fusion | flops 8613000192 | bytes 37773312 | tf_op jit(solution)/shard_map/dot_general | solution.py:56
  478.5 24.7 %copy.45 = bf16[1,1024,2048]{2,0,1:T(2,128)(2,1)} copy(bf16[1,1024,2048]{2,1,0:T(8,128)(2,1)S(1)} %bitcast.115) | data formatting | bytes 8388608 | tf_op jit(solution)/shard_map/reshape | solution.py:198
  503.7 26.7 %reduce.5 = bf16[1024,2048]{1,0:T(8,128)(2,1)} reduce(bf16[1024,1,2048]{2,1,0:T(2,128)(2,1)} %bitcast.111, bf16[]{:T(256)} %broadcast.119), dimensions={1}, to_apply=%bitcast.101.reduce_sub_computation | reduce | bytes 8388610
  543.5 13.1 %fusion.14 = bf16[1,1024,2048]{2,1,0:T(8,128)(2,1)S(1)} fusion(bf16[1024,2048]{1,0:T(8,128)(2,1)} %get-tuple-element.14, bf16[2048,2048]{1,0:T(8,128)(2,1)} %param.17, bf16[8,128,2048]{2,1,0:T(8,128)(2,1)} %all-to-all-done), kind=kOutput, calls=%fused_computation.50 | convolution fusion | flops 8596226048 | bytes 20971520 | tf_op jit(solution)/shard_map/dot_general | solution.py:52
  556.7 24.7 %copy.46 = bf16[1,1024,2048]{2,0,1:T(2,128)(2,1)} copy(bf16[1,1024,2048]{2,1,0:T(8,128)(2,1)S(1)} %fusion.14) | data formatting | bytes 8388608 | tf_op jit(solution)/shard_map/reshape | solution.py:179
  581.3 26.7 %reduce.4 = bf16[1024,2048]{1,0:T(8,128)(2,1)} reduce(bf16[1024,1,2048]{2,1,0:T(2,128)(2,1)} %bitcast.112, bf16[]{:T(256)} %broadcast.119), dimensions={1}, to_apply=%bitcast.102.reduce_sub_computation | reduce | bytes 8388610
  622.0 84.4 %all-reduce.3 = (f32[2048]{0:T(1024)S(1)}, f32[2048]{0:T(1024)S(1)}, f32[2048]{0:T(1024)S(1)}) all-reduce(f32[2048]{0:T(1024)S(1)} %get-tuple-element.23, f32[2048]{0:T(1024)S(1)} %copy-done.20, f32[2048]{0:T(1024)S(1)} %copy-done.19), channel_id=2, replica_groups=mesh['dp'=2,'sp'=8] {'sp'}, use_global_device_ids=true, to_apply=%region_7.0.clone | all-reduce | flops 6144 | bytes 49152
  708.4 8.8 %reshape.218 = bf16[1024,1,2048]{2,1,0:T(2,128)(2,1)} reshape(bf16[8,2,131072]{2,1,0:T(2,128)(2,1)} %all-to-all-done.4) | data formatting | bytes 8388608
  725.2 8.8 %reshape.216 = bf16[1024,1,2048]{2,1,0:T(2,128)(2,1)} reshape(bf16[8,2,131072]{2,1,0:T(2,128)(2,1)} %all-to-all-done.2) | data formatting | bytes 8388608
  733.9 8.0 copy.23
  742.0 62.2 %reduce-scatter.11.cloned.1.call-done = f32[256,2048]{1,0:T(8,128)} async-done(((f32[2048,2048]{1,0:T(8,128)}), f32[256,2048]{1,0:T(8,128)}) %reduce-scatter.11.cloned.1.call-update) | async-done | bytes 2097168 | tf_op jit(solution)/shard_map/reduce_scatter | solution.py:153
  (103 shorter events, 129.2 us)
Async XLA Ops:
  7.2 15.8 %copy-start.21 = (bf16[2048]{0:T(1024)(128)(2,1)S(1)}, bf16[2048]{0:T(1024)(128)(2,1)}, u32[]{:S(2)}) copy-start(bf16[2048]{0:T(1024)(128)(2,1)} %param.13) | copy-start | bytes 12292
  7.2 15.8 %copy-start.22 = (bf16[2048]{0:T(1024)(128)(2,1)S(1)}, bf16[2048]{0:T(1024)(128)(2,1)}, u32[]{:S(2)}) copy-start(bf16[2048]{0:T(1024)(128)(2,1)} %param.18) | copy-start | bytes 12292
  7.2 15.8 %copy-start.23 = (bf16[2048]{0:T(1024)(128)(2,1)S(1)}, bf16[2048]{0:T(1024)(128)(2,1)}, u32[]{:S(2)}) copy-start(bf16[2048]{0:T(1024)(128)(2,1)} %param.19) | copy-start | bytes 12292
  17.8 53.8 %all-to-all-start = ((bf16[8,128,2048]{2,1,0:T(8,128)(2,1)}), bf16[8,128,2048]{2,1,0:T(8,128)(2,1)}, u32[]{:S(2)}, u32[]{:S(2)}) async-start(bf16[8,128,2048]{2,1,0:T(8,128)(2,1)} %param.10), calls=%async_computation | async-start | bytes 8388608 | tf_op jit(solution)/shard_map/all_to_all | solution.py:157
  23.0 61.0 %copy-start.13 = (f32[2048]{0:T(1024)}, f32[2048]{0:T(1024)S(1)}, u32[]{:S(2)}) copy-start(f32[2048]{0:T(1024)S(1)} %convert_element_type.78) | copy-start | bytes 24580
  23.0 74.0 %copy-start.11 = (f32[2048]{0:T(1024)}, f32[2048]{0:T(1024)S(1)}, u32[]{:S(2)}) copy-start(f32[2048]{0:T(1024)S(1)} %convert_element_type.80) | copy-start | bytes 24580
  71.6 112.7 %all-to-all-start.3 = ((bf16[8,128,2048]{2,1,0:T(8,128)(2,1)}), bf16[8,128,2048]{2,1,0:T(8,128)(2,1)}, u32[]{:S(2)}, u32[]{:S(2)}) async-start(bf16[8,128,2048]{2,1,0:T(8,128)(2,1)} %param.11), calls=%async_computation.3 | async-start | bytes 8388608 | tf_op jit(solution)/shard_map/all_to_all | solution.py:159
  77.1 664.8 %reduce-scatter.7.cloned.1.call-start = ((), (), s32[]{:S(2)}) async-start(), calls=%async_computation.10 | async-start | bytes 18874368 | tf_op jit(solution)/shard_map/reduce_scatter | solution.py:153
  80.8 16.2 %copy-start.17 = (f32[1024]{0:T(1024)}, f32[1024]{0:T(1024)S(1)}, u32[]{:S(2)}) copy-start(f32[1024]{0:T(1024)S(1)} %rsqrt_bitcast_fusion) | copy-start | bytes 12292
  84.0 25.6 %copy-start.4 = (bf16[1024,2048]{1,0:T(8,128)(2,1)}, bf16[1024,2048]{1,0:T(8,128)(2,1)S(1)}, u32[]{:S(2)}) copy-start(bf16[1024,2048]{1,0:T(8,128)(2,1)S(1)} %fusion.11) | copy-start | bytes 12582916
  96.9 3.2 copy-start.2
  97.0 7.2 copy-start.15
  163.3 8.3 %copy-start.5 = (bf16[1024,2048]{1,0:T(8,128)(2,1)S(1)}, bf16[1024,2048]{1,0:T(8,128)(2,1)}, u32[]{:S(2)}) copy-start(bf16[1024,2048]{1,0:T(8,128)(2,1)} %copy-done.4) | copy-start | bytes 12582916
  274.0 5.3 copy-start.3
  324.4 9.9 %copy-start = (f32[1024,16,128]{2,1,0:T(8,128)S(1)}, f32[1024,16,128]{2,1,0:T(8,128)}, u32[]{:S(2)}) copy-start(f32[1024,16,128]{2,1,0:T(8,128)} %pad_maximum_fusion.1) | copy-start | bytes 25165828
  334.3 7.8 copy-start.6
  340.1 2.0 copy-start.8
  353.9 388.1 %reduce-scatter.5.cloned.1.call-start = ((), (), s32[]{:S(2)}) async-start(), calls=%async_computation.9 | async-start | bytes 18874368 | tf_op jit(solution)/shard_map/reduce_scatter | solution.py:153
  353.9 11.2 %copy-start.12 = (f32[2048]{0:T(1024)S(1)}, f32[2048]{0:T(1024)}, u32[]{:S(2)}) copy-start(f32[2048]{0:T(1024)} %copy-done.11) | copy-start | bytes 24580
  353.9 11.2 %copy-start.16 = (f32[1024]{0:T(1024)S(1)}, f32[1024]{0:T(1024)}, u32[]{:S(2)}) copy-start(f32[1024]{0:T(1024)} %copy-done.15) | copy-start | bytes 12292
  365.2 10.1 %copy-start.1 = (f32[1024,16,128]{2,1,0:T(8,128)S(1)}, f32[1024,16,128]{2,1,0:T(8,128)}, u32[]{:S(2)}) copy-start(f32[1024,16,128]{2,1,0:T(8,128)} %pad_maximum_fusion) | copy-start | bytes 25165828
  375.2 7.8 copy-start.7
  394.8 347.1 %reduce-scatter.9.cloned.1.call-start = ((), (), s32[]{:S(2)}) async-start(), calls=%async_computation.11 | async-start | bytes 18874368 | tf_op jit(solution)/shard_map/reduce_scatter | solution.py:153
  410.2 394.0 %reduce-scatter.11.cloned.1.call-start = ((), (), s32[]{:S(2)}) async-start(), calls=%async_computation.12 | async-start | bytes 18874368 | tf_op jit(solution)/shard_map/reduce_scatter | solution.py:153
  425.9 14.6 %copy-start.10 = (bf16[1024,2048]{1,0:T(8,128)(2,1)S(1)}, bf16[1024,2048]{1,0:T(8,128)(2,1)}, u32[]{:S(2)}) copy-start(bf16[1024,2048]{1,0:T(8,128)(2,1)} %copy-done.9) | copy-start | bytes 12582916
  440.6 13.2 %copy-start.14 = (f32[2048]{0:T(1024)S(1)}, f32[2048]{0:T(1024)}, u32[]{:S(2)}) copy-start(f32[2048]{0:T(1024)} %copy-done.13) | copy-start | bytes 24580
  440.6 13.2 %copy-start.18 = (f32[1024]{0:T(1024)S(1)}, f32[1024]{0:T(1024)}, u32[]{:S(2)}) copy-start(f32[1024]{0:T(1024)} %copy-done.17) | copy-start | bytes 12292
  538.3 77.6 %all-to-all-start.4 = ((bf16[8,2,131072]{2,1,0:T(2,128)(2,1)}), bf16[8,2,131072]{2,1,0:T(2,128)(2,1)}, u32[]{:S(2)}, u32[]{:S(2)}) async-start(bf16[8,2,131072]{2,1,0:T(2,128)(2,1)} %reshape.217), calls=%async_computation.4 | async-start | bytes 8388608 | tf_op jit(solution)/shard_map/all_to_all | solution.py:198
  608.1 12.7 %copy-start.24 = (u32[16]{0:T(128)S(1)}, u32[16]{0:T(128)}, u32[]{:S(2)}) copy-start(u32[16]{0:T(128)} %constant.18) | copy-start | bytes 196
  608.1 13.9 %copy-start.19 = (f32[2048]{0:T(1024)S(1)}, f32[2048]{0:T(1024)}, u32[]{:S(2)}) copy-start(f32[2048]{0:T(1024)} %get-tuple-element.19) | copy-start | bytes 24580
  608.1 13.9 %copy-start.20 = (f32[2048]{0:T(1024)S(1)}, f32[2048]{0:T(1024)}, u32[]{:S(2)}) copy-start(f32[2048]{0:T(1024)} %get-tuple-element.21) | copy-start | bytes 24580
  615.9 109.2 %all-to-all-start.2 = ((bf16[8,2,131072]{2,1,0:T(2,128)(2,1)}), bf16[8,2,131072]{2,1,0:T(2,128)(2,1)}, u32[]{:S(2)}, u32[]{:S(2)}) async-start(bf16[8,2,131072]{2,1,0:T(2,128)(2,1)} %reshape.215), calls=%async_computation.2 | async-start | bytes 8388608 | tf_op jit(solution)/shard_map/all_to_all | solution.py:179
  (1 other events, 2.0 us)
Sparse Core Ops, SparseCore 0:
  354.0 89.0 reduce-scatter.6
  446.0 87.3 reduce-scatter.4
  536.4 177.5 reduce-scatter.8
  716.8 87.3 reduce-scatter.10

commit v2 on v1

--- a/solution.py
+++ b/solution.py
@@ -18,34 +18,9 @@
 def rope_tables(positions):
     half_dim = HEAD_DIM // 2
     inv_freq = ROPE_BASE ** (-jnp.arange(half_dim, dtype=jnp.float32) * (2.0 / HEAD_DIM))
-    angles = positions.astype(jnp.float32)[..., None] * inv_freq
-    return jnp.cos(angles)[:, None, :], jnp.sin(angles)[:, None, :]
-
-
-def rope_apply(values, cos_t, sin_t):
-    half_dim = values.shape[-1] // 2
-    first_half = values[..., :half_dim]
-    second_half = values[..., half_dim:]
-    return jnp.concatenate([first_half * cos_t - second_half * sin_t, second_half * cos_t + first_half * sin_t], axis=-1)
-
-
-def rope_revert(grads_in, cos_t, sin_t):
-    half_dim = grads_in.shape[-1] // 2
-    first_half = grads_in[..., :half_dim]
-    second_half = grads_in[..., half_dim:]
-    return jnp.concatenate([first_half * cos_t + second_half * sin_t, second_half * cos_t - first_half * sin_t], axis=-1)
-
-
-def rms_forward(values, gain_vec):
-    inv_rms = lax.rsqrt(jnp.mean(values * values, axis=-1, keepdims=True) + NORM_EPS)
-    normed = values * inv_rms
-    return normed * gain_vec.astype(jnp.float32), normed, inv_rms
-
-
-def rms_backward(d_out, normed, inv_rms, gain_vec):
-    d_normed = d_out * gain_vec.astype(jnp.float32)
-    d_in = inv_rms * (d_normed - normed * jnp.mean(d_normed * normed, axis=-1, keepdims=True))
-    return d_in, d_out * normed
+    angles = positions.astype(jnp.float32)[:, None] * inv_freq
+    cos_h, sin_h = jnp.cos(angles), jnp.sin(angles)
+    return jnp.concatenate([cos_h, cos_h], axis=1), jnp.concatenate([-sin_h, sin_h], axis=1)
 
 
 def dot_nn(a, b):
@@ -145,58 +120,392 @@
     )(q, k, v, d_out, lse)
 
 
+MESH = pl.DeviceIdType.MESH
+ROW_BLOCK = 256
+
+
+def row_inv(values):
+    return lax.rsqrt(jnp.mean(values * values, axis=-1, keepdims=True) + NORM_EPS)
+
+
+def qkv_kernel(x_ref, cos_ref, sin_ref, gn_ref, gq_ref, gk_ref, wq_ref, wk_ref, wv_ref,
+               q_ref, k_ref, v_ref, ht_ref, q1_ref, k1_ref):
+    x_f = x_ref[...].astype(jnp.float32)
+    hidden_f = x_f * row_inv(x_f) * gn_ref[...].astype(jnp.float32)
+    hidden = hidden_f.astype(jnp.bfloat16)
+    ht_ref[...] = hidden.T
+    v_ref[...] = dot_nn(hidden, wv_ref[...]).astype(jnp.bfloat16)
+    cos_t, sin_t = cos_ref[...], sin_ref[...]
+    for w_ref, g_ref, raw_ref, out_ref in ((wq_ref, gq_ref, q1_ref, q_ref), (wk_ref, gk_ref, k1_ref, k_ref)):
+        raw_ref[...] = dot_nn(hidden, w_ref[...])
+        raw = raw_ref[...]
+        inv = row_inv(raw)
+        for at in range(0, raw.shape[1], HEAD_DIM):
+            u = raw_ref[:, at:at + HEAD_DIM] * inv * g_ref[:, at:at + HEAD_DIM].astype(jnp.float32)
+            out_ref[:, at:at + HEAD_DIM] = (u * cos_t + pltpu.roll(u, HEAD_DIM // 2, 1) * sin_t).astype(jnp.bfloat16)
+
+
+def project_qkv(x_bf, cos_t, sin_t, g_norm, g_query, g_key, w_query, w_key, w_value):
+    rows, d_model = x_bf.shape
+    blk = ROW_BLOCK
+    row_spec = pl.BlockSpec((blk, d_model), lambda i: (i, 0))
+    tab_spec = pl.BlockSpec((blk, HEAD_DIM), lambda i: (i, 0))
+    vec_spec = pl.BlockSpec((1, d_model), lambda i: (0, 0))
+    mat_spec = pl.BlockSpec((d_model, d_model), lambda i: (0, 0), pipeline_mode=pl.Buffered(1))
+    act = jax.ShapeDtypeStruct((rows, d_model), jnp.bfloat16)
+    raw = jax.ShapeDtypeStruct((rows, d_model), jnp.float32)
+    return pl.pallas_call(
+        qkv_kernel,
+        grid=(rows // blk,),
+        out_shape=(act, act, act, jax.ShapeDtypeStruct((d_model, rows), jnp.bfloat16), raw, raw),
+        in_specs=[row_spec, tab_spec, tab_spec, vec_spec, vec_spec, vec_spec, mat_spec, mat_spec, mat_spec],
+        out_specs=(row_spec, row_spec, row_spec, pl.BlockSpec((d_model, blk), lambda i: (0, i)), row_spec, row_spec),
+        compiler_params=pltpu.CompilerParams(vmem_limit_bytes=62 * 1024 * 1024),
+        cost_estimate=pl.CostEstimate(flops=6 * rows * d_model * d_model, bytes_accessed=60 * 1024 * 1024, transcendentals=0),
+        name="qkv_proj",
+    )(x_bf, cos_t, sin_t, g_norm[None], g_query[None], g_key[None], w_query, w_key, w_value)
+
+
+def norm_back_kernel(dq_ref, dk_ref, q1_ref, k1_ref, cos_ref, sin_ref, gq_ref, gk_ref,
+                     oq_ref, ok_ref, tq_ref, tk_ref, tmp_ref, nrm_ref):
+    cos_t, sin_t = cos_ref[...], sin_ref[...]
+    for d_ref, raw_ref, g_ref, out_ref, t_ref in ((dq_ref, q1_ref, gq_ref, oq_ref, tq_ref), (dk_ref, k1_ref, gk_ref, ok_ref, tk_ref)):
+        raw = raw_ref[...]
+        inv = row_inv(raw)
+        total = jnp.zeros((raw.shape[0], HEAD_DIM), jnp.float32)
+        for at in range(0, raw.shape[1], HEAD_DIM):
+            d_u = d_ref[:, at:at + HEAD_DIM].astype(jnp.float32)
+            d_n = d_u * cos_t - pltpu.roll(d_u, HEAD_DIM // 2, 1) * sin_t
+            hat = raw_ref[:, at:at + HEAD_DIM] * inv
+            terms = jnp.sum(d_n * hat, axis=0, keepdims=True)
+
+            @pl.when(pl.program_id(0) == 0)
+            def _():
+                t_ref[:, at:at + HEAD_DIM] = terms
+
+            @pl.when(pl.program_id(0) > 0)
+            def _():
+                t_ref[:, at:at + HEAD_DIM] += terms
+
+            d_n = d_n * g_ref[:, at:at + HEAD_DIM].astype(jnp.float32)
+            total = total + d_n * hat
+            tmp_ref[:, at:at + HEAD_DIM] = d_n
+            nrm_ref[:, at:at + HEAD_DIM] = hat
+        mean = jnp.sum(total, axis=-1, keepdims=True) * (1.0 / raw.shape[1])
+        out_ref[...] = (inv * (tmp_ref[...] - nrm_ref[...] * mean)).astype(jnp.bfloat16)
+
+
+def norm_back(d_q, d_k, q1, k1, cos_t, sin_t, g_query, g_key):
+    rows, d_model = d_q.shape
+    blk = ROW_BLOCK
+    row_spec = pl.BlockSpec((blk, d_model), lambda i: (i, 0))
+    tab_spec = pl.BlockSpec((blk, HEAD_DIM), lambda i: (i, 0))
+    vec_spec = pl.BlockSpec((1, d_model), lambda i: (0, 0))
+    act = jax.ShapeDtypeStruct((rows, d_model), jnp.bfloat16)
+    vec = jax.ShapeDtypeStruct((1, d_model), jnp.float32)
+    return pl.pallas_call(
+        norm_back_kernel,
+        grid=(rows // blk,),
+        out_shape=(act, act, vec, vec),
+        in_specs=[row_spec] * 4 + [tab_spec] * 2 + [vec_spec] * 2,
+        out_specs=(row_spec, row_spec, vec_spec, vec_spec),
+        scratch_shapes=[pltpu.VMEM((blk, d_model), jnp.float32)] * 2,
+        cost_estimate=pl.CostEstimate(flops=40 * rows * d_model, bytes_accessed=24 * rows * d_model, transcendentals=0),
+        name="norm_back",
+    )(d_q, d_k, q1, k1, cos_t, sin_t, g_query[None], g_key[None])
+
+
+N_SLOTS = 4
+
+
+def tail_kernel(n_dev, ht_ref, dy_v, dy_k, dy_q, w_v, w_k, w_q, x_ref, gy_ref, gn_ref, tq_ref, tk_ref,
+                gw_v, gw_k, gw_q, gx_ref, gain_ref,
+                ht_own, ht_par, dy_own, dy_par, rs, dh, wbuf, xbuf, gybuf, n_acc, gsend, grecv,
+                load_sem, part_send, part_recv, rs_send, rs_recv, w_sem, xy_sem, gx_send, gx_recv, gx_loc,
+                gain_send, gain_recv, fin_loc, fin_send, fin_recv):
+    me = lax.axis_index('sp')
+    chip, core = me // 2, me % 2
+    n_chips = n_dev // 2
+    step_dir = 1 - 2 * core
+    partner = me + step_dir
+    right = 2 * lax.rem(chip + step_dir + n_chips, n_chips) + core
+    rows, d_model = x_ref.shape
+    half = d_model // 2
+    piece = rows // n_dev
+    chunk = d_model // n_chips
+    own_rows = d_model // n_dev
+    dys, ws, gws = (dy_v, dy_k, dy_q), (w_v, w_k, w_q), (gw_v, gw_k, gw_q)
+    mine = pl.ds(pl.multiple_of(core * half, half), half)
+    other = pl.ds(pl.multiple_of((1 - core) * half, half), half)
+
+    loads = [pltpu.make_async_copy(ht_ref, ht_own, load_sem.at[0])]
+    loads += [pltpu.make_async_copy(dys[i], dy_own.at[i], load_sem.at[1 + i]) for i in range(3)]
+    for cp in loads:
+        cp.start()
+
+    barrier = pltpu.get_barrier_semaphore()
+    for off in range(1, n_dev):
+        pl.semaphore_signal(barrier, inc=1, device_id={'sp': lax.rem(me + off, n_dev)}, device_id_type=MESH)
+    pl.semaphore_wait(barrier, n_dev - 1)
+
+    def to_partner(src, dst, idx):
+        return pltpu.make_async_remote_copy(src_ref=src, dst_ref=dst, send_sem=part_send.at[idx], recv_sem=part_recv.at[idx],
+                                            device_id={'sp': partner}, device_id_type=MESH)
+
+    parts = [to_partner(ht_ref, ht_par, 0)]
+    parts += [to_partner(dys[i].at[:, other], dy_par.at[i], 1 + i) for i in range(3)]
+    for cp in parts:
+        cp.start()
+
+    def rs_copy(w, s):
+        return pltpu.make_async_remote_copy(src_ref=rs.at[w, s], dst_ref=rs.at[w, s + 1], send_sem=rs_send.at[w, s], recv_sem=rs_recv.at[w, s],
+                                            device_id={'sp': right}, device_id_type=MESH)
+
+    n_tile = 256
+
+    def ring_step(w, s):
+        owner = lax.rem(chip - step_dir * (1 + s) + 2 * n_chips, n_chips)
+        row_at = pl.multiple_of(owner * chunk, chunk)
+
+        def tile(t, carry):
+            col = pl.multiple_of(t * n_tile, n_tile)
+            term = dot_nn(ht_own[pl.ds(row_at, chunk), :], dy_own[w, :, pl.ds(pl.multiple_of(core * half + col, n_tile), n_tile)])
+            term = term + dot_nn(ht_par[pl.ds(row_at, chunk), :], dy_par[w, :, pl.ds(col, n_tile)])
+
+            @pl.when(s == 0)
+            def _():
+                rs[w, s, :, pl.ds(col, n_tile)] = term
+
+            @pl.when(s > 0)
+            def _():
+                rs[w, s, :, pl.ds(col, n_tile)] += term
+
+            return carry
+
+        lax.fori_loop(0, half // n_tile, tile, 0)
+
+    def w_copy(i, n, slot):
+        return pltpu.make_async_copy(ws[i].at[pl.ds(pl.multiple_of(n * n_tile, n_tile), n_tile), :], wbuf.at[slot, i], w_sem.at[slot, i])
+
+    def dh_block(n):
+        slot = lax.rem(n, 2)
+        for i in range(3):
+            w_copy(i, n, slot).wait()
+
+        @pl.when(n + 1 < d_model // n_tile)
+        def _():
+            for i in range(3):
+                w_copy(i, n + 1, 1 - slot).start()
+
+        m_tile = 256
+
+        def tile(t, carry):
+            at = pl.ds(pl.multiple_of(t * m_tile, m_tile), m_tile)
+            total = dot_nt(dy_own[0, at, :], wbuf[slot, 0]) + dot_nt(dy_own[1, at, :], wbuf[slot, 1]) + dot_nt(dy_own[2, at, :], wbuf[slot, 2])
+            dh[at, pl.ds(pl.multiple_of(n * n_tile, n_tile), n_tile)] = total.astype(jnp.bfloat16)
+            return carry
+
+        lax.fori_loop(0, rows // m_tile, tile, 0)
+
+    def xy_copies(p, slot):
+        at = pl.ds(pl.multiple_of(p * piece, piece), piece)
+        return (pltpu.make_async_copy(x_ref.at[at, :], xbuf.at[slot], xy_sem.at[slot, 0]),
+                pltpu.make_async_copy(gy_ref.at[at, :], gybuf.at[slot], xy_sem.at[slot, 1]))
+
+    def gx_remote(off):
+        dest = lax.rem(me + off, n_dev)
+        at = pl.ds(pl.multiple_of(dest * piece, piece), piece)
+        return pltpu.make_async_remote_copy(src_ref=dh.at[at, :], dst_ref=gx_ref.at[me], send_sem=gx_send.at[off], recv_sem=gx_recv.at[off],
+                                            device_id={'sp': dest}, device_id_type=MESH)
+
+    def gx_own():
+        at = pl.ds(pl.multiple_of(me * piece, piece), piece)
+        return pltpu.make_async_copy(dh.at[at, :], gx_ref.at[me], gx_loc)
+
+    def gain_copy(off):
+        dest = lax.rem(me + off, n_dev)
+        return pltpu.make_async_remote_copy(src_ref=gsend.at[dest], dst_ref=grecv.at[off], send_sem=gain_send.at[off], recv_sem=gain_recv.at[off],
+                                            device_id={'sp': dest}, device_id_type=MESH)
+
+    def grad_x_pieces():
+        n_acc[...] = jnp.zeros_like(n_acc)
+        for cp in xy_copies(0, 0):
+            cp.start()
+
+        def one(p, carry):
+            slot = lax.rem(p, 2)
+            for cp in xy_copies(p, slot):
+                cp.wait()
+
+            @pl.when(p + 1 < n_dev)
+            def _():
+                for cp in xy_copies(p + 1, 1 - slot):
+                    cp.start()
+
+            at = pl.ds(pl.multiple_of(p * piece, piece), piece)
+            sub = 32
+
+            def rows_of(j, c2):
+                ra = pl.ds(pl.multiple_of(j * sub, sub), sub)
+                rb = pl.ds(pl.multiple_of(p * piece + j * sub, sub), sub)
+                x_f = xbuf[slot, ra, :].astype(jnp.float32)
+                inv = row_inv(x_f)
+                hat = x_f * inv
+                d_h = dh[rb, :].astype(jnp.float32)
+                n_acc[...] += jnp.sum(d_h * hat, axis=0, keepdims=True)
+                d_n = d_h * gn_ref[...].astype(jnp.float32)
+                mean = jnp.mean(d_n * hat, axis=-1, keepdims=True)
+                out = gybuf[slot, ra, :].astype(jnp.float32) + inv * (d_n - hat * mean)
+                dh[rb, :] = out.astype(jnp.bfloat16)
+                return c2
+
+            lax.fori_loop(0, piece // sub, rows_of, 0)
+            return carry
+
+        lax.fori_loop(0, n_dev, one, 0)
+        for off in range(1, n_dev):
+            gx_remote(off).start()
+        gx_own().start()
+        for d in range(n_dev):
+            gsend[d] = jnp.zeros(gsend.shape[1:], jnp.float32)
+            cols = slice(d * own_rows, (d + 1) * own_rows)
+            gsend[d, 0:1, :] = n_acc[:, cols]
+            gsend[d, 1:2, :] = tq_ref[:, cols]
+            gsend[d, 2:3, :] = tk_ref[:, cols]
+        for off in range(1, n_dev):
+            gain_copy(off).start()
+
+    def finish_out(w):
+        keep = pl.ds(pl.multiple_of(core * own_rows, own_rows), own_rows)
+        give = pl.ds(pl.multiple_of((1 - core) * own_rows, own_rows), own_rows)
+        loc = pltpu.make_async_copy(rs.at[w, N_SLOTS - 1, keep, :], gws[w].at[:, mine], fin_loc.at[w])
+        rem = pltpu.make_async_remote_copy(src_ref=rs.at[w, N_SLOTS - 1, give, :], dst_ref=gws[w].at[:, mine], send_sem=fin_send.at[w], recv_sem=fin_recv.at[w],
+                                           device_id={'sp': partner}, device_id_type=MESH)
+        return loc, rem
+
+    for cp in loads:
+        cp.wait()
+    for i in range(3):
+        w_copy(i, 0, 0).start()
+    parts[0].wait_recv()
+    n_blocks = d_model // n_tile
+    dh_from = 2
+
+    def main(it, carry):
+        s, w = it // 3, lax.rem(it, 3)
+
+        @pl.when(s == 0)
+        def _():
+            pltpu.make_async_remote_copy(src_ref=dy_v.at[:, other], dst_ref=dy_par.at[w], send_sem=part_send.at[1 + w], recv_sem=part_recv.at[1 + w],
+                                         device_id={'sp': partner}, device_id_type=MESH).wait_recv()
+
+        @pl.when(s > 0)
+        def _():
+            rs_copy(w, s - 1).wait_recv()
+
+        ring_step(w, s)
+
+        @pl.when(s < N_SLOTS - 1)
+        def _():
+            rs_copy(w, s).start()
+
+        for j in range(2):
+            blk_i = 2 * (it - dh_from) + j
+
+            @pl.when(jnp.logical_and(blk_i >= 0, blk_i < n_blocks))
+            def _():
+                dh_block(blk_i)
+
+        @pl.when(it == dh_from + n_blocks // 2)
+        def _():
+            grad_x_pieces()
+
+        for i in range(3):
+            @pl.when(jnp.logical_and(s == N_SLOTS - 1, w == i))
+            def _():
+                for cp in finish_out(i):
+                    cp.start()
+
+        return carry
+
+    lax.fori_loop(0, 3 * N_SLOTS, main, 0)
+
+    for cp in parts:
+        cp.wait_send()
+
+    def drain(it, carry):
+        rs_copy(lax.rem(it, 3), it // 3).wait_send()
+        return carry
+
+    lax.fori_loop(0, 3 * (N_SLOTS - 1), drain, 0)
+    for off in range(1, n_dev):
+        gain_copy(off).wait()
+    total = gsend[me]
+    for off in range(1, n_dev):
+        total = total + grecv[off]
+    gain_ref[...] = total
+    for off in range(1, n_dev):
+        gx_remote(off).wait()
+    gx_own().wait()
+    for i in range(3):
+        loc, rem = finish_out(i)
+        loc.wait()
+        rem.wait()
+
+
+def tail(n_dev, ht, dys, ws, x_bf, gy, g_norm, t_q, t_k):
+    rows, d_model = x_bf.shape
+    half, chunk, own_rows, piece = d_model // 2, d_model // (n_dev // 2), d_model // n_dev, rows // n_dev
+    hbm = pl.BlockSpec(memory_space=pl.ANY)
+    vmem = pl.BlockSpec(memory_space=pltpu.VMEM)
+    f32, bf16 = jnp.float32, jnp.bfloat16
+    gw = jax.ShapeDtypeStruct((own_rows, d_model), f32)
+    dma = pltpu.SemaphoreType.DMA
+    return pl.pallas_call(
+        functools.partial(tail_kernel, n_dev),
+        out_shape=(gw, gw, gw, jax.ShapeDtypeStruct((n_dev, piece, d_model), bf16), jax.ShapeDtypeStruct((8, own_rows), f32)),
+        in_specs=[hbm] * 9 + [vmem] * 3,
+        out_specs=(hbm,) * 4 + (vmem,),
+        scratch_shapes=[
+            pltpu.VMEM((d_model, rows), bf16), pltpu.VMEM((d_model, rows), bf16),
+            pltpu.VMEM((3, rows, d_model), bf16), pltpu.VMEM((3, rows, half), bf16),
+            pltpu.VMEM((3, N_SLOTS, chunk, half), f32),
+            pltpu.VMEM((rows, d_model), bf16),
+            pltpu.VMEM((2, 3, 256, d_model), bf16),
+            pltpu.VMEM((2, piece, d_model), bf16), pltpu.VMEM((2, piece, d_model), bf16),
+            pltpu.VMEM((1, d_model), f32), pltpu.VMEM((n_dev, 8, own_rows), f32), pltpu.VMEM((n_dev, 8, own_rows), f32),
+            dma((4,)), dma((4,)), dma((4,)), dma((3, 3)), dma((3, 3)), dma((2, 3)), dma((2, 2)),
+            dma((n_dev,)), dma((n_dev,)), dma, dma((n_dev,)), dma((n_dev,)), dma((3,)), dma((3,)), dma((3,)),
+        ],
+        compiler_params=pltpu.CompilerParams(collective_id=0, has_side_effects=True, vmem_limit_bytes=67043328),
+        cost_estimate=pl.CostEstimate(flops=12 * rows * d_model * d_model, bytes_accessed=64 * 1024 * 1024, transcendentals=0),
+        name="tail",
+    )(ht, *dys, *ws, x_bf, gy, g_norm[None], t_q, t_k)
+
+
 def solution(mesh):
-    to_seqs = functools.partial(lax.all_to_all, axis_name='sp', split_axis=0, concat_axis=1, tiled=True)
-    to_tokens = functools.partial(lax.all_to_all, axis_name='sp', split_axis=1, concat_axis=0, tiled=True)
+    n_dev = mesh.shape['sp']
+    exchange = functools.partial(lax.all_to_all, axis_name='sp', split_axis=0, concat_axis=0, tiled=True)
 
     def sum_rows(partial_sum):
         return lax.psum_scatter(partial_sum, 'sp', scatter_dimension=0, tiled=True)
 
     def device_step(x_loc, gy_loc, pos_loc, g_norm, w_query, w_key, w_value, w_out, g_query, g_key):
-        d_model = x_loc.shape[-1]
-        x_seq = to_seqs(x_loc)
-        pos_seq = to_seqs(pos_loc)
-        gy_seq = to_seqs(gy_loc)
-        n_seq, seq_len = pos_seq.shape
-        rows = n_seq * seq_len
-        cos_t, sin_t = rope_tables(pos_seq.reshape(rows))
-        x_bf = x_seq.reshape(rows, d_model)
-        gy = gy_seq.reshape(rows, d_model)
-        heads = (rows, d_model // HEAD_DIM, HEAD_DIM)
-
-        hid_f, x_hat, x_inv = rms_forward(x_bf.astype(jnp.float32), g_norm)
-        hidden = hid_f.astype(jnp.bfloat16)
-        q_nrm, q_hat, q_inv = rms_forward(dot_nn(hidden, w_query), g_query)
-        k_nrm, k_hat, k_inv = rms_forward(dot_nn(hidden, w_key), g_key)
-        q_rot = rope_apply(q_nrm.reshape(heads), cos_t, sin_t).astype(jnp.bfloat16).reshape(rows, d_model)
-        k_rot = rope_apply(k_nrm.reshape(heads), cos_t, sin_t).astype(jnp.bfloat16).reshape(rows, d_model)
-        v_val = dot_nn(hidden, w_value).astype(jnp.bfloat16)
-
-        outs = [attend_forward(q_rot[i:i + seq_len], k_rot[i:i + seq_len], v_val[i:i + seq_len]) for i in range(0, rows, seq_len)]
-        attended = outs[0][0] if n_seq == 1 else jnp.concatenate([o[0] for o in outs])
+        n_batch, loc_len, d_model = x_loc.shape
+        rows = n_batch * loc_len
+        x_bf = exchange(x_loc).reshape(rows, d_model)
+        pos_seq = exchange(pos_loc).reshape(rows)
+        gy = exchange(gy_loc).reshape(rows, d_model)
+        cos_t, sin_t = rope_tables(pos_seq)
+        q_rot, k_rot, v_val, h_t, q1, k1 = project_qkv(x_bf, cos_t, sin_t, g_norm, g_query, g_key, w_query, w_key, w_value)
+        attended, lse = attend_forward(q_rot, k_rot, v_val)
         grad_wo = sum_rows(dot_tn(attended, gy))
         y_seq = (x_bf.astype(jnp.float32) + dot_nn(attended, w_out)).astype(jnp.bfloat16)
-        y_out = to_tokens(y_seq.reshape(n_seq, seq_len, d_model))
+        y_out = exchange(y_seq.reshape(n_batch, loc_len, d_model))
         d_attn = dot_nt(gy, w_out).astype(jnp.bfloat16)
-
-        bwd = [attend_backward(q_rot[i:i + seq_len], k_rot[i:i + seq_len], v_val[i:i + seq_len], d_attn[i:i + seq_len], outs[i // seq_len][1]) for i in range(0, rows, seq_len)]
-        d_q, d_k, d_v = bwd[0] if n_seq == 1 else [jnp.concatenate([b[j] for b in bwd]) for j in range(3)]
-
-        dq_rot = rope_revert(d_q.astype(jnp.float32).reshape(heads), cos_t, sin_t).reshape(rows, d_model)
-        dk_rot = rope_revert(d_k.astype(jnp.float32).reshape(heads), cos_t, sin_t).reshape(rows, d_model)
-        dq_raw, q_terms = rms_backward(dq_rot, q_hat, q_inv, g_query)
-        dk_raw, k_terms = rms_backward(dk_rot, k_hat, k_inv, g_key)
-        dq_bf = dq_raw.astype(jnp.bfloat16)
-        dk_bf = dk_raw.astype(jnp.bfloat16)
-        grad_wv = sum_rows(dot_tn(hidden, d_v))
-        grad_wk = sum_rows(dot_tn(hidden, dk_bf))
-        grad_wq = sum_rows(dot_tn(hidden, dq_bf))
-        d_hidden = dot_nt(dq_bf, w_query) + dot_nt(dk_bf, w_key) + dot_nt(d_v, w_value)
-        d_hidden = d_hidden.astype(jnp.bfloat16).astype(jnp.float32)
-        dx_norm, n_terms = rms_backward(d_hidden, x_hat, x_inv, g_norm)
-        gx_seq = (gy.astype(jnp.float32) + dx_norm).astype(jnp.bfloat16)
-        grad_x = to_tokens(gx_seq.reshape(n_seq, seq_len, d_model))
-        gains = [sum_rows(jnp.sum(t, axis=0)) for t in (n_terms, q_terms, k_terms)]
+        d_q, d_k, d_v = attend_backward(q_rot, k_rot, v_val, d_attn, lse)
+        dq_bf, dk_bf, t_q, t_k = norm_back(d_q, d_k, q1, k1, cos_t, sin_t, g_query, g_key)
+        grad_wv, grad_wk, grad_wq, grad_x, gains = tail(n_dev, h_t, (d_v, dk_bf, dq_bf), (w_value, w_key, w_query), x_bf, gy, g_norm, t_q, t_k)
         return y_out, grad_x, gains[0], grad_wq, grad_wk, grad_wv, grad_wo, gains[1], gains[2]
 
     seq_spec = P('dp', 'sp', None)

time: 816 us -> 580 us (0.71)
  Pallas kernels: 72.6 us -> 427 us
  other arithmetic: 189 us -> 3.22 us
  local copies, waits for them, and re-layouts: 142 us -> 16.2 us
  matrix products: 167 us -> 43.8 us
  waiting for transfers between devices: 109 us -> 0.06 us
  blocking collectives: 95 us -> 64 us
  starting transfers between devices: 21.5 us -> 10.6 us
    pallas_call x0 -> x3, Pallas kernels: none -> 355 us  [the longest x1 289 us: tail(): pl.pallas_call(functools.partial(tail_kernel, n_dev), out_shape=(gw, gw,...]
    unnamed x1 -> x0, blocking collectives: 84.4 us -> none
    unnamed x67 -> x19, local copies, waits for them, and re-layouts: 92.4 us -> 13 us
    unnamed x6 -> x0, other arithmetic: 69.1 us -> none
    reduce_scatter x4 -> x1, waiting for transfers between devices: 62.2 us -> 0.01 us  [sum_rows(): return lax.psum_scatter(partial_sum, 'sp', scatter_dimension=0, tiled=True)]
    all_to_all x1 -> x2, blocking collectives: 10.6 us -> 64 us  [the longest x1 53.6 us: device_step(): x_bf = exchange(x_loc).reshape(rows, d_model)]
    reshape x2 -> x0, local copies, waits for them, and re-layouts: 49.3 us -> none  [the longest x1 24.7 us: device_step(): grad_x = to_tokens(gx_seq.reshape(n_seq, seq_len, d_model))]
    all_to_all x4 -> x2, waiting for transfers between devices: 46.7 us -> 0.01 us  [the longest x1 0.01 us: device_step(): gy = exchange(gy_loc).reshape(rows, d_model)]
  transfers between devices with their start and end apart: 8 -> 3, of which waited for: 2 -> 0; matrix products, arithmetic and copies ran while one was open for 49% -> 6% of each run, Pallas kernels for 0% -> 74%
where the time goes in v2:
time: 580 us; the launch traced here: 579 us
  Pallas kernels  427 us (74%)
  blocking collectives  64 us (11%)
  matrix products  43.8 us (8%)
  local copies, waits for them, and re-layouts  16.2 us (3%)
  between operations  14.1 us (2%)
  starting transfers between devices  10.6 us (2%)
    pallas_call x1, Pallas kernels, tail(): pl.pallas_call(functools.partial(tail_kernel, n_dev), out_shape=(gw, gw,...  289 us
    all_to_all x1, blocking collectives, device_step(): x_bf = exchange(x_loc).reshape(rows, d_model)  53.6 us
    pallas_call x1, Pallas kernels, attend_backward(): pl.pallas_call(functools.partial(attn_bwd_kernel, seq_len), grid=(n_heads...  41.3 us
    pallas_call x1, Pallas kernels, project_qkv(): pl.pallas_call(qkv_kernel, grid=(rows // blk,), out_shape=(act, act, act,...  40.9 us
    pallas_call x1, Pallas kernels, attend_forward(): pl.pallas_call(functools.partial(attn_fwd_kernel, seq_len), grid=(n_heads...  30.9 us
    pallas_call x1, Pallas kernels, norm_back(): pl.pallas_call(norm_back_kernel, grid=(rows // blk,), out_shape=(act, act...  24.7 us
    dot_general x1, matrix products, dot_tn(): lax.dot_general(a, b, (((0,), (0,)), ((), ())), preferred_element_type=jn...  15.2 us
    dot_general x1, matrix products, dot_nn(): lax.dot_general(a, b, (((1,), (0,)), ((), ())), preferred_element_type=jn...  14.7 us
  transfers between devices with their start and end apart: 3, of which 0 were waited for; matrix products, arithmetic and copies ran while one was open for 6% of the time, Pallas kernels for 74%

profile of v2, /device:TPU:113, one launch (start us, length us, event | category | flops | bytes accessed | tf_op | source)
XLA Modules:
  0.0 578.8 jit_solution(1922802491367895378)
XLA Ops:
  7.2 10.4 %all_to_all.24 = s32[8,1,128]{2,1,0:T(1,128)S(1)} all-to-all(s32[8,1,128]{2,1,0:T(1,128)} %bitcast.19), channel_id=1, replica_groups=mesh['dp'=2,'sp'=8] {'sp'}, dimensions={0} | all-to-all | bytes 8192 | tf_op jit(solution)/shard_map/all_to_all | solution.py:497
  17.6 53.6 %all_to_all.25 = bf16[8,128,2048]{2,1,0:T(8,128)(2,1)} all-to-all(bf16[8,128,2048]{2,1,0:T(8,128)(2,1)} %param.10), channel_id=1, replica_groups=mesh['dp'=2,'sp'=8] {'sp'}, dimensions={0} | all-to-all | bytes 8388608 | tf_op jit(solution)/shard_map/all_to_all | solution.py:496
  71.2 5.7 all-to-all-start.3
  76.9 0.0 reduce-scatter.2.cloned.1.call-start
  76.9 0.0 copy-done.4
  76.9 0.6 broadcast_in_dim.6.gn_ref
  77.5 0.0 copy-done.5
  77.5 0.6 broadcast_in_dim.7.gq_ref
  78.1 0.0 copy-done.6
  78.1 0.6 broadcast_in_dim.16.gk_ref
  78.7 1.9 fusion
  80.7 1.3 pad_maximum_fusion
  82.0 40.9 %qkv_proj.1 = (bf16[1024,2048]{1,0:T(8,128)(2,1)}, bf16[1024,2048]{1,0:T(8,128)(2,1)}, bf16[1024,2048]{1,0:T(8,128)(2,1)}, bf16[2048,1024]{1,0:T(8,128)(2,1)}, f...) custom-call(bf16[1024,2048]{1,0:T(8,128)(2,1)} %bitcast.14, f32[1024,128]{1,0:T(8,128)} %get-tuple-element.55.cos_ref, ...), custom_call_target="tpu_custom_call" | custom-call | flops 25769803776 | bytes 62914560 | tf_op jit(solution)/shard_map/qkv_proj/pallas_call | solution.py:157
  122.9 30.9 %attn_fwd.1 = (bf16[1024,2048]{1,0:T(8,128)(2,1)}, f32[16,1,1024]{2,1,0:T(1,128)}) custom-call(bf16[1024,2048]{1,0:T(8,128)(2,1)} %get-tuple-element.29.q_ref, bf16[1024,2048]{1,0:T(8,128)(2,1)} %get-tuple-element.30.k_ref, bf16[1024,2048]{1,0:T(8,128)(2,1)} %get-tuple-element.31.v_ref), custom_call_target="tpu_custom_call" | custom-call | flops 8589934592 | bytes 16777216 | tf_op jit(solution)/shard_map/attn_fwd/pallas_call | solution.py:95
  153.8 0.0 all-to-all-done.3
  153.8 15.2 %fusion.2 = f32[2048,2048]{1,0:T(8,128)} fusion(bf16[1024,2048]{1,0:T(8,128)(2,1)} %get-tuple-element.32, bf16[1024,2048]{1,0:T(8,128)(2,1)} %bitcast.4.gy_ref), kind=kOutput, calls=%fused_computation.9 | convolution fusion | flops 8589934592 | bytes 25165824 | tf_op jit(solution)/shard_map/dot_general | solution.py:35
  169.1 0.1 reduce-scatter.2.cloned.1.call-update
  169.1 14.7 %add_convert_fusion = bf16[1024,2048]{1,0:T(8,128)(2,1)} fusion(bf16[1024,2048]{1,0:T(8,128)(2,1)} %bitcast.15, bf16[1024,2048]{1,0:T(8,128)(2,1)} %get-tuple-element.32, bf16[2048,2048]{1,0:T(8,128)(2,1)} %param.17), kind=kOutput, calls=%fused_computation | convolution fusion | flops 8596226048 | bytes 20971520 | tf_op jit(solution)/shard_map/dot_general | solution.py:27
  183.8 4.9 all-to-all-start.2
  188.7 13.9 %convolution_convert_fusion.do_ref = bf16[1024,2048]{1,0:T(8,128)(2,1)} fusion(bf16[1024,2048]{1,0:T(8,128)(2,1)} %bitcast.4.gy_ref, bf16[2048,2048]{1,0:T(8,128)(2,1)} %param.17), kind=kOutput, calls=%fused_computation.1 | convolution fusion | flops 8592031744 | bytes 16777216 | tf_op jit(solution)/shard_map/dot_general | solution.py:31
  202.6 41.3 %attn_bwd.1 = (bf16[1024,2048]{1,0:T(8,128)(2,1)}, bf16[1024,2048]{1,0:T(8,128)(2,1)}, bf16[1024,2048]{1,0:T(8,128)(2,1)}) custom-call(bf16[1024,2048]{1,0:T(8,128)(2,1)} %get-tuple-element.29.q_ref, bf16[1024,2048]{1,0:T(8,128)(2,1)} %get-tuple-element.30.k_ref, bf16[1024,2048]{1,0:T(8,128)(2,1)} %get-tuple-element.31.v_ref, ...), custom_call_target="tpu_custom_call" | custom-call | flops 21474836480 | bytes 29360128 | tf_op jit(solution)/shard_map/attn_bwd/pallas_call | solution.py:111
  243.9 24.7 %norm_back.1 = (bf16[1024,2048]{1,0:T(8,128)(2,1)}, bf16[1024,2048]{1,0:T(8,128)(2,1)}, f32[1,2048]{1,0:T(1,128)}, f32[1,2048]{1,0:T(1,128)}) custom-call(bf16[1024,2048]{1,0:T(8,128)(2,1)} %get-tuple-element.36.dq_ref, bf16[1024,2048]{1,0:T(8,128)(2,1)} %get-tuple-element.37.dk_ref, f32[1024,2048]{1,0:T(8,128)} %get-tuple-element.38.q1_ref, ...), custom_call_target="tpu_custom_call" | custom-call | flops 83886080 | bytes 50331648 | tf_op jit(solution)/shard_map/norm_back/pallas_call | solution.py:206
  268.5 289.0 %tail.1 = (f32[256,2048]{1,0:T(8,128)}, f32[256,2048]{1,0:T(8,128)}, f32[256,2048]{1,0:T(8,128)}, bf16[8,128,2048]{2,1,0:T(8,128)(2,1)}, f32[8,256]{1,0:T(8,128)}) custom-call(bf16[2048,1024]{1,0:T(8,128)(2,1)} %get-tuple-element.33.ht_ref, bf16[1024,2048]{1,0:T(8,128)(2,1)} %get-tuple-element.35.dy_v, bf16[1024,2048]{1,0:T(8,128)(2,1)} %get-tuple-element.40.dy_k, ...), custom_call_target="tpu_custom_call" | custom-call | flops 51539607552 | bytes 67108864 | tf_op jit(solution)/shard_map/tail/pallas_call | solution.py:464
  557.5 1.4 fusion.1
  558.9 0.0 all-to-all-done.2
  558.9 4.9 copy.24
  563.8 2.1 copy.25
  566.0 1.0 copy-done.3
  566.9 1.3 copy.26
  568.3 1.0 copy-done.2
  569.3 1.3 copy.27
  570.6 1.3 copy.28
  (12 shorter events, 0.0 us)
Async XLA Ops:
  71.2 5.7 copy-start.4
  71.2 6.3 %copy-start.5 = (bf16[2048]{0:T(1024)(128)(2,1)S(1)}, bf16[2048]{0:T(1024)(128)(2,1)}, u32[]{:S(2)}) copy-start(bf16[2048]{0:T(1024)(128)(2,1)} %param.18) | copy-start | bytes 12292
  71.2 6.9 %copy-start.6 = (bf16[2048]{0:T(1024)(128)(2,1)S(1)}, bf16[2048]{0:T(1024)(128)(2,1)}, u32[]{:S(2)}) copy-start(bf16[2048]{0:T(1024)(128)(2,1)} %param.19) | copy-start | bytes 12292
  71.2 82.6 %all-to-all-start.3 = ((bf16[8,128,2048]{2,1,0:T(8,128)(2,1)}), bf16[8,128,2048]{2,1,0:T(8,128)(2,1)}, u32[]{:S(2)}, u32[]{:S(2)}) async-start(bf16[8,128,2048]{2,1,0:T(8,128)(2,1)} %param.11), calls=%async_computation.3 | async-start | bytes 8388608 | tf_op jit(solution)/shard_map/all_to_all | solution.py:498
  76.9 482.0 %reduce-scatter.2.cloned.1.call-start = ((), (), s32[]{:S(2)}) async-start(), calls=%async_computation.5 | async-start | bytes 18874368 | tf_op jit(solution)/shard_map/reduce_scatter | solution.py:491
  183.8 375.1 %all-to-all-start.2 = ((bf16[8,128,2048]{2,1,0:T(8,128)(2,1)}), bf16[8,128,2048]{2,1,0:T(8,128)(2,1)}, u32[]{:S(2)}, u32[]{:S(2)}) async-start(bf16[8,128,2048]{2,1,0:T(8,128)(2,1)} %bitcast.17), calls=%async_computation.2 | async-start | bytes 8388608 | tf_op jit(solution)/shard_map/all_to_all | solution.py:504
  558.9 4.9 copy-start
  563.8 3.1 copy-start.3
  566.9 2.3 copy-start.2
  566.9 3.7 copy-start.1
Sparse Core Ops, SparseCore 0:
  169.2 147.4 reduce-scatter.1

commit v3 on v2

--- a/solution.py
+++ b/solution.py
@@ -15,12 +15,18 @@
 Q_BLOCK = 256
 
 
-def rope_tables(positions):
+def rope_table(n_pos):
     half_dim = HEAD_DIM // 2
     inv_freq = ROPE_BASE ** (-jnp.arange(half_dim, dtype=jnp.float32) * (2.0 / HEAD_DIM))
-    angles = positions.astype(jnp.float32)[:, None] * inv_freq
+    angles = jnp.arange(n_pos, dtype=jnp.float32)[:, None] * inv_freq
     cos_h, sin_h = jnp.cos(angles), jnp.sin(angles)
-    return jnp.concatenate([cos_h, cos_h], axis=1), jnp.concatenate([-sin_h, sin_h], axis=1)
+    table = jnp.concatenate([cos_h, cos_h, -sin_h, sin_h], axis=1)
+    parts = []
+    for _ in range(3):
+        part = lax.reduce_precision(table, 8, 7)
+        parts.append(part.astype(jnp.bfloat16))
+        table = table - part
+    return jnp.stack(parts)
 
 
 def dot_nn(a, b):
@@ -128,47 +134,149 @@
     return lax.rsqrt(jnp.mean(values * values, axis=-1, keepdims=True) + NORM_EPS)
 
 
-def qkv_kernel(x_ref, cos_ref, sin_ref, gn_ref, gq_ref, gk_ref, wq_ref, wk_ref, wv_ref,
-               q_ref, k_ref, v_ref, ht_ref, q1_ref, k1_ref):
-    x_f = x_ref[...].astype(jnp.float32)
-    hidden_f = x_f * row_inv(x_f) * gn_ref[...].astype(jnp.float32)
-    hidden = hidden_f.astype(jnp.bfloat16)
-    ht_ref[...] = hidden.T
-    v_ref[...] = dot_nn(hidden, wv_ref[...]).astype(jnp.bfloat16)
-    cos_t, sin_t = cos_ref[...], sin_ref[...]
-    for w_ref, g_ref, raw_ref, out_ref in ((wq_ref, gq_ref, q1_ref, q_ref), (wk_ref, gk_ref, k1_ref, k_ref)):
-        raw_ref[...] = dot_nn(hidden, w_ref[...])
-        raw = raw_ref[...]
-        inv = row_inv(raw)
-        for at in range(0, raw.shape[1], HEAD_DIM):
-            u = raw_ref[:, at:at + HEAD_DIM] * inv * g_ref[:, at:at + HEAD_DIM].astype(jnp.float32)
-            out_ref[:, at:at + HEAD_DIM] = (u * cos_t + pltpu.roll(u, HEAD_DIM // 2, 1) * sin_t).astype(jnp.bfloat16)
-
-
-def project_qkv(x_bf, cos_t, sin_t, g_norm, g_query, g_key, w_query, w_key, w_value):
-    rows, d_model = x_bf.shape
-    blk = ROW_BLOCK
-    row_spec = pl.BlockSpec((blk, d_model), lambda i: (i, 0))
-    tab_spec = pl.BlockSpec((blk, HEAD_DIM), lambda i: (i, 0))
-    vec_spec = pl.BlockSpec((1, d_model), lambda i: (0, 0))
-    mat_spec = pl.BlockSpec((d_model, d_model), lambda i: (0, 0), pipeline_mode=pl.Buffered(1))
-    act = jax.ShapeDtypeStruct((rows, d_model), jnp.bfloat16)
-    raw = jax.ShapeDtypeStruct((rows, d_model), jnp.float32)
+def front_kernel(n_dev, x_loc, pos_loc, tab_ref, gn_ref, gq_ref, gk_ref, wq_ref, wk_ref, wv_ref,
+                 x_seq, cs_ref, q_ref, k_ref, v_ref, ht_ref, q1_ref, k1_ref,
+                 xv, posv, wbuf, csb, qb, kb, vb, htb, q1b, k1b,
+                 w_sem, x_send, x_recv, p_send, p_recv, own_sem, xs_sem, out_sem):
+    me = lax.axis_index('sp')
+    chip, core = me // 2, me % 2
+    n_chips = n_dev // 2
+    piece = x_loc.shape[1]
+    blk = 2 * piece
+    n_pos = tab_ref.shape[1]
+    d_model = x_loc.shape[2]
+
+    for cp in [pltpu.make_async_copy(w, wbuf.at[i], w_sem.at[i]) for i, w in enumerate((wv_ref, wq_ref, wk_ref))]:
+        cp.start()
+    mine = pl.ds(pl.multiple_of(me * piece, piece), piece)
+    own = [pltpu.make_async_copy(x_loc.at[me], xv.at[mine, :], own_sem.at[0]), pltpu.make_async_copy(pos_loc.at[me], posv.at[me], own_sem.at[1])]
+    for cp in own:
+        cp.start()
+
+    barrier = pltpu.get_barrier_semaphore()
+    for off in range(1, n_dev):
+        pl.semaphore_signal(barrier, inc=1, device_id={'sp': lax.rem(me + off, n_dev)}, device_id_type=MESH)
+    pl.semaphore_wait(barrier, n_dev - 1)
+
+    sends = []
+    dests = [2 * chip + 1 - core]
+    for hop in (1, n_chips - 1, 2):
+        dests += [2 * lax.rem(chip + hop, n_chips) + lax.rem(core + flip, 2) for flip in range(2)]
+    for i, dest in enumerate(dests):
+        sends.append(pltpu.make_async_remote_copy(src_ref=pos_loc.at[dest], dst_ref=posv.at[me], send_sem=p_send.at[i], recv_sem=p_recv.at[me],
+                                                  device_id={'sp': dest}, device_id_type=MESH))
+        sends.append(pltpu.make_async_remote_copy(src_ref=x_loc.at[dest], dst_ref=xv.at[mine, :], send_sem=x_send.at[i], recv_sem=x_recv.at[me],
+                                                  device_id={'sp': dest}, device_id_type=MESH))
+    for cp in sends:
+        cp.start()
+
+    def arrival(src):
+        at = pl.ds(pl.multiple_of(src * piece, piece), piece)
+        return (pltpu.make_async_remote_copy(src_ref=x_loc.at[src], dst_ref=xv.at[at, :], send_sem=x_send.at[0], recv_sem=x_recv.at[src],
+                                             device_id={'sp': src}, device_id_type=MESH),
+                pltpu.make_async_remote_copy(src_ref=pos_loc.at[src], dst_ref=posv.at[src], send_sem=p_send.at[0], recv_sem=p_recv.at[src],
+                                             device_id={'sp': src}, device_id_type=MESH))
+
+    def outs(at, slot):
+        rows = pl.ds(pl.multiple_of(at, blk), blk)
+        pairs = [(csb.at[slot], cs_ref.at[rows, :]), (qb.at[slot], q_ref.at[rows, :]), (kb.at[slot], k_ref.at[rows, :]), (vb.at[slot], v_ref.at[rows, :]),
+                 (htb.at[slot], ht_ref.at[:, rows]), (q1b.at[slot], q1_ref.at[rows, :]), (k1b.at[slot], k1_ref.at[rows, :])]
+        return [pltpu.make_async_copy(s, d, out_sem.at[slot, i]) for i, (s, d) in enumerate(pairs)]
+
+    def x_out(src_chip):
+        rows = pl.ds(pl.multiple_of(src_chip * blk, blk), blk)
+        return pltpu.make_async_copy(xv.at[rows, :], x_seq.at[rows, :], xs_sem.at[src_chip])
+
+    def block(b, carry):
+        hop = b + (b // 2) * (5 - 2 * b)
+        src_chip = lax.rem(chip + hop, n_chips)
+        at = pl.multiple_of(src_chip * blk, blk)
+        slot = lax.rem(b, 2)
+
+        @pl.when(b == 0)
+        def _():
+            for cp in own:
+                cp.wait()
+            for cp in arrival(2 * chip + 1 - core):
+                cp.wait_recv()
+
+        @pl.when(b > 0)
+        def _():
+            for e in range(2):
+                for cp in arrival(2 * src_chip + e):
+                    cp.wait_recv()
+
+        x_out(src_chip).start()
+
+        @pl.when(b >= 2)
+        def _():
+            for cp in outs(at, slot):
+                cp.wait()
+
+        for e in range(2):
+            hot = (lax.broadcasted_iota(jnp.int32, (n_pos, piece), 0) == posv[2 * src_chip + e]).astype(jnp.bfloat16)
+            csb[slot, e * piece:(e + 1) * piece, :] = (dot_tn(hot, tab_ref[0]) + dot_tn(hot, tab_ref[1])) + dot_tn(hot, tab_ref[2])
+        x_f = xv[pl.ds(at, blk), :].astype(jnp.float32)
+        hidden = (x_f * row_inv(x_f) * gn_ref[...].astype(jnp.float32)).astype(jnp.bfloat16)
+        htb[slot] = hidden.T
+
+        @pl.when(b == 0)
+        def _():
+            for i, w in enumerate((wv_ref, wq_ref, wk_ref)):
+                pltpu.make_async_copy(w, wbuf.at[i], w_sem.at[i]).wait()
+
+        vb[slot] = dot_nn(hidden, wbuf[0]).astype(jnp.bfloat16)
+        cos_t, sin_t = csb[slot, :, 0:HEAD_DIM], csb[slot, :, HEAD_DIM:2 * HEAD_DIM]
+        for i, g_ref, raw_ref, out_ref in ((1, gq_ref, q1b, qb), (2, gk_ref, k1b, kb)):
+            raw_ref[slot] = dot_nn(hidden, wbuf[i])
+            inv = row_inv(raw_ref[slot])
+            for c in range(0, d_model, HEAD_DIM):
+                u = raw_ref[slot, :, c:c + HEAD_DIM] * inv * g_ref[:, c:c + HEAD_DIM].astype(jnp.float32)
+                out_ref[slot, :, c:c + HEAD_DIM] = (u * cos_t + pltpu.roll(u, HEAD_DIM // 2, 1) * sin_t).astype(jnp.bfloat16)
+        for cp in outs(at, slot):
+            cp.start()
+        return carry
+
+    lax.fori_loop(0, n_chips, block, 0)
+    for slot in range(2):
+        for cp in outs(0, slot):
+            cp.wait()
+    for i in range(n_chips):
+        x_out(i).wait()
+    for cp in sends:
+        cp.wait_send()
+
+
+def front(n_dev, x_loc, pos_loc, g_norm, g_query, g_key, w_query, w_key, w_value):
+    n_batch, piece, d_model = x_loc.shape
+    rows, blk = n_batch * piece, 2 * piece
+    hbm = pl.BlockSpec(memory_space=pl.ANY)
+    vmem = pl.BlockSpec(memory_space=pltpu.VMEM)
+    bf16, f32 = jnp.bfloat16, jnp.float32
+    act = jax.ShapeDtypeStruct((rows, d_model), bf16)
+    raw = jax.ShapeDtypeStruct((rows, d_model), f32)
+    dma = pltpu.SemaphoreType.DMA
+    stage = pltpu.VMEM((2, blk, d_model), bf16)
     return pl.pallas_call(
-        qkv_kernel,
-        grid=(rows // blk,),
-        out_shape=(act, act, act, jax.ShapeDtypeStruct((d_model, rows), jnp.bfloat16), raw, raw),
-        in_specs=[row_spec, tab_spec, tab_spec, vec_spec, vec_spec, vec_spec, mat_spec, mat_spec, mat_spec],
-        out_specs=(row_spec, row_spec, row_spec, pl.BlockSpec((d_model, blk), lambda i: (0, i)), row_spec, row_spec),
-        compiler_params=pltpu.CompilerParams(vmem_limit_bytes=62 * 1024 * 1024),
+        functools.partial(front_kernel, n_dev),
+        out_shape=(act, jax.ShapeDtypeStruct((rows, 2 * HEAD_DIM), f32), act, act, act, jax.ShapeDtypeStruct((d_model, rows), bf16), raw, raw),
+        in_specs=[hbm, hbm] + [vmem] * 4 + [hbm] * 3,
+        out_specs=(hbm,) * 8,
+        scratch_shapes=[
+            pltpu.VMEM((rows, d_model), bf16), pltpu.VMEM((n_dev, 1, piece), jnp.int32), pltpu.VMEM((3, d_model, d_model), bf16),
+            pltpu.VMEM((2, blk, 2 * HEAD_DIM), f32), stage, stage, stage, pltpu.VMEM((2, d_model, blk), bf16),
+            pltpu.VMEM((2, blk, d_model), f32), pltpu.VMEM((2, blk, d_model), f32),
+            dma((3,)), dma((n_dev,)), dma((n_dev,)), dma((n_dev,)), dma((n_dev,)), dma((2,)), dma((n_dev // 2,)), dma((2, 7)),
+        ],
+        compiler_params=pltpu.CompilerParams(collective_id=1, has_side_effects=True, vmem_limit_bytes=62 * 1024 * 1024),
         cost_estimate=pl.CostEstimate(flops=6 * rows * d_model * d_model, bytes_accessed=60 * 1024 * 1024, transcendentals=0),
-        name="qkv_proj",
-    )(x_bf, cos_t, sin_t, g_norm[None], g_query[None], g_key[None], w_query, w_key, w_value)
-
-
-def norm_back_kernel(dq_ref, dk_ref, q1_ref, k1_ref, cos_ref, sin_ref, gq_ref, gk_ref,
+        name="front",
+    )(x_loc, pos_loc[:, None, :], rope_table(rows), g_norm[None], g_query[None], g_key[None], w_query, w_key, w_value)
+
+
+def norm_back_kernel(dq_ref, dk_ref, q1_ref, k1_ref, cs_ref, gq_ref, gk_ref,
                      oq_ref, ok_ref, tq_ref, tk_ref, tmp_ref, nrm_ref):
-    cos_t, sin_t = cos_ref[...], sin_ref[...]
+    cos_t, sin_t = cs_ref[:, 0:HEAD_DIM], cs_ref[:, HEAD_DIM:2 * HEAD_DIM]
     for d_ref, raw_ref, g_ref, out_ref, t_ref in ((dq_ref, q1_ref, gq_ref, oq_ref, tq_ref), (dk_ref, k1_ref, gk_ref, ok_ref, tk_ref)):
         raw = raw_ref[...]
         inv = row_inv(raw)
@@ -195,11 +303,11 @@
         out_ref[...] = (inv * (tmp_ref[...] - nrm_ref[...] * mean)).astype(jnp.bfloat16)
 
 
-def norm_back(d_q, d_k, q1, k1, cos_t, sin_t, g_query, g_key):
+def norm_back(d_q, d_k, q1, k1, cos_sin, g_query, g_key):
     rows, d_model = d_q.shape
     blk = ROW_BLOCK
     row_spec = pl.BlockSpec((blk, d_model), lambda i: (i, 0))
-    tab_spec = pl.BlockSpec((blk, HEAD_DIM), lambda i: (i, 0))
+    tab_spec = pl.BlockSpec((blk, 2 * HEAD_DIM), lambda i: (i, 0))
     vec_spec = pl.BlockSpec((1, d_model), lambda i: (0, 0))
     act = jax.ShapeDtypeStruct((rows, d_model), jnp.bfloat16)
     vec = jax.ShapeDtypeStruct((1, d_model), jnp.float32)
@@ -207,12 +315,12 @@
         norm_back_kernel,
         grid=(rows // blk,),
         out_shape=(act, act, vec, vec),
-        in_specs=[row_spec] * 4 + [tab_spec] * 2 + [vec_spec] * 2,
+        in_specs=[row_spec] * 4 + [tab_spec] + [vec_spec] * 2,
         out_specs=(row_spec, row_spec, vec_spec, vec_spec),
         scratch_shapes=[pltpu.VMEM((blk, d_model), jnp.float32)] * 2,
         cost_estimate=pl.CostEstimate(flops=40 * rows * d_model, bytes_accessed=24 * rows * d_model, transcendentals=0),
         name="norm_back",
-    )(d_q, d_k, q1, k1, cos_t, sin_t, g_query[None], g_key[None])
+    )(d_q, d_k, q1, k1, cos_sin, g_query[None], g_key[None])
 
 
 N_SLOTS = 4
@@ -493,18 +601,16 @@
     def device_step(x_loc, gy_loc, pos_loc, g_norm, w_query, w_key, w_value, w_out, g_query, g_key):
         n_batch, loc_len, d_model = x_loc.shape
         rows = n_batch * loc_len
-        x_bf = exchange(x_loc).reshape(rows, d_model)
-        pos_seq = exchange(pos_loc).reshape(rows)
-        gy = exchange(gy_loc).reshape(rows, d_model)
-        cos_t, sin_t = rope_tables(pos_seq)
-        q_rot, k_rot, v_val, h_t, q1, k1 = project_qkv(x_bf, cos_t, sin_t, g_norm, g_query, g_key, w_query, w_key, w_value)
+        x_bf, cos_sin, q_rot, k_rot, v_val, h_t, q1, k1 = front(n_dev, x_loc, pos_loc, g_norm, g_query, g_key, w_query, w_key, w_value)
+        gy_late, q_rot = lax.optimization_barrier((gy_loc, q_rot))
+        gy = exchange(gy_late).reshape(rows, d_model)
         attended, lse = attend_forward(q_rot, k_rot, v_val)
         grad_wo = sum_rows(dot_tn(attended, gy))
         y_seq = (x_bf.astype(jnp.float32) + dot_nn(attended, w_out)).astype(jnp.bfloat16)
         y_out = exchange(y_seq.reshape(n_batch, loc_len, d_model))
         d_attn = dot_nt(gy, w_out).astype(jnp.bfloat16)
         d_q, d_k, d_v = attend_backward(q_rot, k_rot, v_val, d_attn, lse)
-        dq_bf, dk_bf, t_q, t_k = norm_back(d_q, d_k, q1, k1, cos_t, sin_t, g_query, g_key)
+        dq_bf, dk_bf, t_q, t_k = norm_back(d_q, d_k, q1, k1, cos_sin, g_query, g_key)
         grad_wv, grad_wk, grad_wq, grad_x, gains = tail(n_dev, h_t, (d_v, dk_bf, dq_bf), (w_value, w_key, w_query), x_bf, gy, g_norm, t_q, t_k)
         return y_out, grad_x, gains[0], grad_wq, grad_wk, grad_wv, grad_wo, gains[1], gains[2]
 

time: 580 us -> 557 us (0.960)
  blocking collectives: 64 us -> 0 us
  Pallas kernels: 427 us -> 449 us
  waiting for transfers between devices: 0.06 us -> 17.2 us
    all_to_all x2 -> x0, blocking collectives: 64 us -> none  [the longest x1 53.6 us: device_step(): x_bf = exchange(x_loc).reshape(rows, d_model)]
    pallas_call x1, Pallas kernels: 40.9 us -> 65 us  [front(): pl.pallas_call(functools.partial(front_kernel, n_dev), out_shape=(act, ja...]
    all_to_all x1, waiting for transfers between devices: 0.01 us -> 17.1 us  [device_step(): gy = exchange(gy_late).reshape(rows, d_model)]
    unnamed x19 -> x13, local copies, waits for them, and re-layouts: 13 us -> 13 us
  transfers between devices with their start and end apart: 3 -> 3, of which waited for: 0 -> 1; matrix products, arithmetic and copies ran while one was open for 6% -> 5% of each run, Pallas kernels for 74% -> 69%
where the time goes in v3:
time: 557 us
  Pallas kernels  449 us (81%)
  matrix products  43.6 us (8%)
  local copies, waits for them, and re-layouts  18.3 us (3%)
  waiting for transfers between devices  17.2 us (3%)
  between operations  14.1 us (3%)
  starting transfers between devices  10.4 us (2%)
    pallas_call x1, Pallas kernels, tail(): pl.pallas_call(functools.partial(tail_kernel, n_dev), out_shape=(gw, gw,...  287 us
    pallas_call x1, Pallas kernels, front(): pl.pallas_call(functools.partial(front_kernel, n_dev), out_shape=(act, ja...  65 us
    pallas_call x1, Pallas kernels, attend_backward(): pl.pallas_call(functools.partial(attn_bwd_kernel, seq_len), grid=(n_heads...  41.3 us
    pallas_call x1, Pallas kernels, attend_forward(): pl.pallas_call(functools.partial(attn_fwd_kernel, seq_len), grid=(n_heads...  30.9 us
    pallas_call x1, Pallas kernels, norm_back(): pl.pallas_call(norm_back_kernel, grid=(rows // blk,), out_shape=(act, act...  24.8 us
    all_to_all x1, waiting for transfers between devices, device_step(): gy = exchange(gy_late).reshape(rows, d_model)  17.1 us
    dot_general x1, matrix products, dot_tn(): lax.dot_general(a, b, (((0,), (0,)), ((), ())), preferred_element_type=jn...  15.3 us
    dot_general x1, matrix products, dot_nn(): lax.dot_general(a, b, (((1,), (0,)), ((), ())), preferred_element_type=jn...  14.4 us
  transfers between devices with their start and end apart: 3, of which 1 were waited for; matrix products, arithmetic and copies ran while one was open for 5% of the time, Pallas kernels for 69%

profile of v3, /device:TPU:113, one launch (start us, length us, event | category | flops | bytes accessed | tf_op | source)
XLA Modules:
  0.0 556.6 jit_solution(1228830850061911783)
XLA Ops:
  7.2 1.3 broadcast_in_dim.18.gn_ref
  8.5 1.3 broadcast_in_dim.19.gq_ref
  9.8 1.3 broadcast_in_dim.20.gk_ref
  11.1 2.0 cosine_bitcast_fusion
  13.0 0.5 reduce-precision_convert_fusion.1
  13.5 1.3 pad_maximum_fusion.tab_ref
  14.9 65.0 %front.1 = (bf16[1024,2048]{1,0:T(8,128)(2,1)}, f32[1024,256]{1,0:T(8,128)}, bf16[1024,2048]{1,0:T(8,128)(2,1)}, bf16[1024,2048]{1,0:T(8,128)(2,1)}, bf16[1024,2...) custom-call(bf16[8,128,2048]{2,1,0:T(8,128)(2,1)} %x_loc.1, ...), custom_call_target="tpu_custom_call" | custom-call | flops 25769803776 | bytes 62914560 | tf_op jit(solution)/shard_map/front/pallas_call | solution.py:260
  79.9 4.7 all-to-all-start.1
  84.6 0.2 reduce-scatter.2.cloned.1.call-start
  84.8 30.9 %attn_fwd.1 = (bf16[1024,2048]{1,0:T(8,128)(2,1)}, f32[16,1,1024]{2,1,0:T(1,128)}) custom-call(bf16[1024,2048]{1,0:T(8,128)(2,1)} %get-tuple-element.35.q_ref, bf16[1024,2048]{1,0:T(8,128)(2,1)} %get-tuple-element.36.k_ref, bf16[1024,2048]{1,0:T(8,128)(2,1)} %get-tuple-element.37.v_ref), custom_call_target="tpu_custom_call" | custom-call | flops 8589934592 | bytes 16777216 | tf_op jit(solution)/shard_map/attn_fwd/pallas_call | solution.py:101
  115.8 17.1 %all-to-all-done.1 = bf16[8,128,2048]{2,1,0:T(8,128)(2,1)} async-done(((bf16[8,128,2048]{2,1,0:T(8,128)(2,1)}), bf16[8,128,2048]{2,1,0:T(8,128)(2,1)}, u32[]{:S(2)}, u32[]{:S(2)}) %all-to-all-start.1) | async-done | bytes 4194336 | tf_op jit(solution)/shard_map/all_to_all | solution.py:606
  132.9 15.3 %fusion.5 = f32[2048,2048]{1,0:T(8,128)} fusion(bf16[1024,2048]{1,0:T(8,128)(2,1)} %get-tuple-element.38, bf16[1024,2048]{1,0:T(8,128)(2,1)} %bitcast.5.gy_ref), kind=kOutput, calls=%fused_computation.17 | convolution fusion | flops 8589934592 | bytes 25165824 | tf_op jit(solution)/shard_map/dot_general | solution.py:41
  148.3 0.1 reduce-scatter.2.cloned.1.call-update
  148.3 14.4 %add_convert_fusion = bf16[1024,2048]{1,0:T(8,128)(2,1)} fusion(bf16[1024,2048]{1,0:T(8,128)(2,1)} %get-tuple-element.33.x_ref, bf16[1024,2048]{1,0:T(8,128)(2,1)} %get-tuple-element.38, bf16[2048,2048]{1,0:T(8,128)(2,1)} %param.17), kind=kOutput, calls=%fused_computation | convolution fusion | flops 8596226048 | bytes 20971520 | tf_op jit(solution)/shard_map/dot_general | solution.py:33
  162.7 5.5 all-to-all-start
  168.2 13.9 %convolution_convert_fusion.do_ref = bf16[1024,2048]{1,0:T(8,128)(2,1)} fusion(bf16[1024,2048]{1,0:T(8,128)(2,1)} %bitcast.5.gy_ref, bf16[2048,2048]{1,0:T(8,128)(2,1)} %param.17), kind=kOutput, calls=%fused_computation.1 | convolution fusion | flops 8592031744 | bytes 16777216 | tf_op jit(solution)/shard_map/dot_general | solution.py:37
  182.1 41.3 %attn_bwd.1 = (bf16[1024,2048]{1,0:T(8,128)(2,1)}, bf16[1024,2048]{1,0:T(8,128)(2,1)}, bf16[1024,2048]{1,0:T(8,128)(2,1)}) custom-call(bf16[1024,2048]{1,0:T(8,128)(2,1)} %get-tuple-element.35.q_ref, bf16[1024,2048]{1,0:T(8,128)(2,1)} %get-tuple-element.36.k_ref, bf16[1024,2048]{1,0:T(8,128)(2,1)} %get-tuple-element.37.v_ref, ...), custom_call_target="tpu_custom_call" | custom-call | flops 21474836480 | bytes 29360128 | tf_op jit(solution)/shard_map/attn_bwd/pallas_call | solution.py:117
  223.4 24.8 %norm_back.1 = (bf16[1024,2048]{1,0:T(8,128)(2,1)}, bf16[1024,2048]{1,0:T(8,128)(2,1)}, f32[1,2048]{1,0:T(1,128)}, f32[1,2048]{1,0:T(1,128)}) custom-call(bf16[1024,2048]{1,0:T(8,128)(2,1)} %get-tuple-element.43.dq_ref, bf16[1024,2048]{1,0:T(8,128)(2,1)} %get-tuple-element.44.dk_ref, f32[1024,2048]{1,0:T(8,128)} %get-tuple-element.45.q1_ref, ...), custom_call_target="tpu_custom_call" | custom-call | flops 83886080 | bytes 50331648 | tf_op jit(solution)/shard_map/norm_back/pallas_call | solution.py:314
  248.2 287.1 %tail.1 = (f32[256,2048]{1,0:T(8,128)}, f32[256,2048]{1,0:T(8,128)}, f32[256,2048]{1,0:T(8,128)}, bf16[8,128,2048]{2,1,0:T(8,128)(2,1)}, f32[8,256]{1,0:T(8,128)}) custom-call(bf16[2048,1024]{1,0:T(8,128)(2,1)} %get-tuple-element.39.ht_ref, bf16[1024,2048]{1,0:T(8,128)(2,1)} %get-tuple-element.42.dy_v, bf16[1024,2048]{1,0:T(8,128)(2,1)} %get-tuple-element.48.dy_k, ...), custom_call_target="tpu_custom_call" | custom-call | flops 51539607552 | bytes 67108864 | tf_op jit(solution)/shard_map/tail/pallas_call | solution.py:572
  535.3 0.0 all-to-all-done
  535.3 1.4 fusion.4
  536.7 0.0 reduce-scatter.2.cloned.1.call-done
  536.7 0.0 copy-start
  536.7 4.9 copy.24
  541.6 0.0 copy-done
  541.6 2.1 copy.25
  543.7 1.0 copy-done.3
  544.7 1.3 copy.26
  546.0 1.0 copy-done.2
  547.1 1.3 copy.27
  548.4 0.0 copy-done.1
  548.4 1.3 copy.28
  (4 shorter events, 0.0 us)
Async XLA Ops:
  79.9 53.0 %all-to-all-start.1 = ((bf16[8,128,2048]{2,1,0:T(8,128)(2,1)}), bf16[8,128,2048]{2,1,0:T(8,128)(2,1)}, u32[]{:S(2)}, u32[]{:S(2)}) async-start(bf16[8,128,2048]{2,1,0:T(8,128)(2,1)} %param.11), calls=%async_computation.1 | async-start | bytes 8388608 | tf_op jit(solution)/shard_map/all_to_all | solution.py:606
  84.6 452.1 %reduce-scatter.2.cloned.1.call-start = ((), (), s32[]{:S(2)}) async-start(), calls=%async_computation.3 | async-start | bytes 18874368 | tf_op jit(solution)/shard_map/reduce_scatter | solution.py:599
  162.7 372.5 %all-to-all-start = ((bf16[8,128,2048]{2,1,0:T(8,128)(2,1)}), bf16[8,128,2048]{2,1,0:T(8,128)(2,1)}, u32[]{:S(2)}, u32[]{:S(2)}) async-start(bf16[8,128,2048]{2,1,0:T(8,128)(2,1)} %bitcast.18), calls=%async_computation | async-start | bytes 8388608 | tf_op jit(solution)/shard_map/all_to_all | solution.py:610
  536.7 4.9 copy-start
  541.6 3.1 copy-start.3
  544.7 2.3 copy-start.2
  544.7 3.7 copy-start.1
Sparse Core Ops, SparseCore 0:
  148.4 144.1 reduce-scatter.1

commit v4 on v3

--- a/solution.py
+++ b/solution.py
@@ -41,7 +41,7 @@
     return lax.dot_general(a, b, (((0,), (0,)), ((), ())), preferred_element_type=jnp.float32)
 
 
-def attn_fwd_kernel(seq_len, q_ref, k_ref, v_ref, o_ref, lse_ref):
+def attn_fwd_kernel(seq_len, q_ref, k_ref, v_ref, o_ref, ot_ref, lse_ref):
     scale2 = LOG2E * HEAD_DIM ** -0.5
     for start in range(0, seq_len, Q_BLOCK):
         stop = start + Q_BLOCK
@@ -62,35 +62,10 @@
             p_past = jnp.exp2(s_past * scale2 - m2)
             l = l + jnp.sum(p_past, axis=0, keepdims=True)
             acc = acc + dot_tn(v_ref[0:start, :], p_past.astype(jnp.bfloat16))
-        o_ref[start:stop, :] = (acc / l).T.astype(o_ref.dtype)
+        out = acc / l
+        ot_ref[:, start:stop] = out.astype(ot_ref.dtype)
+        o_ref[start:stop, :] = out.T.astype(o_ref.dtype)
         lse_ref[0, :, start:stop] = m2 + jnp.log2(l)
-
-
-def attn_bwd_kernel(seq_len, q_ref, k_ref, v_ref, do_ref, lse_ref, dq_ref, dk_ref, dv_ref, dk_acc, dv_acc):
-    scale = HEAD_DIM ** -0.5
-    scale2 = LOG2E * scale
-    dk_acc[...] = jnp.zeros_like(dk_acc)
-    dv_acc[...] = jnp.zeros_like(dv_acc)
-    for start in range(0, seq_len, Q_BLOCK):
-        stop = start + Q_BLOCK
-        q_blk = q_ref[start:stop, :]
-        do_blk = do_ref[start:stop, :]
-        lse = lse_ref[0, :, start:stop]
-        k_all = k_ref[0:stop, :]
-        s = dot_nt(k_all, q_blk)
-        p = jnp.exp2(s * scale2 - lse)
-        key_i = lax.broadcasted_iota(jnp.int32, (Q_BLOCK, Q_BLOCK), 0)
-        qry_i = lax.broadcasted_iota(jnp.int32, (Q_BLOCK, Q_BLOCK), 1)
-        p_diag = jnp.where(key_i <= qry_i, p[start:stop, :], 0.0)
-        p = jnp.concatenate([p[0:start, :], p_diag], axis=0) if start else p_diag
-        dp = dot_nt(v_ref[0:stop, :], do_blk)
-        delta = jnp.sum(p * dp, axis=0, keepdims=True)
-        ds = (p * (dp - delta) * scale).astype(jnp.bfloat16)
-        dv_acc[0:stop, :] += dot_nn(p.astype(jnp.bfloat16), do_blk)
-        dk_acc[0:stop, :] += dot_nn(ds, q_blk)
-        dq_ref[start:stop, :] = dot_tn(k_all, ds).T.astype(dq_ref.dtype)
-    dk_ref[...] = dk_acc[...].astype(dk_ref.dtype)
-    dv_ref[...] = dv_acc[...].astype(dv_ref.dtype)
 
 
 def attend_forward(q, k, v):
@@ -101,29 +76,12 @@
     return pl.pallas_call(
         functools.partial(attn_fwd_kernel, seq_len),
         grid=(n_heads,),
-        out_shape=(jax.ShapeDtypeStruct(q.shape, jnp.bfloat16), jax.ShapeDtypeStruct((n_heads, 1, seq_len), jnp.float32)),
+        out_shape=(jax.ShapeDtypeStruct(q.shape, jnp.bfloat16), jax.ShapeDtypeStruct((d_model, seq_len), jnp.bfloat16), jax.ShapeDtypeStruct((n_heads, 1, seq_len), jnp.float32)),
         in_specs=[head_spec] * 3,
-        out_specs=(head_spec, pl.BlockSpec((1, 1, seq_len), lambda h: (h, 0, 0))),
+        out_specs=(head_spec, pl.BlockSpec((HEAD_DIM, seq_len), lambda h: (h, 0)), pl.BlockSpec((1, 1, seq_len), lambda h: (h, 0, 0))),
         cost_estimate=pl.CostEstimate(flops=flops, bytes_accessed=4 * q.size * 2, transcendentals=seq_len * seq_len * n_heads),
         name="attn_fwd",
     )(q, k, v)
-
-
-def attend_backward(q, k, v, d_out, lse):
-    seq_len, d_model = q.shape
-    n_heads = d_model // HEAD_DIM
-    head_spec = pl.BlockSpec((seq_len, HEAD_DIM), lambda h: (0, h))
-    flops = 5 * 2 * seq_len * seq_len * d_model
-    return pl.pallas_call(
-        functools.partial(attn_bwd_kernel, seq_len),
-        grid=(n_heads,),
-        out_shape=(jax.ShapeDtypeStruct(q.shape, jnp.bfloat16),) * 3,
-        in_specs=[head_spec] * 4 + [pl.BlockSpec((1, 1, seq_len), lambda h: (h, 0, 0))],
-        out_specs=(head_spec,) * 3,
-        scratch_shapes=[pltpu.VMEM((seq_len, HEAD_DIM), jnp.float32)] * 2,
-        cost_estimate=pl.CostEstimate(flops=flops, bytes_accessed=7 * q.size * 2, transcendentals=seq_len * seq_len * n_heads),
-        name="attn_bwd",
-    )(q, k, v, d_out, lse)
 
 
 MESH = pl.DeviceIdType.MESH
@@ -274,53 +232,267 @@
     )(x_loc, pos_loc[:, None, :], rope_table(rows), g_norm[None], g_query[None], g_key[None], w_query, w_key, w_value)
 
 
-def norm_back_kernel(dq_ref, dk_ref, q1_ref, k1_ref, cs_ref, gq_ref, gk_ref,
-                     oq_ref, ok_ref, tq_ref, tk_ref, tmp_ref, nrm_ref):
-    cos_t, sin_t = cs_ref[:, 0:HEAD_DIM], cs_ref[:, HEAD_DIM:2 * HEAD_DIM]
-    for d_ref, raw_ref, g_ref, out_ref, t_ref in ((dq_ref, q1_ref, gq_ref, oq_ref, tq_ref), (dk_ref, k1_ref, gk_ref, ok_ref, tk_ref)):
-        raw = raw_ref[...]
-        inv = row_inv(raw)
-        total = jnp.zeros((raw.shape[0], HEAD_DIM), jnp.float32)
-        for at in range(0, raw.shape[1], HEAD_DIM):
-            d_u = d_ref[:, at:at + HEAD_DIM].astype(jnp.float32)
-            d_n = d_u * cos_t - pltpu.roll(d_u, HEAD_DIM // 2, 1) * sin_t
-            hat = raw_ref[:, at:at + HEAD_DIM] * inv
-            terms = jnp.sum(d_n * hat, axis=0, keepdims=True)
-
-            @pl.when(pl.program_id(0) == 0)
+def middle_kernel(n_dev, y_seq, at_ref, gy_ref, wo_ref, q_ref, k_ref, v_ref, q1_ref, k1_ref, cs_ref, lse_ref, gq_ref, gk_ref,
+                  y_out, gw_ref, dq_ref, dk_ref, dv_ref, tq_ref, tk_ref,
+                  wo, at_own, at_par, gy_own, gy_par, rs, dqk, hbuf, dvb, dob, dk_acc, dv_acc, rawb, tmp, nrm,
+                  load_sem, y_send, y_recv, y_loc, part_send, part_recv, rs_send, rs_recv, h_sem, dv_sem, raw_sem, dqk_sem,
+                  fin_loc, fin_send, fin_recv):
+    me = lax.axis_index('sp')
+    chip, core = me // 2, me % 2
+    n_chips = n_dev // 2
+    step_dir = 1 - 2 * core
+    partner = me + step_dir
+    right = 2 * lax.rem(chip + step_dir + n_chips, n_chips) + core
+    rows, d_model = gy_ref.shape
+    n_heads = d_model // HEAD_DIM
+    half, sub = d_model // 2, d_model // 4
+    piece, chunk, own_rows = rows // n_dev, d_model // n_chips, d_model // n_dev
+    other = pl.ds(pl.multiple_of((1 - core) * half, half), half)
+
+    loads = [pltpu.make_async_copy(s, d, load_sem.at[i]) for i, (s, d) in enumerate(((at_ref, at_own), (gy_ref, gy_own), (wo_ref, wo)))]
+    for cp in loads:
+        cp.start()
+
+    def head_copies(h, slot):
+        cols = pl.ds(pl.multiple_of(h * HEAD_DIM, HEAD_DIM), HEAD_DIM)
+        return [pltpu.make_async_copy(r.at[:, cols], hbuf.at[slot, i], h_sem.at[slot, i]) for i, r in enumerate((q_ref, k_ref, v_ref))]
+
+    for cp in head_copies(0, 0):
+        cp.start()
+
+    barrier = pltpu.get_barrier_semaphore()
+    for off in range(1, n_dev):
+        pl.semaphore_signal(barrier, inc=1, device_id={'sp': lax.rem(me + off, n_dev)}, device_id_type=MESH)
+    pl.semaphore_wait(barrier, n_dev - 1)
+
+    parts = [pltpu.make_async_remote_copy(src_ref=s, dst_ref=d, send_sem=part_send.at[i], recv_sem=part_recv.at[i], device_id={'sp': partner}, device_id_type=MESH)
+             for i, (s, d) in enumerate(((at_ref, at_par), (gy_ref.at[:, other], gy_par)))]
+    for cp in parts:
+        cp.start()
+
+    def rs_copy(ch, s):
+        return pltpu.make_async_remote_copy(src_ref=rs.at[ch, s], dst_ref=rs.at[ch, s + 1], send_sem=rs_send.at[ch, s], recv_sem=rs_recv.at[ch, s],
+                                            device_id={'sp': right}, device_id_type=MESH)
+
+    n_tile = 256
+
+    def ring_step(ch, s):
+        owner = lax.rem(chip - step_dir * (1 + s) + 2 * n_chips, n_chips)
+        row_at = pl.ds(pl.multiple_of(owner * chunk, chunk), chunk)
+
+        def tile(t, carry):
+            col = pl.multiple_of(t * n_tile, n_tile)
+            in_half = pl.multiple_of(ch * sub + col, n_tile)
+            term = dot_nn(at_own[row_at, :], gy_own[:, pl.ds(pl.multiple_of(core * half + in_half, n_tile), n_tile)])
+            term = term + dot_nn(at_par[row_at, :], gy_par[:, pl.ds(in_half, n_tile)])
+
+            @pl.when(s == 0)
             def _():
-                t_ref[:, at:at + HEAD_DIM] = terms
-
-            @pl.when(pl.program_id(0) > 0)
+                rs[ch, s, :, pl.ds(col, n_tile)] = term
+
+            @pl.when(s > 0)
             def _():
-                t_ref[:, at:at + HEAD_DIM] += terms
-
-            d_n = d_n * g_ref[:, at:at + HEAD_DIM].astype(jnp.float32)
-            total = total + d_n * hat
-            tmp_ref[:, at:at + HEAD_DIM] = d_n
-            nrm_ref[:, at:at + HEAD_DIM] = hat
-        mean = jnp.sum(total, axis=-1, keepdims=True) * (1.0 / raw.shape[1])
-        out_ref[...] = (inv * (tmp_ref[...] - nrm_ref[...] * mean)).astype(jnp.bfloat16)
-
-
-def norm_back(d_q, d_k, q1, k1, cos_sin, g_query, g_key):
-    rows, d_model = d_q.shape
-    blk = ROW_BLOCK
-    row_spec = pl.BlockSpec((blk, d_model), lambda i: (i, 0))
-    tab_spec = pl.BlockSpec((blk, 2 * HEAD_DIM), lambda i: (i, 0))
-    vec_spec = pl.BlockSpec((1, d_model), lambda i: (0, 0))
-    act = jax.ShapeDtypeStruct((rows, d_model), jnp.bfloat16)
-    vec = jax.ShapeDtypeStruct((1, d_model), jnp.float32)
+                rs[ch, s, :, pl.ds(col, n_tile)] += term
+
+            return carry
+
+        lax.fori_loop(0, sub // n_tile, tile, 0)
+
+    def ring(i):
+        ch, s = lax.rem(i, 2), i // 2
+
+        @pl.when(s > 0)
+        def _():
+            rs_copy(ch, s - 1).wait_recv()
+
+        ring_step(ch, s)
+
+        @pl.when(s < N_SLOTS - 1)
+        def _():
+            rs_copy(ch, s).start()
+
+    def y_remote(off):
+        dest = lax.rem(me + off, n_dev)
+        return pltpu.make_async_remote_copy(src_ref=y_seq.at[dest], dst_ref=y_out.at[me], send_sem=y_send.at[off], recv_sem=y_recv.at[off],
+                                            device_id={'sp': dest}, device_id_type=MESH)
+
+    y_own = pltpu.make_async_copy(y_seq.at[me], y_out.at[me], y_loc)
+    for off in range(1, n_dev):
+        y_remote(off).start()
+    y_own.start()
+
+    def finish_out(ch):
+        keep = pl.ds(pl.multiple_of(core * own_rows, own_rows), own_rows)
+        give = pl.ds(pl.multiple_of((1 - core) * own_rows, own_rows), own_rows)
+        cols = pl.ds(pl.multiple_of(core * half + ch * sub, sub), sub)
+        loc = pltpu.make_async_copy(rs.at[ch, N_SLOTS - 1, keep, :], gw_ref.at[:, cols], fin_loc.at[ch])
+        rem = pltpu.make_async_remote_copy(src_ref=rs.at[ch, N_SLOTS - 1, give, :], dst_ref=gw_ref.at[:, cols], send_sem=fin_send.at[ch], recv_sem=fin_recv.at[ch],
+                                           device_id={'sp': partner}, device_id_type=MESH)
+        return loc, rem
+
+    scale = HEAD_DIM ** -0.5
+    scale2 = LOG2E * scale
+
+    def dv_copy(h, slot):
+        cols = pl.ds(pl.multiple_of(h * HEAD_DIM, HEAD_DIM), HEAD_DIM)
+        return pltpu.make_async_copy(dvb.at[slot], dv_ref.at[:, cols], dv_sem.at[slot])
+
+    def head(h, carry):
+        slot = lax.rem(h, 2)
+        cols = pl.ds(pl.multiple_of(h * HEAD_DIM, HEAD_DIM), HEAD_DIM)
+        in_pair = pl.ds(pl.multiple_of(slot * HEAD_DIM, HEAD_DIM), HEAD_DIM)
+
+        @pl.when(slot == 0)
+        def _():
+            def do_tile(t, c2):
+                ra = pl.ds(pl.multiple_of(t * 256, 256), 256)
+                dob[ra, :] = dot_nt(gy_own[ra, :], wo[pl.ds(pl.multiple_of(h * HEAD_DIM, 2 * HEAD_DIM), 2 * HEAD_DIM), :]).astype(jnp.bfloat16)
+                return c2
+
+            lax.fori_loop(0, rows // 256, do_tile, 0)
+
+        for cp in head_copies(h, slot):
+            cp.wait()
+
+        @pl.when(h + 1 < n_heads)
+        def _():
+            for cp in head_copies(h + 1, 1 - slot):
+                cp.start()
+
+        dk_acc[...] = jnp.zeros_like(dk_acc)
+        dv_acc[...] = jnp.zeros_like(dv_acc)
+        for start in range(0, rows, Q_BLOCK):
+            stop = start + Q_BLOCK
+            q_blk = hbuf[slot, 0, start:stop, :]
+            do_blk = dob[start:stop, in_pair]
+            lse = lse_ref[h, :, start:stop]
+            k_all = hbuf[slot, 1, 0:stop, :]
+            p = jnp.exp2(dot_nt(k_all, q_blk) * scale2 - lse)
+            key_i = lax.broadcasted_iota(jnp.int32, (Q_BLOCK, Q_BLOCK), 0)
+            qry_i = lax.broadcasted_iota(jnp.int32, (Q_BLOCK, Q_BLOCK), 1)
+            p_diag = jnp.where(key_i <= qry_i, p[start:stop, :], 0.0)
+            p = jnp.concatenate([p[0:start, :], p_diag], axis=0) if start else p_diag
+            dp = dot_nt(hbuf[slot, 2, 0:stop, :], do_blk)
+            delta = jnp.sum(p * dp, axis=0, keepdims=True)
+            ds = (p * (dp - delta) * scale).astype(jnp.bfloat16)
+            dv_acc[0:stop, :] += dot_nn(p.astype(jnp.bfloat16), do_blk)
+            dk_acc[0:stop, :] += dot_nn(ds, q_blk)
+            dqk[0, start:stop, cols] = dot_tn(k_all, ds).T.astype(jnp.bfloat16)
+        dqk[1, :, cols] = dk_acc[...].astype(jnp.bfloat16)
+
+        @pl.when(h >= 2)
+        def _():
+            dv_copy(h, slot).wait()
+
+        dvb[slot] = dv_acc[...].astype(jnp.bfloat16)
+        dv_copy(h, slot).start()
+
+        ring_from = n_heads - 6
+
+        @pl.when(jnp.logical_and(h >= ring_from, lax.rem(h - ring_from, 2) == 1))
+        def _():
+            ring(2 + (h - ring_from) // 2)
+
+        return carry
+
+    loads[0].wait()
+    loads[1].wait()
+    for cp in parts:
+        cp.wait_recv()
+    for i in range(2):
+        ring(i)
+    loads[2].wait()
+    lax.fori_loop(0, n_heads, head, 0)
+    for slot in range(2):
+        dv_copy(0, slot).wait()
+
+    def raw_copy(i, b, slot):
+        src = (q1_ref, k1_ref)[i]
+        return pltpu.make_async_copy(src.at[pl.ds(pl.multiple_of(b * piece, piece), piece), :], rawb.at[slot], raw_sem.at[slot])
+
+    for i, g_ref, t_ref in ((0, gq_ref, tq_ref), (1, gk_ref, tk_ref)):
+        t_ref[...] = jnp.zeros_like(t_ref)
+        raw_copy(i, 0, 0).start()
+
+        def norm_rows(b, carry):
+            slot = lax.rem(b, 2)
+            raw_copy(i, b, slot).wait()
+
+            @pl.when(b + 1 < n_dev)
+            def _():
+                raw_copy(i, b + 1, 1 - slot).start()
+
+            at = pl.ds(pl.multiple_of(b * piece, piece), piece)
+            inv = row_inv(rawb[slot])
+            cos_t, sin_t = cs_ref[at, 0:HEAD_DIM], cs_ref[at, HEAD_DIM:2 * HEAD_DIM]
+            total = jnp.zeros((piece, HEAD_DIM), jnp.float32)
+            for c in range(0, d_model, HEAD_DIM):
+                d_u = dqk[i, at, c:c + HEAD_DIM].astype(jnp.float32)
+                d_n = d_u * cos_t - pltpu.roll(d_u, HEAD_DIM // 2, 1) * sin_t
+                hat = rawb[slot, :, c:c + HEAD_DIM] * inv
+                t_ref[:, c:c + HEAD_DIM] += jnp.sum(d_n * hat, axis=0, keepdims=True)
+                d_n = d_n * g_ref[:, c:c + HEAD_DIM].astype(jnp.float32)
+                total = total + d_n * hat
+                tmp[:, c:c + HEAD_DIM] = d_n
+                nrm[:, c:c + HEAD_DIM] = hat
+            mean = jnp.sum(total, axis=-1, keepdims=True) * (1.0 / d_model)
+            for c in range(0, d_model, HEAD_DIM):
+                dqk[i, at, c:c + HEAD_DIM] = (inv * (tmp[:, c:c + HEAD_DIM] - nrm[:, c:c + HEAD_DIM] * mean)).astype(jnp.bfloat16)
+            return carry
+
+        lax.fori_loop(0, n_dev, norm_rows, 0)
+        pltpu.make_async_copy(dqk.at[i], (dq_ref, dk_ref)[i], dqk_sem.at[i]).start()
+        if i == 0:
+            ring(jnp.int32(5))
+
+    for ch in range(2):
+        ring(jnp.int32(6 + ch))
+        for cp in finish_out(ch):
+            cp.start()
+    for cp in parts:
+        cp.wait_send()
+    for ch in range(2):
+        for s in range(N_SLOTS - 1):
+            rs_copy(ch, s).wait_send()
+    for off in range(1, n_dev):
+        y_remote(off).wait()
+    y_own.wait()
+    for i in range(2):
+        pltpu.make_async_copy(dqk.at[i], (dq_ref, dk_ref)[i], dqk_sem.at[i]).wait()
+    for ch in range(2):
+        loc, rem = finish_out(ch)
+        loc.wait()
+        rem.wait()
+
+
+def middle(n_dev, y_seq, a_t, gy, w_out, q_rot, k_rot, v_val, q1, k1, cos_sin, lse, g_query, g_key):
+    rows, d_model = gy.shape
+    piece, chunk, own_rows, sub = rows // n_dev, d_model // (n_dev // 2), d_model // n_dev, d_model // 4
+    hbm = pl.BlockSpec(memory_space=pl.ANY)
+    vmem = pl.BlockSpec(memory_space=pltpu.VMEM)
+    f32, bf16 = jnp.float32, jnp.bfloat16
+    act = jax.ShapeDtypeStruct((rows, d_model), bf16)
+    vec = jax.ShapeDtypeStruct((1, d_model), f32)
+    dma = pltpu.SemaphoreType.DMA
     return pl.pallas_call(
-        norm_back_kernel,
-        grid=(rows // blk,),
-        out_shape=(act, act, vec, vec),
-        in_specs=[row_spec] * 4 + [tab_spec] + [vec_spec] * 2,
-        out_specs=(row_spec, row_spec, vec_spec, vec_spec),
-        scratch_shapes=[pltpu.VMEM((blk, d_model), jnp.float32)] * 2,
-        cost_estimate=pl.CostEstimate(flops=40 * rows * d_model, bytes_accessed=24 * rows * d_model, transcendentals=0),
-        name="norm_back",
-    )(d_q, d_k, q1, k1, cos_sin, g_query[None], g_key[None])
+        functools.partial(middle_kernel, n_dev),
+        out_shape=(jax.ShapeDtypeStruct((n_dev, piece, d_model), bf16), jax.ShapeDtypeStruct((own_rows, d_model), f32), act, act, act, vec, vec),
+        in_specs=[hbm] * 9 + [vmem] * 4,
+        out_specs=(hbm,) * 5 + (vmem,) * 2,
+        scratch_shapes=[
+            pltpu.VMEM((d_model, d_model), bf16), pltpu.VMEM((d_model, rows), bf16), pltpu.VMEM((d_model, rows), bf16),
+            pltpu.VMEM((rows, d_model), bf16), pltpu.VMEM((rows, d_model // 2), bf16),
+            pltpu.VMEM((2, N_SLOTS, chunk, sub), f32), pltpu.VMEM((2, rows, d_model), bf16),
+            pltpu.VMEM((2, 3, rows, HEAD_DIM), bf16), pltpu.VMEM((2, rows, HEAD_DIM), bf16), pltpu.VMEM((rows, 2 * HEAD_DIM), bf16),
+            pltpu.VMEM((rows, HEAD_DIM), f32), pltpu.VMEM((rows, HEAD_DIM), f32),
+            pltpu.VMEM((2, piece, d_model), f32), pltpu.VMEM((piece, d_model), f32), pltpu.VMEM((piece, d_model), f32),
+            dma((3,)), dma((n_dev,)), dma((n_dev,)), dma, dma((2,)), dma((2,)), dma((2, 3)), dma((2, 3)), dma((2, 3)), dma((2,)), dma((2,)), dma((2,)),
+            dma((2,)), dma((2,)), dma((2,)),
+        ],
+        compiler_params=pltpu.CompilerParams(collective_id=2, has_side_effects=True, vmem_limit_bytes=67043328),
+        cost_estimate=pl.CostEstimate(flops=12 * rows * rows * d_model, bytes_accessed=64 * 1024 * 1024, transcendentals=0),
+        name="middle",
+    )(y_seq.reshape(n_dev, piece, d_model), a_t, gy, w_out, q_rot, k_rot, v_val, q1, k1, cos_sin, lse, g_query[None], g_key[None])
 
 
 N_SLOTS = 4
@@ -595,22 +767,15 @@
     n_dev = mesh.shape['sp']
     exchange = functools.partial(lax.all_to_all, axis_name='sp', split_axis=0, concat_axis=0, tiled=True)
 
-    def sum_rows(partial_sum):
-        return lax.psum_scatter(partial_sum, 'sp', scatter_dimension=0, tiled=True)
-
     def device_step(x_loc, gy_loc, pos_loc, g_norm, w_query, w_key, w_value, w_out, g_query, g_key):
         n_batch, loc_len, d_model = x_loc.shape
         rows = n_batch * loc_len
         x_bf, cos_sin, q_rot, k_rot, v_val, h_t, q1, k1 = front(n_dev, x_loc, pos_loc, g_norm, g_query, g_key, w_query, w_key, w_value)
         gy_late, q_rot = lax.optimization_barrier((gy_loc, q_rot))
         gy = exchange(gy_late).reshape(rows, d_model)
-        attended, lse = attend_forward(q_rot, k_rot, v_val)
-        grad_wo = sum_rows(dot_tn(attended, gy))
+        attended, a_t, lse = attend_forward(q_rot, k_rot, v_val)
         y_seq = (x_bf.astype(jnp.float32) + dot_nn(attended, w_out)).astype(jnp.bfloat16)
-        y_out = exchange(y_seq.reshape(n_batch, loc_len, d_model))
-        d_attn = dot_nt(gy, w_out).astype(jnp.bfloat16)
-        d_q, d_k, d_v = attend_backward(q_rot, k_rot, v_val, d_attn, lse)
-        dq_bf, dk_bf, t_q, t_k = norm_back(d_q, d_k, q1, k1, cos_sin, g_query, g_key)
+        y_out, grad_wo, dq_bf, dk_bf, d_v, t_q, t_k = middle(n_dev, y_seq, a_t, gy, w_out, q_rot, k_rot, v_val, q1, k1, cos_sin, lse, g_query, g_key)
         grad_wv, grad_wk, grad_wq, grad_x, gains = tail(n_dev, h_t, (d_v, dk_bf, dq_bf), (w_value, w_key, w_query), x_bf, gy, g_norm, t_q, t_k)
         return y_out, grad_x, gains[0], grad_wq, grad_wk, grad_wv, grad_wo, gains[1], gains[2]
 

time: 557 us -> 540 us (0.969)
  Pallas kernels: 449 us -> 492 us
  matrix products: 43.6 us -> 14.5 us
  waiting for transfers between devices: 17.2 us -> 2.84 us
  between operations: 14.1 us -> 0.7 us
  starting transfers between devices: 10.4 us -> 4.81 us
    pallas_call x2 -> x1, Pallas kernels: 66.1 us -> 123 us  [middle(): pl.pallas_call(functools.partial(middle_kernel, n_dev), out_shape=(jax.Sh...]
    dot_general x2 -> x0, matrix products: 29.2 us -> none  [the longest x1 15.3 us: dot_tn(): lax.dot_general(a, b, (((0,), (0,)), ((), ())), preferred_element_type=jn...]
    all_to_all x1, waiting for transfers between devices: 17.1 us -> 2.84 us  [device_step(): gy = exchange(gy_late).reshape(rows, d_model)]
    pallas_call x1, Pallas kernels: 287 us -> 273 us  [tail(): pl.pallas_call(functools.partial(tail_kernel, n_dev), out_shape=(gw, gw,...]
    unnamed x13 -> x16, local copies, waits for them, and re-layouts: 13 us -> 14.4 us
  transfers between devices with their start and end apart: 3 -> 1, of which waited for: 1 -> 1; matrix products, arithmetic and copies ran while one was open for 5% -> 3% of each run, Pallas kernels for 69% -> 6%
where the time goes in v4:
time: 540 us; the launch traced here: 538 us
  Pallas kernels  492 us (91%)
  local copies, waits for them, and re-layouts  19.6 us (4%)
  matrix products  14.5 us (3%)
    pallas_call x1, Pallas kernels, tail(): pl.pallas_call(functools.partial(tail_kernel, n_dev), out_shape=(gw, gw,...  273 us
    pallas_call x1, Pallas kernels, middle(): pl.pallas_call(functools.partial(middle_kernel, n_dev), out_shape=(jax.Sh...  123 us
    pallas_call x1, Pallas kernels, front(): pl.pallas_call(functools.partial(front_kernel, n_dev), out_shape=(act, ja...  65.1 us
    pallas_call x1, Pallas kernels, attend_forward(): pl.pallas_call(functools.partial(attn_fwd_kernel, seq_len), grid=(n_heads...  30.9 us
    dot_general x1, matrix products, dot_nn(): lax.dot_general(a, b, (((1,), (0,)), ((), ())), preferred_element_type=jn...  14.5 us
    unnamed x16, local copies, waits for them, and re-layouts  14.4 us
  transfers between devices with their start and end apart: 1, of which 1 were waited for; matrix products, arithmetic and copies ran while one was open for 3% of the time, Pallas kernels for 6%

profile of v4, /device:TPU:113, one launch (start us, length us, event | category | flops | bytes accessed | tf_op | source)
XLA Modules:
  0.0 538.2 jit_solution(2388570419246122941)
XLA Ops:
  0.7 1.3 broadcast_in_dim.18.gn_ref
  1.9 1.3 broadcast_in_dim.19.gq_ref
  3.2 1.3 broadcast_in_dim.20.gk_ref
  4.5 2.0 cosine_bitcast_fusion
  6.5 0.5 reduce-precision_convert_fusion.1
  7.0 1.3 pad_maximum_fusion.tab_ref
  8.3 65.1 %front.1 = (bf16[1024,2048]{1,0:T(8,128)(2,1)}, f32[1024,256]{1,0:T(8,128)}, bf16[1024,2048]{1,0:T(8,128)(2,1)}, bf16[1024,2048]{1,0:T(8,128)(2,1)}, bf16[1024,2...) custom-call(bf16[8,128,2048]{2,1,0:T(8,128)(2,1)} %x_loc.1, ...), custom_call_target="tpu_custom_call" | custom-call | flops 25769803776 | bytes 62914560 | tf_op jit(solution)/shard_map/front/pallas_call | solution.py:218
  73.5 4.8 all-to-all-start
  78.3 30.9 %attn_fwd.1 = (bf16[1024,2048]{1,0:T(8,128)(2,1)}, bf16[2048,1024]{1,0:T(8,128)(2,1)}, f32[16,1,1024]{2,1,0:T(1,128)}) custom-call(bf16[1024,2048]{1,0:T(8,128)(2,1)} %get-tuple-element.36.q_ref, bf16[1024,2048]{1,0:T(8,128)(2,1)} %get-tuple-element.37.k_ref, bf16[1024,2048]{1,0:T(8,128)(2,1)} %get-tuple-element.38.v_ref), custom_call_target="tpu_custom_call" | custom-call | flops 8589934592 | bytes 16777216 | tf_op jit(solution)/shard_map/attn_fwd/pallas_call | solution.py:76
  109.2 14.5 %add_convert_fusion = bf16[1024,2048]{1,0:T(8,128)(2,1)} fusion(bf16[1024,2048]{1,0:T(8,128)(2,1)} %get-tuple-element.34.x_ref, bf16[1024,2048]{1,0:T(8,128)(2,1)} %get-tuple-element.39, bf16[2048,2048]{1,0:T(8,128)(2,1)} %wo_ref.1), kind=kOutput, calls=%fused_computation | convolution fusion | flops 8596226048 | bytes 20971520 | tf_op jit(solution)/shard_map/dot_general | solution.py:33
  123.6 2.8 all-to-all-done
  126.5 122.9 %middle.1 = (bf16[8,128,2048]{2,1,0:T(8,128)(2,1)}, f32[256,2048]{1,0:T(8,128)}, bf16[1024,2048]{1,0:T(8,128)(2,1)}, bf16[1024,2048]{1,0:T(8,128)(2,1)}, bf16[10...) custom-call(bf16[8,128,2048]{2,1,0:T(8,128)(2,1)} %bitcast.18, ...), custom_call_target="tpu_custom_call" | custom-call | flops 25769803776 | bytes 67108864 | tf_op jit(solution)/shard_map/middle/pallas_call | solution.py:477
  249.3 273.1 %tail.1 = (f32[256,2048]{1,0:T(8,128)}, f32[256,2048]{1,0:T(8,128)}, f32[256,2048]{1,0:T(8,128)}, bf16[8,128,2048]{2,1,0:T(8,128)(2,1)}, f32[8,256]{1,0:T(8,128)}) custom-call(bf16[2048,1024]{1,0:T(8,128)(2,1)} %get-tuple-element.47.ht_ref, bf16[1024,2048]{1,0:T(8,128)(2,1)} %get-tuple-element.48.dy_v, bf16[1024,2048]{1,0:T(8,128)(2,1)} %get-tuple-element.49.dy_k, ...), custom_call_target="tpu_custom_call" | custom-call | flops 51539607552 | bytes 67108864 | tf_op jit(solution)/shard_map/tail/pallas_call | solution.py:744
  522.5 1.4 fusion.4
  523.9 0.0 copy-start
  523.9 4.9 copy.25
  528.8 0.0 copy-done
  528.8 0.0 copy-start.4
  528.8 2.1 copy.26
  531.0 1.0 copy-done.4
  531.9 0.0 copy-start.3
  531.9 0.0 copy-start.2
  531.9 1.3 copy.27
  533.2 1.0 copy-done.3
  534.3 0.0 copy-start.1
  534.3 1.3 copy.28
  535.6 0.0 copy-done.2
  535.6 1.3 copy.29
  536.9 0.0 copy-done.1
  536.9 1.3 copy.30
  (1 shorter events, 0.0 us)
Async XLA Ops:
  73.5 53.0 %all-to-all-start = ((bf16[8,128,2048]{2,1,0:T(8,128)(2,1)}), bf16[8,128,2048]{2,1,0:T(8,128)(2,1)}, u32[]{:S(2)}, u32[]{:S(2)}) async-start(bf16[8,128,2048]{2,1,0:T(8,128)(2,1)} %param.11), calls=%async_computation | async-start | bytes 8388608 | tf_op jit(solution)/shard_map/all_to_all | solution.py:775
  523.9 4.9 copy-start
  528.8 3.1 copy-start.4
  531.9 2.3 copy-start.3
  531.9 3.7 copy-start.2
  534.3 2.6 copy-start.1

commit v5 on v4

--- a/solution.py
+++ b/solution.py
@@ -41,47 +41,28 @@
     return lax.dot_general(a, b, (((0,), (0,)), ((), ())), preferred_element_type=jnp.float32)
 
 
-def attn_fwd_kernel(seq_len, q_ref, k_ref, v_ref, o_ref, ot_ref, lse_ref):
+def attend_head(seq_len, load_q, load_k, load_v, store):
     scale2 = LOG2E * HEAD_DIM ** -0.5
     for start in range(0, seq_len, Q_BLOCK):
         stop = start + Q_BLOCK
-        q_blk = q_ref[start:stop, :]
-        s_diag = dot_nt(k_ref[start:stop, :], q_blk)
+        q_blk = load_q(start, stop)
+        s_diag = dot_nt(load_k(start, stop), q_blk)
         key_i = lax.broadcasted_iota(jnp.int32, s_diag.shape, 0)
         qry_i = lax.broadcasted_iota(jnp.int32, s_diag.shape, 1)
         s_diag = jnp.where(key_i <= qry_i, s_diag, NEG_BIG)
         m = jnp.max(s_diag, axis=0, keepdims=True)
         if start:
-            s_past = dot_nt(k_ref[0:start, :], q_blk)
+            s_past = dot_nt(load_k(0, start), q_blk)
             m = jnp.maximum(m, jnp.max(s_past, axis=0, keepdims=True))
         m2 = m * scale2
         p_diag = jnp.exp2(s_diag * scale2 - m2)
         l = jnp.sum(p_diag, axis=0, keepdims=True)
-        acc = dot_tn(v_ref[start:stop, :], p_diag.astype(jnp.bfloat16))
+        acc = dot_tn(load_v(start, stop), p_diag.astype(jnp.bfloat16))
         if start:
             p_past = jnp.exp2(s_past * scale2 - m2)
             l = l + jnp.sum(p_past, axis=0, keepdims=True)
-            acc = acc + dot_tn(v_ref[0:start, :], p_past.astype(jnp.bfloat16))
-        out = acc / l
-        ot_ref[:, start:stop] = out.astype(ot_ref.dtype)
-        o_ref[start:stop, :] = out.T.astype(o_ref.dtype)
-        lse_ref[0, :, start:stop] = m2 + jnp.log2(l)
-
-
-def attend_forward(q, k, v):
-    seq_len, d_model = q.shape
-    n_heads = d_model // HEAD_DIM
-    head_spec = pl.BlockSpec((seq_len, HEAD_DIM), lambda h: (0, h))
-    flops = 2 * 2 * seq_len * seq_len * d_model
-    return pl.pallas_call(
-        functools.partial(attn_fwd_kernel, seq_len),
-        grid=(n_heads,),
-        out_shape=(jax.ShapeDtypeStruct(q.shape, jnp.bfloat16), jax.ShapeDtypeStruct((d_model, seq_len), jnp.bfloat16), jax.ShapeDtypeStruct((n_heads, 1, seq_len), jnp.float32)),
-        in_specs=[head_spec] * 3,
-        out_specs=(head_spec, pl.BlockSpec((HEAD_DIM, seq_len), lambda h: (h, 0)), pl.BlockSpec((1, 1, seq_len), lambda h: (h, 0, 0))),
-        cost_estimate=pl.CostEstimate(flops=flops, bytes_accessed=4 * q.size * 2, transcendentals=seq_len * seq_len * n_heads),
-        name="attn_fwd",
-    )(q, k, v)
+            acc = acc + dot_tn(load_v(0, start), p_past.astype(jnp.bfloat16))
+        store(start, stop, acc / l, m2 + jnp.log2(l))
 
 
 MESH = pl.DeviceIdType.MESH
@@ -92,10 +73,10 @@
     return lax.rsqrt(jnp.mean(values * values, axis=-1, keepdims=True) + NORM_EPS)
 
 
-def front_kernel(n_dev, x_loc, pos_loc, tab_ref, gn_ref, gq_ref, gk_ref, wq_ref, wk_ref, wv_ref,
-                 x_seq, cs_ref, q_ref, k_ref, v_ref, ht_ref, q1_ref, k1_ref,
-                 xv, posv, wbuf, csb, qb, kb, vb, htb, q1b, k1b,
-                 w_sem, x_send, x_recv, p_send, p_recv, own_sem, xs_sem, out_sem):
+def front_kernel(n_dev, x_loc, gy_loc, pos_loc, tab_ref, g_ref, wq_ref, wk_ref, wv_ref,
+                 x_seq, gy_seq, cs_ref, q_ref, k_ref, v_ref, ht_ref, ht_par, q1_ref, k1_ref, a_ref, at_ref, lse_ref,
+                 xv, posv, wbuf, csb, qb, kb, vb, htb, q1b, k1b, ab, atb,
+                 w_sem, x_send, x_recv, g_send, g_recv, p_send, p_recv, own_sem, xs_sem, out_sem, hp_send, hp_recv, a_sem):
     me = lax.axis_index('sp')
     chip, core = me // 2, me % 2
     n_chips = n_dev // 2
@@ -108,7 +89,8 @@
         cp.start()
     mine = pl.ds(pl.multiple_of(me * piece, piece), piece)
     own = [pltpu.make_async_copy(x_loc.at[me], xv.at[mine, :], own_sem.at[0]), pltpu.make_async_copy(pos_loc.at[me], posv.at[me], own_sem.at[1])]
-    for cp in own:
+    own_gy = pltpu.make_async_copy(gy_loc.at[me], gy_seq.at[me], own_sem.at[2])
+    for cp in own + [own_gy]:
         cp.start()
 
     barrier = pltpu.get_barrier_semaphore()
@@ -125,7 +107,9 @@
                                                   device_id={'sp': dest}, device_id_type=MESH))
         sends.append(pltpu.make_async_remote_copy(src_ref=x_loc.at[dest], dst_ref=xv.at[mine, :], send_sem=x_send.at[i], recv_sem=x_recv.at[me],
                                                   device_id={'sp': dest}, device_id_type=MESH))
-    for cp in sends:
+    gy_sends = [pltpu.make_async_remote_copy(src_ref=gy_loc.at[dest], dst_ref=gy_seq.at[me], send_sem=g_send.at[i], recv_sem=g_recv.at[me],
+                                             device_id={'sp': dest}, device_id_type=MESH) for i, dest in enumerate(dests)]
+    for cp in sends + gy_sends:
         cp.start()
 
     def arrival(src):
@@ -137,9 +121,14 @@
 
     def outs(at, slot):
         rows = pl.ds(pl.multiple_of(at, blk), blk)
-        pairs = [(csb.at[slot], cs_ref.at[rows, :]), (qb.at[slot], q_ref.at[rows, :]), (kb.at[slot], k_ref.at[rows, :]), (vb.at[slot], v_ref.at[rows, :]),
+        pairs = [(csb.at[slot], cs_ref.at[rows, :]), (qb.at[rows, :], q_ref.at[rows, :]), (kb.at[rows, :], k_ref.at[rows, :]), (vb.at[rows, :], v_ref.at[rows, :]),
                  (htb.at[slot], ht_ref.at[:, rows]), (q1b.at[slot], q1_ref.at[rows, :]), (k1b.at[slot], k1_ref.at[rows, :])]
         return [pltpu.make_async_copy(s, d, out_sem.at[slot, i]) for i, (s, d) in enumerate(pairs)]
+
+    def ht_send(at, slot, b):
+        cols = pl.ds(pl.multiple_of(at, blk), blk)
+        return pltpu.make_async_remote_copy(src_ref=htb.at[slot], dst_ref=ht_par.at[:, cols], send_sem=hp_send.at[slot], recv_sem=hp_recv.at[b],
+                                            device_id={'sp': 2 * chip + 1 - core}, device_id_type=MESH)
 
     def x_out(src_chip):
         rows = pl.ds(pl.multiple_of(src_chip * blk, blk), blk)
@@ -170,12 +159,13 @@
         def _():
             for cp in outs(at, slot):
                 cp.wait()
+            ht_send(at, slot, b).wait_send()
 
         for e in range(2):
             hot = (lax.broadcasted_iota(jnp.int32, (n_pos, piece), 0) == posv[2 * src_chip + e]).astype(jnp.bfloat16)
             csb[slot, e * piece:(e + 1) * piece, :] = (dot_tn(hot, tab_ref[0]) + dot_tn(hot, tab_ref[1])) + dot_tn(hot, tab_ref[2])
         x_f = xv[pl.ds(at, blk), :].astype(jnp.float32)
-        hidden = (x_f * row_inv(x_f) * gn_ref[...].astype(jnp.float32)).astype(jnp.bfloat16)
+        hidden = (x_f * row_inv(x_f) * g_ref[0:1, :].astype(jnp.float32)).astype(jnp.bfloat16)
         htb[slot] = hidden.T
 
         @pl.when(b == 0)
@@ -183,29 +173,63 @@
             for i, w in enumerate((wv_ref, wq_ref, wk_ref)):
                 pltpu.make_async_copy(w, wbuf.at[i], w_sem.at[i]).wait()
 
-        vb[slot] = dot_nn(hidden, wbuf[0]).astype(jnp.bfloat16)
+        vb[pl.ds(at, blk), :] = dot_nn(hidden, wbuf[0]).astype(jnp.bfloat16)
         cos_t, sin_t = csb[slot, :, 0:HEAD_DIM], csb[slot, :, HEAD_DIM:2 * HEAD_DIM]
-        for i, g_ref, raw_ref, out_ref in ((1, gq_ref, q1b, qb), (2, gk_ref, k1b, kb)):
+        for i, raw_ref, out_ref in ((1, q1b, qb), (2, k1b, kb)):
             raw_ref[slot] = dot_nn(hidden, wbuf[i])
             inv = row_inv(raw_ref[slot])
             for c in range(0, d_model, HEAD_DIM):
-                u = raw_ref[slot, :, c:c + HEAD_DIM] * inv * g_ref[:, c:c + HEAD_DIM].astype(jnp.float32)
-                out_ref[slot, :, c:c + HEAD_DIM] = (u * cos_t + pltpu.roll(u, HEAD_DIM // 2, 1) * sin_t).astype(jnp.bfloat16)
+                u = raw_ref[slot, :, c:c + HEAD_DIM] * inv * g_ref[i:i + 1, c:c + HEAD_DIM].astype(jnp.float32)
+                out_ref[pl.ds(at, blk), c:c + HEAD_DIM] = (u * cos_t + pltpu.roll(u, HEAD_DIM // 2, 1) * sin_t).astype(jnp.bfloat16)
         for cp in outs(at, slot):
             cp.start()
+        ht_send(at, slot, b).start()
         return carry
 
     lax.fori_loop(0, n_chips, block, 0)
+
+    def a_copies(h, slot):
+        cols = pl.ds(pl.multiple_of(h * HEAD_DIM, HEAD_DIM), HEAD_DIM)
+        return (pltpu.make_async_copy(ab.at[slot], a_ref.at[:, cols], a_sem.at[slot, 0]), pltpu.make_async_copy(atb.at[slot], at_ref.at[cols, :], a_sem.at[slot, 1]))
+
+    def head(h, carry):
+        slot = lax.rem(h, 2)
+        cols = pl.ds(pl.multiple_of(h * HEAD_DIM, HEAD_DIM), HEAD_DIM)
+
+        @pl.when(h >= 2)
+        def _():
+            for cp in a_copies(h, slot):
+                cp.wait()
+
+        def store(start, stop, out, lse):
+            atb[slot, :, start:stop] = out.astype(jnp.bfloat16)
+            ab[slot, start:stop, :] = out.T.astype(jnp.bfloat16)
+            lse_ref[h, :, start:stop] = lse
+
+        attend_head(n_dev * piece, lambda i, j: qb[i:j, cols], lambda i, j: kb[i:j, cols], lambda i, j: vb[i:j, cols], store)
+        for cp in a_copies(h, slot):
+            cp.start()
+        return carry
+
+    lax.fori_loop(0, d_model // HEAD_DIM, head, 0)
     for slot in range(2):
-        for cp in outs(0, slot):
+        for cp in outs(0, slot) + list(a_copies(0, slot)):
             cp.wait()
+        ht_send(0, slot, 0).wait_send()
     for i in range(n_chips):
         x_out(i).wait()
+        ht_send(0, 0, i).wait_recv()
     for cp in sends:
         cp.wait_send()
-
-
-def front(n_dev, x_loc, pos_loc, g_norm, g_query, g_key, w_query, w_key, w_value):
+    own_gy.wait()
+    for i, cp in enumerate(gy_sends):
+        cp.wait_send()
+        src = dests[i]
+        pltpu.make_async_remote_copy(src_ref=gy_loc.at[src], dst_ref=gy_seq.at[src], send_sem=g_send.at[0], recv_sem=g_recv.at[src],
+                                     device_id={'sp': src}, device_id_type=MESH).wait_recv()
+
+
+def front(n_dev, x_loc, gy_loc, pos_loc, gains, w_query, w_key, w_value):
     n_batch, piece, d_model = x_loc.shape
     rows, blk = n_batch * piece, 2 * piece
     hbm = pl.BlockSpec(memory_space=pl.ANY)
@@ -213,30 +237,33 @@
     bf16, f32 = jnp.bfloat16, jnp.float32
     act = jax.ShapeDtypeStruct((rows, d_model), bf16)
     raw = jax.ShapeDtypeStruct((rows, d_model), f32)
+    turned = jax.ShapeDtypeStruct((d_model, rows), bf16)
     dma = pltpu.SemaphoreType.DMA
-    stage = pltpu.VMEM((2, blk, d_model), bf16)
+    whole = pltpu.VMEM((rows, d_model), bf16)
     return pl.pallas_call(
         functools.partial(front_kernel, n_dev),
-        out_shape=(act, jax.ShapeDtypeStruct((rows, 2 * HEAD_DIM), f32), act, act, act, jax.ShapeDtypeStruct((d_model, rows), bf16), raw, raw),
-        in_specs=[hbm, hbm] + [vmem] * 4 + [hbm] * 3,
-        out_specs=(hbm,) * 8,
+        out_shape=(act, jax.ShapeDtypeStruct(x_loc.shape, bf16), jax.ShapeDtypeStruct((rows, 2 * HEAD_DIM), f32), act, act, act, turned, turned, raw, raw, act, turned,
+                   jax.ShapeDtypeStruct((d_model // HEAD_DIM, 1, rows), f32)),
+        in_specs=[hbm] * 3 + [vmem] * 2 + [hbm] * 3,
+        out_specs=(hbm,) * 12 + (vmem,),
         scratch_shapes=[
             pltpu.VMEM((rows, d_model), bf16), pltpu.VMEM((n_dev, 1, piece), jnp.int32), pltpu.VMEM((3, d_model, d_model), bf16),
-            pltpu.VMEM((2, blk, 2 * HEAD_DIM), f32), stage, stage, stage, pltpu.VMEM((2, d_model, blk), bf16),
+            pltpu.VMEM((2, blk, 2 * HEAD_DIM), f32), whole, whole, whole, pltpu.VMEM((2, d_model, blk), bf16),
             pltpu.VMEM((2, blk, d_model), f32), pltpu.VMEM((2, blk, d_model), f32),
-            dma((3,)), dma((n_dev,)), dma((n_dev,)), dma((n_dev,)), dma((n_dev,)), dma((2,)), dma((n_dev // 2,)), dma((2, 7)),
+            pltpu.VMEM((2, rows, HEAD_DIM), bf16), pltpu.VMEM((2, HEAD_DIM, rows), bf16),
+            dma((3,)), dma((n_dev,)), dma((n_dev,)), dma((n_dev,)), dma((n_dev,)), dma((n_dev,)), dma((n_dev,)), dma((3,)), dma((n_dev // 2,)), dma((2, 7)), dma((2,)), dma((n_dev // 2,)), dma((2, 2)),
         ],
-        compiler_params=pltpu.CompilerParams(collective_id=1, has_side_effects=True, vmem_limit_bytes=62 * 1024 * 1024),
+        compiler_params=pltpu.CompilerParams(collective_id=1, has_side_effects=True, vmem_limit_bytes=67043328),
         cost_estimate=pl.CostEstimate(flops=6 * rows * d_model * d_model, bytes_accessed=60 * 1024 * 1024, transcendentals=0),
         name="front",
-    )(x_loc, pos_loc[:, None, :], rope_table(rows), g_norm[None], g_query[None], g_key[None], w_query, w_key, w_value)
-
-
-def middle_kernel(n_dev, y_seq, at_ref, gy_ref, wo_ref, q_ref, k_ref, v_ref, q1_ref, k1_ref, cs_ref, lse_ref, gq_ref, gk_ref,
-                  y_out, gw_ref, dq_ref, dk_ref, dv_ref, tq_ref, tk_ref,
-                  wo, at_own, at_par, gy_own, gy_par, rs, dqk, hbuf, dvb, dob, dk_acc, dv_acc, rawb, tmp, nrm,
+    )(x_loc, gy_loc, pos_loc[:, None, :], rope_table(rows), gains, w_query, w_key, w_value)
+
+
+def middle_kernel(n_dev, a_seq, x_home, at_ref, gy_ref, wo_ref, q_ref, k_ref, v_ref, q1_ref, k1_ref, cs_ref, lse_ref, g_ref,
+                  y_out, a_home, gw_ref, dq_ref, dk_ref, dv_ref, tq_ref, tk_ref,
+                  wo, at_own, at_par, gy_own, gy_par, rs, dqk, hbuf, dvb, dob, dk_acc, dv_acc, rawb, tmp, nrm, ahb, xhb, yb,
                   load_sem, y_send, y_recv, y_loc, part_send, part_recv, rs_send, rs_recv, h_sem, dv_sem, raw_sem, dqk_sem,
-                  fin_loc, fin_send, fin_recv):
+                  fin_loc, fin_send, fin_recv, ax_sem, yo_sem):
     me = lax.axis_index('sp')
     chip, core = me // 2, me % 2
     n_chips = n_dev // 2
@@ -313,10 +340,10 @@
 
     def y_remote(off):
         dest = lax.rem(me + off, n_dev)
-        return pltpu.make_async_remote_copy(src_ref=y_seq.at[dest], dst_ref=y_out.at[me], send_sem=y_send.at[off], recv_sem=y_recv.at[off],
+        return pltpu.make_async_remote_copy(src_ref=a_seq.at[dest], dst_ref=a_home.at[me], send_sem=y_send.at[off], recv_sem=y_recv.at[off],
                                             device_id={'sp': dest}, device_id_type=MESH)
 
-    y_own = pltpu.make_async_copy(y_seq.at[me], y_out.at[me], y_loc)
+    y_own = pltpu.make_async_copy(a_seq.at[me], a_home.at[me], y_loc)
     for off in range(1, n_dev):
         y_remote(off).start()
     y_own.start()
@@ -406,11 +433,39 @@
     for slot in range(2):
         dv_copy(0, slot).wait()
 
+    for off in range(1, n_dev):
+        y_remote(off).wait()
+    y_own.wait()
+
+    def home_in(b, slot):
+        return (pltpu.make_async_copy(a_home.at[b], ahb.at[slot], ax_sem.at[slot, 0]), pltpu.make_async_copy(x_home.at[b], xhb.at[slot], ax_sem.at[slot, 1]))
+
+    def y_copy(b, slot):
+        return pltpu.make_async_copy(yb.at[slot], y_out.at[b], yo_sem.at[slot])
+
+    def y_rows(b, carry):
+        slot = lax.rem(b, 2)
+        for cp in home_in(b, slot):
+            cp.wait()
+
+        @pl.when(b + 1 < n_dev)
+        def _():
+            for cp in home_in(b + 1, 1 - slot):
+                cp.start()
+
+        @pl.when(b >= 2)
+        def _():
+            y_copy(b, slot).wait()
+
+        yb[slot] = (xhb[slot].astype(jnp.float32) + dot_nn(ahb[slot], wo[...])).astype(jnp.bfloat16)
+        y_copy(b, slot).start()
+        return carry
+
     def raw_copy(i, b, slot):
         src = (q1_ref, k1_ref)[i]
         return pltpu.make_async_copy(src.at[pl.ds(pl.multiple_of(b * piece, piece), piece), :], rawb.at[slot], raw_sem.at[slot])
 
-    for i, g_ref, t_ref in ((0, gq_ref, tq_ref), (1, gk_ref, tk_ref)):
+    for i, t_ref in ((0, tq_ref), (1, tk_ref)):
         t_ref[...] = jnp.zeros_like(t_ref)
         raw_copy(i, 0, 0).start()
 
@@ -431,7 +486,7 @@
                 d_n = d_u * cos_t - pltpu.roll(d_u, HEAD_DIM // 2, 1) * sin_t
                 hat = rawb[slot, :, c:c + HEAD_DIM] * inv
                 t_ref[:, c:c + HEAD_DIM] += jnp.sum(d_n * hat, axis=0, keepdims=True)
-                d_n = d_n * g_ref[:, c:c + HEAD_DIM].astype(jnp.float32)
+                d_n = d_n * g_ref[i + 1:i + 2, c:c + HEAD_DIM].astype(jnp.float32)
                 total = total + d_n * hat
                 tmp[:, c:c + HEAD_DIM] = d_n
                 nrm[:, c:c + HEAD_DIM] = hat
@@ -444,19 +499,21 @@
         pltpu.make_async_copy(dqk.at[i], (dq_ref, dk_ref)[i], dqk_sem.at[i]).start()
         if i == 0:
             ring(jnp.int32(5))
+            for cp in home_in(0, 0):
+                cp.start()
+            lax.fori_loop(0, n_dev, y_rows, 0)
 
     for ch in range(2):
         ring(jnp.int32(6 + ch))
         for cp in finish_out(ch):
             cp.start()
+    for slot in range(2):
+        y_copy(0, slot).wait()
     for cp in parts:
         cp.wait_send()
     for ch in range(2):
         for s in range(N_SLOTS - 1):
             rs_copy(ch, s).wait_send()
-    for off in range(1, n_dev):
-        y_remote(off).wait()
-    y_own.wait()
     for i in range(2):
         pltpu.make_async_copy(dqk.at[i], (dq_ref, dk_ref)[i], dqk_sem.at[i]).wait()
     for ch in range(2):
@@ -465,7 +522,7 @@
         rem.wait()
 
 
-def middle(n_dev, y_seq, a_t, gy, w_out, q_rot, k_rot, v_val, q1, k1, cos_sin, lse, g_query, g_key):
+def middle(n_dev, a_seq, x_home, a_t, gy, w_out, q_rot, k_rot, v_val, q1, k1, cos_sin, lse, gains):
     rows, d_model = gy.shape
     piece, chunk, own_rows, sub = rows // n_dev, d_model // (n_dev // 2), d_model // n_dev, d_model // 4
     hbm = pl.BlockSpec(memory_space=pl.ANY)
@@ -476,9 +533,9 @@
     dma = pltpu.SemaphoreType.DMA
     return pl.pallas_call(
         functools.partial(middle_kernel, n_dev),
-        out_shape=(jax.ShapeDtypeStruct((n_dev, piece, d_model), bf16), jax.ShapeDtypeStruct((own_rows, d_model), f32), act, act, act, vec, vec),
-        in_specs=[hbm] * 9 + [vmem] * 4,
-        out_specs=(hbm,) * 5 + (vmem,) * 2,
+        out_shape=(jax.ShapeDtypeStruct((n_dev, piece, d_model), bf16), jax.ShapeDtypeStruct((n_dev, piece, d_model), bf16), jax.ShapeDtypeStruct((own_rows, d_model), f32), act, act, act, vec, vec),
+        in_specs=[hbm] * 10 + [vmem] * 3,
+        out_specs=(hbm,) * 6 + (vmem,) * 2,
         scratch_shapes=[
             pltpu.VMEM((d_model, d_model), bf16), pltpu.VMEM((d_model, rows), bf16), pltpu.VMEM((d_model, rows), bf16),
             pltpu.VMEM((rows, d_model), bf16), pltpu.VMEM((rows, d_model // 2), bf16),
@@ -486,19 +543,20 @@
             pltpu.VMEM((2, 3, rows, HEAD_DIM), bf16), pltpu.VMEM((2, rows, HEAD_DIM), bf16), pltpu.VMEM((rows, 2 * HEAD_DIM), bf16),
             pltpu.VMEM((rows, HEAD_DIM), f32), pltpu.VMEM((rows, HEAD_DIM), f32),
             pltpu.VMEM((2, piece, d_model), f32), pltpu.VMEM((piece, d_model), f32), pltpu.VMEM((piece, d_model), f32),
+            pltpu.VMEM((2, piece, d_model), bf16), pltpu.VMEM((2, piece, d_model), bf16), pltpu.VMEM((2, piece, d_model), bf16),
             dma((3,)), dma((n_dev,)), dma((n_dev,)), dma, dma((2,)), dma((2,)), dma((2, 3)), dma((2, 3)), dma((2, 3)), dma((2,)), dma((2,)), dma((2,)),
-            dma((2,)), dma((2,)), dma((2,)),
+            dma((2,)), dma((2,)), dma((2,)), dma((2, 2)), dma((2,)),
         ],
         compiler_params=pltpu.CompilerParams(collective_id=2, has_side_effects=True, vmem_limit_bytes=67043328),
         cost_estimate=pl.CostEstimate(flops=12 * rows * rows * d_model, bytes_accessed=64 * 1024 * 1024, transcendentals=0),
         name="middle",
-    )(y_seq.reshape(n_dev, piece, d_model), a_t, gy, w_out, q_rot, k_rot, v_val, q1, k1, cos_sin, lse, g_query[None], g_key[None])
+    )(a_seq.reshape(n_dev, piece, d_model), x_home, a_t, gy, w_out, q_rot, k_rot, v_val, q1, k1, cos_sin, lse, gains)
 
 
 N_SLOTS = 4
 
 
-def tail_kernel(n_dev, ht_ref, dy_v, dy_k, dy_q, w_v, w_k, w_q, x_ref, gy_ref, gn_ref, tq_ref, tk_ref,
+def tail_kernel(n_dev, ht_ref, htp_ref, dy_v, dy_k, dy_q, w_v, w_k, w_q, x_ref, gy_ref, gn_ref, tq_ref, tk_ref,
                 gw_v, gw_k, gw_q, gx_ref, gain_ref,
                 ht_own, ht_par, dy_own, dy_par, rs, dh, wbuf, xbuf, gybuf, n_acc, gsend, grecv,
                 load_sem, part_send, part_recv, rs_send, rs_recv, w_sem, xy_sem, gx_send, gx_recv, gx_loc,
@@ -518,8 +576,8 @@
     mine = pl.ds(pl.multiple_of(core * half, half), half)
     other = pl.ds(pl.multiple_of((1 - core) * half, half), half)
 
-    loads = [pltpu.make_async_copy(ht_ref, ht_own, load_sem.at[0])]
-    loads += [pltpu.make_async_copy(dys[i], dy_own.at[i], load_sem.at[1 + i]) for i in range(3)]
+    loads = [pltpu.make_async_copy(dys[i], dy_own.at[i], load_sem.at[i]) for i in range(3)]
+    loads[1:1] = [pltpu.make_async_copy(ht_ref, ht_own, load_sem.at[3]), pltpu.make_async_copy(htp_ref, ht_par, load_sem.at[4])]
     for cp in loads:
         cp.start()
 
@@ -532,8 +590,7 @@
         return pltpu.make_async_remote_copy(src_ref=src, dst_ref=dst, send_sem=part_send.at[idx], recv_sem=part_recv.at[idx],
                                             device_id={'sp': partner}, device_id_type=MESH)
 
-    parts = [to_partner(ht_ref, ht_par, 0)]
-    parts += [to_partner(dys[i].at[:, other], dy_par.at[i], 1 + i) for i in range(3)]
+    parts = [to_partner(dys[i].at[:, other], dy_par.at[i], i) for i in range(3)]
     for cp in parts:
         cp.start()
 
@@ -633,7 +690,7 @@
                 hat = x_f * inv
                 d_h = dh[rb, :].astype(jnp.float32)
                 n_acc[...] += jnp.sum(d_h * hat, axis=0, keepdims=True)
-                d_n = d_h * gn_ref[...].astype(jnp.float32)
+                d_n = d_h * gn_ref[0:1, :].astype(jnp.float32)
                 mean = jnp.mean(d_n * hat, axis=-1, keepdims=True)
                 out = gybuf[slot, ra, :].astype(jnp.float32) + inv * (d_n - hat * mean)
                 dh[rb, :] = out.astype(jnp.bfloat16)
@@ -663,11 +720,10 @@
                                            device_id={'sp': partner}, device_id_type=MESH)
         return loc, rem
 
-    for cp in loads:
+    for cp in loads[:3]:
         cp.wait()
     for i in range(3):
         w_copy(i, 0, 0).start()
-    parts[0].wait_recv()
     n_blocks = d_model // n_tile
     dh_from = 2
 
@@ -676,8 +732,12 @@
 
         @pl.when(s == 0)
         def _():
-            pltpu.make_async_remote_copy(src_ref=dy_v.at[:, other], dst_ref=dy_par.at[w], send_sem=part_send.at[1 + w], recv_sem=part_recv.at[1 + w],
+            pltpu.make_async_remote_copy(src_ref=dy_v.at[:, other], dst_ref=dy_par.at[w], send_sem=part_send.at[w], recv_sem=part_recv.at[w],
                                          device_id={'sp': partner}, device_id_type=MESH).wait_recv()
+
+        @pl.when(jnp.logical_and(s == 0, w > 0))
+        def _():
+            pltpu.make_async_copy(dy_v, dy_own.at[w], load_sem.at[w]).wait()
 
         @pl.when(s > 0)
         def _():
@@ -733,7 +793,7 @@
         rem.wait()
 
 
-def tail(n_dev, ht, dys, ws, x_bf, gy, g_norm, t_q, t_k):
+def tail(n_dev, ht, ht_par, dys, ws, x_bf, gy, gains, t_q, t_k):
     rows, d_model = x_bf.shape
     half, chunk, own_rows, piece = d_model // 2, d_model // (n_dev // 2), d_model // n_dev, rows // n_dev
     hbm = pl.BlockSpec(memory_space=pl.ANY)
@@ -744,7 +804,7 @@
     return pl.pallas_call(
         functools.partial(tail_kernel, n_dev),
         out_shape=(gw, gw, gw, jax.ShapeDtypeStruct((n_dev, piece, d_model), bf16), jax.ShapeDtypeStruct((8, own_rows), f32)),
-        in_specs=[hbm] * 9 + [vmem] * 3,
+        in_specs=[hbm] * 10 + [vmem] * 3,
         out_specs=(hbm,) * 4 + (vmem,),
         scratch_shapes=[
             pltpu.VMEM((d_model, rows), bf16), pltpu.VMEM((d_model, rows), bf16),
@@ -754,30 +814,27 @@
             pltpu.VMEM((2, 3, 256, d_model), bf16),
             pltpu.VMEM((2, piece, d_model), bf16), pltpu.VMEM((2, piece, d_model), bf16),
             pltpu.VMEM((1, d_model), f32), pltpu.VMEM((n_dev, 8, own_rows), f32), pltpu.VMEM((n_dev, 8, own_rows), f32),
-            dma((4,)), dma((4,)), dma((4,)), dma((3, 3)), dma((3, 3)), dma((2, 3)), dma((2, 2)),
+            dma((5,)), dma((3,)), dma((3,)), dma((3, 3)), dma((3, 3)), dma((2, 3)), dma((2, 2)),
             dma((n_dev,)), dma((n_dev,)), dma, dma((n_dev,)), dma((n_dev,)), dma((3,)), dma((3,)), dma((3,)),
         ],
         compiler_params=pltpu.CompilerParams(collective_id=0, has_side_effects=True, vmem_limit_bytes=67043328),
         cost_estimate=pl.CostEstimate(flops=12 * rows * d_model * d_model, bytes_accessed=64 * 1024 * 1024, transcendentals=0),
         name="tail",
-    )(ht, *dys, *ws, x_bf, gy, g_norm[None], t_q, t_k)
+    )(ht, ht_par, *dys, *ws, x_bf, gy, gains, t_q, t_k)
 
 
 def solution(mesh):
     n_dev = mesh.shape['sp']
-    exchange = functools.partial(lax.all_to_all, axis_name='sp', split_axis=0, concat_axis=0, tiled=True)
 
     def device_step(x_loc, gy_loc, pos_loc, g_norm, w_query, w_key, w_value, w_out, g_query, g_key):
         n_batch, loc_len, d_model = x_loc.shape
         rows = n_batch * loc_len
-        x_bf, cos_sin, q_rot, k_rot, v_val, h_t, q1, k1 = front(n_dev, x_loc, pos_loc, g_norm, g_query, g_key, w_query, w_key, w_value)
-        gy_late, q_rot = lax.optimization_barrier((gy_loc, q_rot))
-        gy = exchange(gy_late).reshape(rows, d_model)
-        attended, a_t, lse = attend_forward(q_rot, k_rot, v_val)
-        y_seq = (x_bf.astype(jnp.float32) + dot_nn(attended, w_out)).astype(jnp.bfloat16)
-        y_out, grad_wo, dq_bf, dk_bf, d_v, t_q, t_k = middle(n_dev, y_seq, a_t, gy, w_out, q_rot, k_rot, v_val, q1, k1, cos_sin, lse, g_query, g_key)
-        grad_wv, grad_wk, grad_wq, grad_x, gains = tail(n_dev, h_t, (d_v, dk_bf, dq_bf), (w_value, w_key, w_query), x_bf, gy, g_norm, t_q, t_k)
-        return y_out, grad_x, gains[0], grad_wq, grad_wk, grad_wv, grad_wo, gains[1], gains[2]
+        gains = jnp.stack([g_norm, g_query, g_key])
+        x_bf, gy, cos_sin, q_rot, k_rot, v_val, h_t, h_t_par, q1, k1, attended, a_t, lse = front(n_dev, x_loc, gy_loc, pos_loc, gains, w_query, w_key, w_value)
+        gy = gy.reshape(rows, d_model)
+        y_out, _, grad_wo, dq_bf, dk_bf, d_v, t_q, t_k = middle(n_dev, attended, x_loc, a_t, gy, w_out, q_rot, k_rot, v_val, q1, k1, cos_sin, lse, gains)
+        grad_wv, grad_wk, grad_wq, grad_x, sums = tail(n_dev, h_t, h_t_par, (d_v, dk_bf, dq_bf), (w_value, w_key, w_query), x_bf, gy, gains, t_q, t_k)
+        return y_out, grad_x, sums[0], grad_wq, grad_wk, grad_wv, grad_wo, sums[1], sums[2]
 
     seq_spec = P('dp', 'sp', None)
     mat_rep = P(None, None)

time: 540 us -> 526 us (0.974)
  matrix products: 14.5 us -> 0 us
  Pallas kernels: 492 us -> 501 us
    pallas_call x1, Pallas kernels: 65.1 us -> 100 us  [front(): pl.pallas_call(functools.partial(front_kernel, n_dev), out_shape=(act, ja...]
    pallas_call x1 -> x0, Pallas kernels: 30.9 us -> none  [attend_forward(): pl.pallas_call(functools.partial(attn_fwd_kernel, seq_len), grid=(n_heads...]
    dot_general x1 -> x0, matrix products: 14.5 us -> none  [dot_nn(): lax.dot_general(a, b, (((1,), (0,)), ((), ())), preferred_element_type=jn...]
    pallas_call x1, Pallas kernels: 123 us -> 133 us  [middle(): pl.pallas_call(functools.partial(middle_kernel, n_dev), out_shape=(jax.Sh...]
  transfers between devices with their start and end apart: 1 -> 0, of which waited for: 1 -> 0; matrix products, arithmetic and copies ran while one was open for 3% -> 0% of each run, Pallas kernels for 6% -> 0%
where the time goes in v5:
time: 526 us; the launch traced here: 524 us
  Pallas kernels  501 us (95%)
  local copies, waits for them, and re-layouts  17.8 us (3%)
    pallas_call x1, Pallas kernels, tail(): pl.pallas_call(functools.partial(tail_kernel, n_dev), out_shape=(gw, gw,...  268 us
    pallas_call x1, Pallas kernels, middle(): pl.pallas_call(functools.partial(middle_kernel, n_dev), out_shape=(jax.Sh...  133 us
    pallas_call x1, Pallas kernels, front(): pl.pallas_call(functools.partial(front_kernel, n_dev), out_shape=(act, ja...  100 us
    unnamed x16, local copies, waits for them, and re-layouts  14.4 us

profile of v5, /device:TPU:113, one launch (start us, length us, event | category | flops | bytes accessed | tf_op | source)
XLA Modules:
  0.0 524.2 jit_solution(8272334478072760408)
XLA Ops:
  0.7 0.7 stack.19
  1.4 0.7 stack.20
  2.0 0.7 stack.21
  2.7 0.6 pad_maximum_fusion.2.g_ref.gn_ref
  3.4 2.0 cosine_bitcast_fusion
  5.3 0.5 reduce-precision_convert_fusion.1
  5.8 1.3 pad_maximum_fusion.tab_ref
  7.2 100.3 %front.1 = (bf16[1024,2048]{1,0:T(8,128)(2,1)}, bf16[8,128,2048]{2,1,0:T(8,128)(2,1)}, f32[1024,256]{1,0:T(8,128)}, bf16[1024,2048]{1,0:T(8,128)(2,1)}, bf16[102...) custom-call(bf16[8,128,2048]{2,1,0:T(8,128)(2,1)} %x_home.1, ...), custom_call_target="tpu_custom_call" | custom-call | flops 25769803776 | bytes 62914560 | tf_op jit(solution)/shard_map/front/pallas_call | solution.py:243
  107.5 132.8 %middle.1 = (bf16[8,128,2048]{2,1,0:T(8,128)(2,1)}, bf16[8,128,2048]{2,1,0:T(8,128)(2,1)}, f32[256,2048]{1,0:T(8,128)}, bf16[1024,2048]{1,0:T(8,128)(2,1)}, bf16...) custom-call(bf16[8,128,2048]{2,1,0:T(8,128)(2,1)} %bitcast.18, ...), custom_call_target="tpu_custom_call" | custom-call | flops 25769803776 | bytes 67108864 | tf_op jit(solution)/shard_map/middle/pallas_call | solution.py:534
  240.3 268.1 %tail.1 = (f32[256,2048]{1,0:T(8,128)}, f32[256,2048]{1,0:T(8,128)}, f32[256,2048]{1,0:T(8,128)}, bf16[8,128,2048]{2,1,0:T(8,128)(2,1)}, f32[8,256]{1,0:T(8,128)}) custom-call(bf16[2048,1024]{1,0:T(8,128)(2,1)} %get-tuple-element.45.ht_ref, bf16[2048,1024]{1,0:T(8,128)(2,1)} %get-tuple-element.46.htp_ref, bf16[1024,2048]{1,0:T(8,128)(2,1)} %get-tuple-element.47.dy_v, ...), custom_call_target="tpu_custom_call" | custom-call | flops 51539607552 | bytes 67108864 | tf_op jit(solution)/shard_map/tail/pallas_call | solution.py:804
  508.5 1.4 fusion.4
  509.9 0.0 copy-start
  509.9 4.9 copy.25
  514.8 0.0 copy-done
  514.8 0.0 copy-start.4
  514.8 2.1 copy.26
  516.9 1.0 copy-done.4
  517.9 0.0 copy-start.3
  517.9 0.0 copy-start.2
  517.9 1.3 copy.27
  519.2 1.0 copy-done.3
  520.3 0.0 copy-start.1
  520.3 1.3 copy.28
  521.6 0.0 copy-done.2
  521.6 1.3 copy.29
  522.9 0.0 copy-done.1
  522.9 1.3 copy.30
  (1 shorter events, 0.0 us)
Async XLA Ops:
  509.9 4.9 copy-start
  514.8 3.1 copy-start.4
  517.9 2.3 copy-start.3
  517.9 3.7 copy-start.2
  520.3 2.6 copy-start.1

commit v6 on v5

--- a/solution.py
+++ b/solution.py
@@ -2,6 +2,7 @@
 import math
 import jax
 import jax.numpy as jnp
+import numpy as np
 from jax import lax
 from jax.experimental import pallas as pl
 from jax.experimental.pallas import tpu as pltpu
@@ -17,16 +18,15 @@
 
 def rope_table(n_pos):
     half_dim = HEAD_DIM // 2
-    inv_freq = ROPE_BASE ** (-jnp.arange(half_dim, dtype=jnp.float32) * (2.0 / HEAD_DIM))
-    angles = jnp.arange(n_pos, dtype=jnp.float32)[:, None] * inv_freq
-    cos_h, sin_h = jnp.cos(angles), jnp.sin(angles)
-    table = jnp.concatenate([cos_h, cos_h, -sin_h, sin_h], axis=1)
+    inv_freq = (ROPE_BASE ** (-np.arange(half_dim) * (2.0 / HEAD_DIM))).astype(np.float32)
+    angles = (np.arange(n_pos, dtype=np.float32)[:, None] * inv_freq).astype(np.float64)
+    rest = np.concatenate([np.cos(angles), np.sin(angles)], axis=1).astype(np.float32)
     parts = []
     for _ in range(3):
-        part = lax.reduce_precision(table, 8, 7)
-        parts.append(part.astype(jnp.bfloat16))
-        table = table - part
-    return jnp.stack(parts)
+        part = rest.astype(jnp.bfloat16)
+        parts.append(part)
+        rest = rest - part.astype(np.float32)
+    return jnp.asarray(np.stack(parts))
 
 
 def dot_nn(a, b):
@@ -163,7 +163,11 @@
 
         for e in range(2):
             hot = (lax.broadcasted_iota(jnp.int32, (n_pos, piece), 0) == posv[2 * src_chip + e]).astype(jnp.bfloat16)
-            csb[slot, e * piece:(e + 1) * piece, :] = (dot_tn(hot, tab_ref[0]) + dot_tn(hot, tab_ref[1])) + dot_tn(hot, tab_ref[2])
+            table = (dot_tn(hot, tab_ref[0]) + dot_tn(hot, tab_ref[1])) + dot_tn(hot, tab_ref[2])
+            swapped = pltpu.roll(table, HEAD_DIM // 2, 1)
+            low = lax.broadcasted_iota(jnp.int32, table.shape, 1) < HEAD_DIM // 2
+            csb[slot, e * piece:(e + 1) * piece, 0:HEAD_DIM] = jnp.where(low, table, swapped)
+            csb[slot, e * piece:(e + 1) * piece, HEAD_DIM:2 * HEAD_DIM] = jnp.where(low, -swapped, table)
         x_f = xv[pl.ds(at, blk), :].astype(jnp.float32)
         hidden = (x_f * row_inv(x_f) * g_ref[0:1, :].astype(jnp.float32)).astype(jnp.bfloat16)
         htb[slot] = hidden.T
@@ -414,11 +418,11 @@
         dvb[slot] = dv_acc[...].astype(jnp.bfloat16)
         dv_copy(h, slot).start()
 
-        ring_from = n_heads - 6
-
-        @pl.when(jnp.logical_and(h >= ring_from, lax.rem(h - ring_from, 2) == 1))
-        def _():
-            ring(2 + (h - ring_from) // 2)
+        ring_from = n_heads - 5
+
+        @pl.when(jnp.logical_or(h == ring_from, h == ring_from + 3))
+        def _():
+            ring(2 + (h - ring_from) // 3)
 
         return carry
 
@@ -438,17 +442,18 @@
     y_own.wait()
 
     def home_in(b, slot):
-        return (pltpu.make_async_copy(a_home.at[b], ahb.at[slot], ax_sem.at[slot, 0]), pltpu.make_async_copy(x_home.at[b], xhb.at[slot], ax_sem.at[slot, 1]))
+        two = pl.ds(2 * b, 2)
+        return (pltpu.make_async_copy(a_home.at[two], ahb.at[slot], ax_sem.at[slot, 0]), pltpu.make_async_copy(x_home.at[two], xhb.at[slot], ax_sem.at[slot, 1]))
 
     def y_copy(b, slot):
-        return pltpu.make_async_copy(yb.at[slot], y_out.at[b], yo_sem.at[slot])
+        return pltpu.make_async_copy(yb.at[slot], y_out.at[pl.ds(2 * b, 2)], yo_sem.at[slot])
 
     def y_rows(b, carry):
         slot = lax.rem(b, 2)
         for cp in home_in(b, slot):
             cp.wait()
 
-        @pl.when(b + 1 < n_dev)
+        @pl.when(b + 1 < n_chips)
         def _():
             for cp in home_in(b + 1, 1 - slot):
                 cp.start()
@@ -457,7 +462,8 @@
         def _():
             y_copy(b, slot).wait()
 
-        yb[slot] = (xhb[slot].astype(jnp.float32) + dot_nn(ahb[slot], wo[...])).astype(jnp.bfloat16)
+        o_proj = dot_nn(ahb[slot].reshape(2 * piece, d_model), wo[...])
+        yb[slot] = (xhb[slot].astype(jnp.float32) + o_proj.reshape(2, piece, d_model)).astype(jnp.bfloat16)
         y_copy(b, slot).start()
         return carry
 
@@ -465,6 +471,8 @@
         src = (q1_ref, k1_ref)[i]
         return pltpu.make_async_copy(src.at[pl.ds(pl.multiple_of(b * piece, piece), piece), :], rawb.at[slot], raw_sem.at[slot])
 
+    for cp in home_in(0, 0):
+        cp.start()
     for i, t_ref in ((0, tq_ref), (1, tk_ref)):
         t_ref[...] = jnp.zeros_like(t_ref)
         raw_copy(i, 0, 0).start()
@@ -498,10 +506,10 @@
         lax.fori_loop(0, n_dev, norm_rows, 0)
         pltpu.make_async_copy(dqk.at[i], (dq_ref, dk_ref)[i], dqk_sem.at[i]).start()
         if i == 0:
+            ring(jnp.int32(4))
+            lax.fori_loop(0, n_chips // 2, y_rows, 0)
             ring(jnp.int32(5))
-            for cp in home_in(0, 0):
-                cp.start()
-            lax.fori_loop(0, n_dev, y_rows, 0)
+            lax.fori_loop(n_chips // 2, n_chips, y_rows, 0)
 
     for ch in range(2):
         ring(jnp.int32(6 + ch))
@@ -543,7 +551,7 @@
             pltpu.VMEM((2, 3, rows, HEAD_DIM), bf16), pltpu.VMEM((2, rows, HEAD_DIM), bf16), pltpu.VMEM((rows, 2 * HEAD_DIM), bf16),
             pltpu.VMEM((rows, HEAD_DIM), f32), pltpu.VMEM((rows, HEAD_DIM), f32),
             pltpu.VMEM((2, piece, d_model), f32), pltpu.VMEM((piece, d_model), f32), pltpu.VMEM((piece, d_model), f32),
-            pltpu.VMEM((2, piece, d_model), bf16), pltpu.VMEM((2, piece, d_model), bf16), pltpu.VMEM((2, piece, d_model), bf16),
+            pltpu.VMEM((2, 2, piece, d_model), bf16), pltpu.VMEM((2, 2, piece, d_model), bf16), pltpu.VMEM((2, 2, piece, d_model), bf16),
             dma((3,)), dma((n_dev,)), dma((n_dev,)), dma, dma((2,)), dma((2,)), dma((2, 3)), dma((2, 3)), dma((2, 3)), dma((2,)), dma((2,)), dma((2,)),
             dma((2,)), dma((2,)), dma((2,)), dma((2, 2)), dma((2,)),
         ],

time: 526 us -> 519 us (0.987)
  no operation moved by 1% of the time
where the time goes in v6:
time: 519 us; the launch traced here: 518 us
  Pallas kernels  499 us (96%)
  local copies, waits for them, and re-layouts  17.8 us (3%)
    pallas_call x1, Pallas kernels, tail(): pl.pallas_call(functools.partial(tail_kernel, n_dev), out_shape=(gw, gw,...  268 us
    pallas_call x1, Pallas kernels, middle(): pl.pallas_call(functools.partial(middle_kernel, n_dev), out_shape=(jax.Sh...  130 us
    pallas_call x1, Pallas kernels, front(): pl.pallas_call(functools.partial(front_kernel, n_dev), out_shape=(act, ja...  100 us
    unnamed x16, local copies, waits for them, and re-layouts  14.4 us

profile of v6, /device:TPU:113, one launch (start us, length us, event | category | flops | bytes accessed | tf_op | source)
XLA Modules:
  0.0 518.0 jit_solution(11662061046146471692)
XLA Ops:
  0.6 0.7 stack.12
  1.3 0.7 stack.13
  2.0 0.7 stack.14
  2.7 0.6 pad_maximum_fusion.g_ref.gn_ref
  3.4 100.4 %front.1 = (bf16[1024,2048]{1,0:T(8,128)(2,1)}, bf16[8,128,2048]{2,1,0:T(8,128)(2,1)}, f32[1024,256]{1,0:T(8,128)}, bf16[1024,2048]{1,0:T(8,128)(2,1)}, bf16[102...) custom-call(bf16[8,128,2048]{2,1,0:T(8,128)(2,1)} %x_home.1, ...), custom_call_target="tpu_custom_call" | custom-call | flops 25769803776 | bytes 62914560 | tf_op jit(solution)/shard_map/front/pallas_call | solution.py:247
  103.8 130.1 %middle.1 = (bf16[8,128,2048]{2,1,0:T(8,128)(2,1)}, bf16[8,128,2048]{2,1,0:T(8,128)(2,1)}, f32[256,2048]{1,0:T(8,128)}, bf16[1024,2048]{1,0:T(8,128)(2,1)}, bf16...) custom-call(bf16[8,128,2048]{2,1,0:T(8,128)(2,1)} %bitcast.12, ...), custom_call_target="tpu_custom_call" | custom-call | flops 25769803776 | bytes 67108864 | tf_op jit(solution)/shard_map/middle/pallas_call | solution.py:542
  233.9 268.3 %tail.1 = (f32[256,2048]{1,0:T(8,128)}, f32[256,2048]{1,0:T(8,128)}, f32[256,2048]{1,0:T(8,128)}, bf16[8,128,2048]{2,1,0:T(8,128)(2,1)}, f32[8,256]{1,0:T(8,128)}) custom-call(bf16[2048,1024]{1,0:T(8,128)(2,1)} %get-tuple-element.45.ht_ref, bf16[2048,1024]{1,0:T(8,128)(2,1)} %get-tuple-element.46.htp_ref, bf16[1024,2048]{1,0:T(8,128)(2,1)} %get-tuple-element.47.dy_v, ...), custom_call_target="tpu_custom_call" | custom-call | flops 51539607552 | bytes 67108864 | tf_op jit(solution)/shard_map/tail/pallas_call | solution.py:812
  502.2 1.4 fusion
  503.6 0.0 copy-start
  503.6 4.9 copy.26
  508.5 0.0 copy-done
  508.6 0.0 copy-start.4
  508.6 2.1 copy.27
  510.7 1.0 copy-done.4
  511.7 0.0 copy-start.3
  511.7 0.0 copy-start.2
  511.7 1.3 copy.28
  513.0 1.0 copy-done.3
  514.0 0.0 copy-start.1
  514.0 1.3 copy.29
  515.3 0.0 copy-done.2
  515.3 1.3 copy.30
  516.6 0.0 copy-done.1
  516.7 1.3 copy.31
Async XLA Ops:
  503.6 4.9 copy-start
  508.6 3.1 copy-start.4
  511.7 2.3 copy-start.3
  511.7 3.7 copy-start.2
  514.0 2.6 copy-start.1

commit v7 on v6

--- a/solution.py
+++ b/solution.py
@@ -263,11 +263,11 @@
     )(x_loc, gy_loc, pos_loc[:, None, :], rope_table(rows), gains, w_query, w_key, w_value)
 
 
-def middle_kernel(n_dev, a_seq, x_home, at_ref, gy_ref, wo_ref, q_ref, k_ref, v_ref, q1_ref, k1_ref, cs_ref, lse_ref, g_ref,
-                  y_out, a_home, gw_ref, dq_ref, dk_ref, dv_ref, tq_ref, tk_ref,
-                  wo, at_own, at_par, gy_own, gy_par, rs, dqk, hbuf, dvb, dob, dk_acc, dv_acc, rawb, tmp, nrm, ahb, xhb, yb,
+def middle_kernel(n_dev, a_seq, at_ref, gy_ref, wo_ref, q_ref, k_ref, v_ref, q1_ref, k1_ref, cs_ref, lse_ref, g_ref,
+                  a_home, gw_ref, dq_ref, dk_ref, dv_ref, tq_ref, tk_ref,
+                  wo, at_own, at_par, gy_own, gy_par, rs, dqk, hbuf, dvb, dob, dk_acc, dv_acc, rawb, tmp, nrm,
                   load_sem, y_send, y_recv, y_loc, part_send, part_recv, rs_send, rs_recv, h_sem, dv_sem, raw_sem, dqk_sem,
-                  fin_loc, fin_send, fin_recv, ax_sem, yo_sem):
+                  fin_loc, fin_send, fin_recv):
     me = lax.axis_index('sp')
     chip, core = me // 2, me % 2
     n_chips = n_dev // 2
@@ -437,42 +437,10 @@
     for slot in range(2):
         dv_copy(0, slot).wait()
 
-    for off in range(1, n_dev):
-        y_remote(off).wait()
-    y_own.wait()
-
-    def home_in(b, slot):
-        two = pl.ds(2 * b, 2)
-        return (pltpu.make_async_copy(a_home.at[two], ahb.at[slot], ax_sem.at[slot, 0]), pltpu.make_async_copy(x_home.at[two], xhb.at[slot], ax_sem.at[slot, 1]))
-
-    def y_copy(b, slot):
-        return pltpu.make_async_copy(yb.at[slot], y_out.at[pl.ds(2 * b, 2)], yo_sem.at[slot])
-
-    def y_rows(b, carry):
-        slot = lax.rem(b, 2)
-        for cp in home_in(b, slot):
-            cp.wait()
-
-        @pl.when(b + 1 < n_chips)
-        def _():
-            for cp in home_in(b + 1, 1 - slot):
-                cp.start()
-
-        @pl.when(b >= 2)
-        def _():
-            y_copy(b, slot).wait()
-
-        o_proj = dot_nn(ahb[slot].reshape(2 * piece, d_model), wo[...])
-        yb[slot] = (xhb[slot].astype(jnp.float32) + o_proj.reshape(2, piece, d_model)).astype(jnp.bfloat16)
-        y_copy(b, slot).start()
-        return carry
-
     def raw_copy(i, b, slot):
         src = (q1_ref, k1_ref)[i]
         return pltpu.make_async_copy(src.at[pl.ds(pl.multiple_of(b * piece, piece), piece), :], rawb.at[slot], raw_sem.at[slot])
 
-    for cp in home_in(0, 0):
-        cp.start()
     for i, t_ref in ((0, tq_ref), (1, tk_ref)):
         t_ref[...] = jnp.zeros_like(t_ref)
         raw_copy(i, 0, 0).start()
@@ -507,21 +475,20 @@
         pltpu.make_async_copy(dqk.at[i], (dq_ref, dk_ref)[i], dqk_sem.at[i]).start()
         if i == 0:
             ring(jnp.int32(4))
-            lax.fori_loop(0, n_chips // 2, y_rows, 0)
             ring(jnp.int32(5))
-            lax.fori_loop(n_chips // 2, n_chips, y_rows, 0)
 
     for ch in range(2):
         ring(jnp.int32(6 + ch))
         for cp in finish_out(ch):
             cp.start()
-    for slot in range(2):
-        y_copy(0, slot).wait()
     for cp in parts:
         cp.wait_send()
     for ch in range(2):
         for s in range(N_SLOTS - 1):
             rs_copy(ch, s).wait_send()
+    for off in range(1, n_dev):
+        y_remote(off).wait()
+    y_own.wait()
     for i in range(2):
         pltpu.make_async_copy(dqk.at[i], (dq_ref, dk_ref)[i], dqk_sem.at[i]).wait()
     for ch in range(2):
@@ -530,7 +497,7 @@
         rem.wait()
 
 
-def middle(n_dev, a_seq, x_home, a_t, gy, w_out, q_rot, k_rot, v_val, q1, k1, cos_sin, lse, gains):
+def middle(n_dev, a_seq, a_t, gy, w_out, q_rot, k_rot, v_val, q1, k1, cos_sin, lse, gains):
     rows, d_model = gy.shape
     piece, chunk, own_rows, sub = rows // n_dev, d_model // (n_dev // 2), d_model // n_dev, d_model // 4
     hbm = pl.BlockSpec(memory_space=pl.ANY)
@@ -541,9 +508,9 @@
     dma = pltpu.SemaphoreType.DMA
     return pl.pallas_call(
         functools.partial(middle_kernel, n_dev),
-        out_shape=(jax.ShapeDtypeStruct((n_dev, piece, d_model), bf16), jax.ShapeDtypeStruct((n_dev, piece, d_model), bf16), jax.ShapeDtypeStruct((own_rows, d_model), f32), act, act, act, vec, vec),
-        in_specs=[hbm] * 10 + [vmem] * 3,
-        out_specs=(hbm,) * 6 + (vmem,) * 2,
+        out_shape=(jax.ShapeDtypeStruct((n_dev, piece, d_model), bf16), jax.ShapeDtypeStruct((own_rows, d_model), f32), act, act, act, vec, vec),
+        in_specs=[hbm] * 9 + [vmem] * 3,
+        out_specs=(hbm,) * 5 + (vmem,) * 2,
         scratch_shapes=[
             pltpu.VMEM((d_model, d_model), bf16), pltpu.VMEM((d_model, rows), bf16), pltpu.VMEM((d_model, rows), bf16),
             pltpu.VMEM((rows, d_model), bf16), pltpu.VMEM((rows, d_model // 2), bf16),
@@ -551,24 +518,23 @@
             pltpu.VMEM((2, 3, rows, HEAD_DIM), bf16), pltpu.VMEM((2, rows, HEAD_DIM), bf16), pltpu.VMEM((rows, 2 * HEAD_DIM), bf16),
             pltpu.VMEM((rows, HEAD_DIM), f32), pltpu.VMEM((rows, HEAD_DIM), f32),
             pltpu.VMEM((2, piece, d_model), f32), pltpu.VMEM((piece, d_model), f32), pltpu.VMEM((piece, d_model), f32),
-            pltpu.VMEM((2, 2, piece, d_model), bf16), pltpu.VMEM((2, 2, piece, d_model), bf16), pltpu.VMEM((2, 2, piece, d_model), bf16),
             dma((3,)), dma((n_dev,)), dma((n_dev,)), dma, dma((2,)), dma((2,)), dma((2, 3)), dma((2, 3)), dma((2, 3)), dma((2,)), dma((2,)), dma((2,)),
-            dma((2,)), dma((2,)), dma((2,)), dma((2, 2)), dma((2,)),
+            dma((2,)), dma((2,)), dma((2,)),
         ],
         compiler_params=pltpu.CompilerParams(collective_id=2, has_side_effects=True, vmem_limit_bytes=67043328),
         cost_estimate=pl.CostEstimate(flops=12 * rows * rows * d_model, bytes_accessed=64 * 1024 * 1024, transcendentals=0),
         name="middle",
-    )(a_seq.reshape(n_dev, piece, d_model), x_home, a_t, gy, w_out, q_rot, k_rot, v_val, q1, k1, cos_sin, lse, gains)
+    )(a_seq.reshape(n_dev, piece, d_model), a_t, gy, w_out, q_rot, k_rot, v_val, q1, k1, cos_sin, lse, gains)
 
 
 N_SLOTS = 4
 
 
-def tail_kernel(n_dev, ht_ref, htp_ref, dy_v, dy_k, dy_q, w_v, w_k, w_q, x_ref, gy_ref, gn_ref, tq_ref, tk_ref,
-                gw_v, gw_k, gw_q, gx_ref, gain_ref,
-                ht_own, ht_par, dy_own, dy_par, rs, dh, wbuf, xbuf, gybuf, n_acc, gsend, grecv,
+def tail_kernel(n_dev, ht_ref, htp_ref, dy_v, dy_k, dy_q, w_v, w_k, w_q, x_ref, gy_ref, ah_ref, xh_ref, wo_ref, gn_ref, tq_ref, tk_ref,
+                gw_v, gw_k, gw_q, gx_ref, y_ref, gain_ref,
+                ht_own, ht_par, dy_own, dy_par, rs, dh, wbuf, xbuf, gybuf, n_acc, gsend, grecv, wob, xhb, yhb,
                 load_sem, part_send, part_recv, rs_send, rs_recv, w_sem, xy_sem, gx_send, gx_recv, gx_loc,
-                gain_send, gain_recv, fin_loc, fin_send, fin_recv):
+                gain_send, gain_recv, fin_loc, fin_send, fin_recv, home_sem):
     me = lax.axis_index('sp')
     chip, core = me // 2, me % 2
     n_chips = n_dev // 2
@@ -585,6 +551,7 @@
     other = pl.ds(pl.multiple_of((1 - core) * half, half), half)
 
     loads = [pltpu.make_async_copy(dys[i], dy_own.at[i], load_sem.at[i]) for i in range(3)]
+    a_load = pltpu.make_async_copy(ah_ref, dh, home_sem.at[0])
     loads[1:1] = [pltpu.make_async_copy(ht_ref, ht_own, load_sem.at[3]), pltpu.make_async_copy(htp_ref, ht_par, load_sem.at[4])]
     for cp in loads:
         cp.start()
@@ -599,7 +566,7 @@
                                             device_id={'sp': partner}, device_id_type=MESH)
 
     parts = [to_partner(dys[i].at[:, other], dy_par.at[i], i) for i in range(3)]
-    for cp in parts:
+    for cp in parts + [a_load]:
         cp.start()
 
     def rs_copy(w, s):
@@ -629,28 +596,41 @@
 
         lax.fori_loop(0, half // n_tile, tile, 0)
 
-    def w_copy(i, n, slot):
-        return pltpu.make_async_copy(ws[i].at[pl.ds(pl.multiple_of(n * n_tile, n_tile), n_tile), :], wbuf.at[slot, i], w_sem.at[slot, i])
-
     def dh_block(n):
-        slot = lax.rem(n, 2)
-        for i in range(3):
-            w_copy(i, n, slot).wait()
-
-        @pl.when(n + 1 < d_model // n_tile)
-        def _():
-            for i in range(3):
-                w_copy(i, n + 1, 1 - slot).start()
+        w_copies = [pltpu.make_async_copy(ws[i].at[pl.ds(pl.multiple_of(n * n_tile, n_tile), n_tile), :], wbuf.at[i], w_sem.at[i]) for i in range(3)]
+        for cp in w_copies:
+            cp.start()
+        for cp in w_copies:
+            cp.wait()
 
         m_tile = 256
 
         def tile(t, carry):
             at = pl.ds(pl.multiple_of(t * m_tile, m_tile), m_tile)
-            total = dot_nt(dy_own[0, at, :], wbuf[slot, 0]) + dot_nt(dy_own[1, at, :], wbuf[slot, 1]) + dot_nt(dy_own[2, at, :], wbuf[slot, 2])
+            total = dot_nt(dy_own[0, at, :], wbuf[0]) + dot_nt(dy_own[1, at, :], wbuf[1]) + dot_nt(dy_own[2, at, :], wbuf[2])
             dh[at, pl.ds(pl.multiple_of(n * n_tile, n_tile), n_tile)] = total.astype(jnp.bfloat16)
             return carry
 
         lax.fori_loop(0, rows // m_tile, tile, 0)
+
+    def y_block(n, carry):
+        cols = pl.ds(pl.multiple_of(n * n_tile, n_tile), n_tile)
+        ins = [pltpu.make_async_copy(wo_ref.at[:, cols], wob, home_sem.at[1]), pltpu.make_async_copy(xh_ref.at[:, cols], xhb, home_sem.at[2])]
+        for cp in ins:
+            cp.start()
+        for cp in ins:
+            cp.wait()
+
+        def tile(t, c2):
+            at = pl.ds(pl.multiple_of(t * 256, 256), 256)
+            yhb[at, :] = (xhb[at, :].astype(jnp.float32) + dot_nn(dh[at, :], wob[...])).astype(jnp.bfloat16)
+            return c2
+
+        lax.fori_loop(0, rows // 256, tile, 0)
+        out = pltpu.make_async_copy(yhb, y_ref.at[:, cols], home_sem.at[3])
+        out.start()
+        out.wait()
+        return carry
 
     def xy_copies(p, slot):
         at = pl.ds(pl.multiple_of(p * piece, piece), piece)
@@ -730,10 +710,8 @@
 
     for cp in loads[:3]:
         cp.wait()
-    for i in range(3):
-        w_copy(i, 0, 0).start()
     n_blocks = d_model // n_tile
-    dh_from = 2
+    dh_from = 3
 
     def main(it, carry):
         s, w = it // 3, lax.rem(it, 3)
@@ -756,6 +734,15 @@
         @pl.when(s < N_SLOTS - 1)
         def _():
             rs_copy(w, s).start()
+
+        @pl.when(it == 1)
+        def _():
+            a_load.wait()
+            lax.fori_loop(0, n_blocks // 2, y_block, 0)
+
+        @pl.when(it == 2)
+        def _():
+            lax.fori_loop(n_blocks // 2, n_blocks, y_block, 0)
 
         for j in range(2):
             blk_i = 2 * (it - dh_from) + j
@@ -801,7 +788,7 @@
         rem.wait()
 
 
-def tail(n_dev, ht, ht_par, dys, ws, x_bf, gy, gains, t_q, t_k):
+def tail(n_dev, ht, ht_par, dys, ws, x_bf, gy, a_home, x_home, w_out, gains, t_q, t_k):
     rows, d_model = x_bf.shape
     half, chunk, own_rows, piece = d_model // 2, d_model // (n_dev // 2), d_model // n_dev, rows // n_dev
     hbm = pl.BlockSpec(memory_space=pl.ANY)
@@ -811,24 +798,25 @@
     dma = pltpu.SemaphoreType.DMA
     return pl.pallas_call(
         functools.partial(tail_kernel, n_dev),
-        out_shape=(gw, gw, gw, jax.ShapeDtypeStruct((n_dev, piece, d_model), bf16), jax.ShapeDtypeStruct((8, own_rows), f32)),
-        in_specs=[hbm] * 10 + [vmem] * 3,
-        out_specs=(hbm,) * 4 + (vmem,),
+        out_shape=(gw, gw, gw, jax.ShapeDtypeStruct((n_dev, piece, d_model), bf16), jax.ShapeDtypeStruct((rows, d_model), bf16), jax.ShapeDtypeStruct((8, own_rows), f32)),
+        in_specs=[hbm] * 13 + [vmem] * 3,
+        out_specs=(hbm,) * 5 + (vmem,),
         scratch_shapes=[
             pltpu.VMEM((d_model, rows), bf16), pltpu.VMEM((d_model, rows), bf16),
             pltpu.VMEM((3, rows, d_model), bf16), pltpu.VMEM((3, rows, half), bf16),
             pltpu.VMEM((3, N_SLOTS, chunk, half), f32),
             pltpu.VMEM((rows, d_model), bf16),
-            pltpu.VMEM((2, 3, 256, d_model), bf16),
+            pltpu.VMEM((3, 256, d_model), bf16),
             pltpu.VMEM((2, piece, d_model), bf16), pltpu.VMEM((2, piece, d_model), bf16),
             pltpu.VMEM((1, d_model), f32), pltpu.VMEM((n_dev, 8, own_rows), f32), pltpu.VMEM((n_dev, 8, own_rows), f32),
-            dma((5,)), dma((3,)), dma((3,)), dma((3, 3)), dma((3, 3)), dma((2, 3)), dma((2, 2)),
-            dma((n_dev,)), dma((n_dev,)), dma, dma((n_dev,)), dma((n_dev,)), dma((3,)), dma((3,)), dma((3,)),
+            pltpu.VMEM((d_model, 256), bf16), pltpu.VMEM((rows, 256), bf16), pltpu.VMEM((rows, 256), bf16),
+            dma((5,)), dma((3,)), dma((3,)), dma((3, 3)), dma((3, 3)), dma((3,)), dma((2, 2)),
+            dma((n_dev,)), dma((n_dev,)), dma, dma((n_dev,)), dma((n_dev,)), dma((3,)), dma((3,)), dma((3,)), dma((4,)),
         ],
         compiler_params=pltpu.CompilerParams(collective_id=0, has_side_effects=True, vmem_limit_bytes=67043328),
         cost_estimate=pl.CostEstimate(flops=12 * rows * d_model * d_model, bytes_accessed=64 * 1024 * 1024, transcendentals=0),
         name="tail",
-    )(ht, ht_par, *dys, *ws, x_bf, gy, gains, t_q, t_k)
+    )(ht, ht_par, *dys, *ws, x_bf, gy, a_home, x_home, w_out, gains, t_q, t_k)
 
 
 def solution(mesh):
@@ -840,8 +828,10 @@
         gains = jnp.stack([g_norm, g_query, g_key])
         x_bf, gy, cos_sin, q_rot, k_rot, v_val, h_t, h_t_par, q1, k1, attended, a_t, lse = front(n_dev, x_loc, gy_loc, pos_loc, gains, w_query, w_key, w_value)
         gy = gy.reshape(rows, d_model)
-        y_out, _, grad_wo, dq_bf, dk_bf, d_v, t_q, t_k = middle(n_dev, attended, x_loc, a_t, gy, w_out, q_rot, k_rot, v_val, q1, k1, cos_sin, lse, gains)
-        grad_wv, grad_wk, grad_wq, grad_x, sums = tail(n_dev, h_t, h_t_par, (d_v, dk_bf, dq_bf), (w_value, w_key, w_query), x_bf, gy, gains, t_q, t_k)
+        a_home, grad_wo, dq_bf, dk_bf, d_v, t_q, t_k = middle(n_dev, attended, a_t, gy, w_out, q_rot, k_rot, v_val, q1, k1, cos_sin, lse, gains)
+        grad_wv, grad_wk, grad_wq, grad_x, y_out, sums = tail(n_dev, h_t, h_t_par, (d_v, dk_bf, dq_bf), (w_value, w_key, w_query), x_bf, gy,
+                                                              a_home.reshape(rows, d_model), x_loc.reshape(rows, d_model), w_out, gains, t_q, t_k)
+        y_out = y_out.reshape(n_batch, loc_len, d_model)
         return y_out, grad_x, sums[0], grad_wq, grad_wk, grad_wv, grad_wo, sums[1], sums[2]
 
     seq_spec = P('dp', 'sp', None)

time: 519 us -> 519 us (level)
  no operation moved by 1% of the time
where the time goes in v7:
time: 519 us; the launch traced here: 518 us
  Pallas kernels  499 us (96%)
  local copies, waits for them, and re-layouts  17.8 us (3%)
    pallas_call x1, Pallas kernels, tail(): pl.pallas_call(functools.partial(tail_kernel, n_dev), out_shape=(gw, gw,...  268 us
    pallas_call x1, Pallas kernels, middle(): pl.pallas_call(functools.partial(middle_kernel, n_dev), out_shape=(jax.Sh...  130 us
    pallas_call x1, Pallas kernels, front(): pl.pallas_call(functools.partial(front_kernel, n_dev), out_shape=(act, ja...  100 us
    unnamed x16, local copies, waits for them, and re-layouts  14.4 us

profile of v7, /device:TPU:113, one launch (start us, length us, event | category | flops | bytes accessed | tf_op | source)
XLA Modules:
  0.0 517.9 jit_solution(14056890799204440658)
XLA Ops:
  0.6 0.7 stack.12
  1.3 0.7 stack.13
  2.0 0.7 stack.14
  2.7 0.6 pad_maximum_fusion.g_ref.gn_ref
  3.4 100.4 %front.1 = (bf16[1024,2048]{1,0:T(8,128)(2,1)}, bf16[8,128,2048]{2,1,0:T(8,128)(2,1)}, f32[1024,256]{1,0:T(8,128)}, bf16[1024,2048]{1,0:T(8,128)(2,1)}, bf16[102...) custom-call(bf16[8,128,2048]{2,1,0:T(8,128)(2,1)} %x_loc.1, ...), custom_call_target="tpu_custom_call" | custom-call | flops 25769803776 | bytes 62914560 | tf_op jit(solution)/shard_map/front/pallas_call | solution.py:247
  103.8 129.9 %middle.1 = (bf16[8,128,2048]{2,1,0:T(8,128)(2,1)}, f32[256,2048]{1,0:T(8,128)}, bf16[1024,2048]{1,0:T(8,128)(2,1)}, bf16[1024,2048]{1,0:T(8,128)(2,1)}, bf16[10...) custom-call(bf16[8,128,2048]{2,1,0:T(8,128)(2,1)} %bitcast.18, ...), custom_call_target="tpu_custom_call" | custom-call | flops 25769803776 | bytes 67108864 | tf_op jit(solution)/shard_map/middle/pallas_call | solution.py:509
  233.7 268.4 %tail.1 = (f32[256,2048]{1,0:T(8,128)}, f32[256,2048]{1,0:T(8,128)}, f32[256,2048]{1,0:T(8,128)}, bf16[8,128,2048]{2,1,0:T(8,128)(2,1)}, bf16[1024,2048]{1,0:T(8,128)(2,1)}, /*index=5*/f32[8,256]{1,0:T(8,128)}) custom-call(bf16[2048,1024]{1,0:T(8,128)(2,1)} %get-tuple-element.35.ht_ref, bf16[2048,1024]{1,0:T(8,128)(2,1)} %get-tuple-element.36.htp_ref, ...), custom_call_target="tpu_custom_call" | custom-call | flops 51539607552 | bytes 67108864 | tf_op jit(solution)/shard_map/tail/pallas_call | solution.py:799
  502.2 1.4 fusion
  503.6 0.0 copy-start
  503.6 4.9 copy.26
  508.5 0.0 copy-done
  508.5 0.0 copy-start.4
  508.5 2.1 copy.27
  510.7 1.0 copy-done.4
  511.6 0.0 copy-start.3
  511.6 0.0 copy-start.2
  511.6 1.3 copy.28
  512.9 1.0 copy-done.3
  514.0 0.0 copy-start.1
  514.0 1.3 copy.29
  515.3 0.0 copy-done.2
  515.3 1.3 copy.30
  516.6 0.0 copy-done.1
  516.6 1.3 copy.31
Async XLA Ops:
  503.6 4.9 copy-start
  508.5 3.1 copy-start.4
  511.6 2.3 copy-start.3
  511.6 3.7 copy-start.2
  514.0 2.6 copy-start.1
